TPU v7x, 32 devices: a whole 2x2x4 slice. The times are simulated.
32 devices in a mesh: member: 2 (over x), lat: 16 (over z, y, core).
Axes of the slice: x: 2, y: 2, z: 4, core: 2. Of those that a mesh axis runs over, the one named last changes fastest.
Arguments:
- height: float32 [128, 32, 1440], P(('member', 'lat')), parts along dimension 0, may hold values from -6 to 6
- zonal_courant: float32 [128, 32, 1440], P(('member', 'lat')), parts along dimension 0, may hold values from -1.5 to 1.5
- merid_courant: float32 [128, 32, 1440], P(('member', 'lat')), parts along dimension 0, may hold values from -1.5 to 1.5
- rates: float32 [64], P('member'), parts along dimension 0, may hold values from 0.05 to 0.5
- thresholds: float32 [64], P('member'), parts along dimension 0, may hold values from -3 to 3
- flags: int32 [64], replicated, may hold values from 0 to 1, as said below
- cutoffs: int32 [64], replicated, may hold values from 45 to 360
Outputs:
- filtered_height: float32 [128, 32, 1440], P(('member', 'lat')), parts along dimension 0
There are 2 independent parts, one for each index of `member`. A program takes and returns all parts, laid end to end along the dimension named above; an argument that names none is the same for every part. Nothing has to cross between parts.
Inputs may be any that keep to these rules, and one draw needn't show every extreme that they name: flags is 1 on a southern band of rows that starts at row 0 and on a northern band that ends at row 63, each band 64 // 8 to 16 rows long, and 0 on all other rows.
All inputs are finite; a program needn't handle non-finite values.
Results may differ from a plain program's by a relative error of at most 0.00007.
Values sent between devices are 32-bit elements; how exact they have to be, the bound alone decides.
No kernel may reach another device: no remote copies, remote signals or barrier semaphores. Data moves between devices by JAX's collectives and lax.ppermute only.
A program may use at most 64 MiB of HBM per device.

v0:
```python
import jax
import jax.numpy as jnp
from jax import lax
from jax.sharding import PartitionSpec as P


def padded_2(cells, sides, width):
    for axis, dim in sides:
        count = lax.axis_size(axis)
        ends = count - 1
        head = lax.slice_in_dim(cells, 0, width, axis=dim)
        tail = lax.slice_in_dim(cells, cells.shape[dim] - width, cells.shape[dim], axis=dim)
        cells = jnp.concatenate(
            [
                lax.ppermute(tail, axis, [(i, (i + 1) % count) for i in range(ends)]),
                cells,
                lax.ppermute(head, axis, [((i + 1) % count, i) for i in range(ends)]),
            ],
            axis=dim,
        )
    return cells


def transform_table(nlon, nkp):
    points = jnp.arange(nlon, dtype=jnp.int32)
    waves = jnp.arange(nkp, dtype=jnp.int32)
    phase = points[:, None] * waves[None, :] % nlon
    angle = 2.0 * jnp.pi / nlon * phase.astype(jnp.float32)
    return jnp.concatenate([jnp.cos(angle), jnp.sin(angle)], axis=1)


def wave_weights(nlon, nkp):
    waves = jnp.arange(nkp, dtype=jnp.int32)
    interior = jnp.where((waves > 0) & (waves < nlon // 2), 2.0, 1.0)
    return jnp.where(waves <= nlon // 2, interior, 0.0).astype(jnp.float32) / nlon


def damping(row_flags, row_cutoffs, nkp):
    waves = jnp.maximum(jnp.arange(nkp), 1).astype(jnp.float32)
    ratio = row_cutoffs.astype(jnp.float32)[:, None] / waves[None, :]
    factor = jnp.minimum(1.0, ratio * ratio)
    return jnp.where(row_flags[:, None] > 0, factor, 1.0)


def filter_units(flat, damp, table, weights):
    highest = lax.Precision.HIGHEST
    spectrum = jnp.dot(flat, table, precision=highest, preferred_element_type=jnp.float32)
    factor = (1.0 - damp) * weights[None, :]
    scaled = spectrum * jnp.concatenate([factor, factor], axis=1)
    dims = (((1,), (1,)), ((), ()))
    removed = lax.dot_general(
        scaled, table, dims, precision=highest, preferred_element_type=jnp.float32
    )
    return flat - removed


def filtered_or_kept(block, row_flags, row_cutoffs, table, weights):
    rows, levels, nlon = block.shape
    damp = damping(row_flags, row_cutoffs, weights.shape[0])
    unit_damp = jnp.broadcast_to(damp[:, None, :], (rows, levels, damp.shape[1])).reshape(
        rows * levels, damp.shape[1]
    )

    def apply_filter(data):
        return filter_units(data.reshape(rows * levels, nlon), unit_damp, table, weights).reshape(
            rows, levels, nlon
        )

    def keep_block(data):
        return data

    return lax.cond(jnp.any(row_flags > 0), apply_filter, keep_block, block)


def face_fluxes(rows_height, rows_speed, face_cos, count):
    face_value = (
        7.0 * (rows_height[1 : count + 1] + rows_height[2 : count + 2])
        - (rows_height[0:count] + rows_height[3 : count + 3])
    ) / 12.0
    speed = 0.5 * (rows_speed[0:count] + rows_speed[1 : count + 1]) * face_cos[:, None, None]
    return speed * face_value


def face_cosines(face_ids, nlat):
    return jnp.where(
        (face_ids > 0) & (face_ids < nlat),
        jnp.sin(jnp.pi * face_ids.astype(jnp.float32) / nlat),
        jnp.float32(0.0),
    )


def local(height, zonal_courant, merid_courant, rates, thresholds, flags, cutoffs):
    lat_rows, levels, nlon = height.shape
    devices = lax.axis_size("lat")
    position = lax.axis_index("lat")
    first_row = position * lat_rows
    nlat = lat_rows * devices
    local_rows = first_row + jnp.arange(lat_rows, dtype=jnp.int32)
    cos_rows = jnp.sin(jnp.pi * (local_rows.astype(jnp.float32) + 0.5) / nlat)
    faces = first_row + jnp.arange(lat_rows + 1, dtype=jnp.int32)
    cos_faces = face_cosines(faces, nlat)
    padded = padded_2(jnp.stack([height, merid_courant]), (("lat", 1),), 2)
    east = jnp.roll(height, -1, axis=2)
    west = jnp.roll(height, 1, axis=2)
    far_east = jnp.roll(height, -2, axis=2)
    face_height = (7.0 * (height + east) - (west + far_east)) / 12.0
    face_speed = 0.5 * (zonal_courant + jnp.roll(zonal_courant, -1, axis=2))
    zonal_flux = face_speed * face_height
    zonal_div = zonal_flux - jnp.roll(zonal_flux, 1, axis=2)
    source = -rates[None, :, None] * jax.nn.softplus(height - thresholds[None, :, None])
    partial_sums = jnp.sum(jnp.sum(source, axis=2) * cos_rows[:, None], axis=0)
    totals = lax.psum(partial_sums, "lat")
    all_rows = jnp.arange(nlat, dtype=jnp.int32)
    area = nlon * jnp.sum(jnp.sin(jnp.pi * (all_rows.astype(jnp.float32) + 0.5) / nlat))
    level_mean = totals / area
    padded_height = padded[0]
    padded_speed = padded[1]
    count = lat_rows + 1
    merid_flux = face_fluxes(padded_height, padded_speed[1:], cos_faces, count)
    merid_div = (merid_flux[1:] - merid_flux[:-1]) / cos_rows[:, None, None]
    updated = height - zonal_div - merid_div + source - level_mean[None, :, None]
    nkp = (nlon // 2 + 128) // 128 * 128
    table = transform_table(nlon, nkp)
    weights = wave_weights(nlon, nkp)
    row_flags = lax.dynamic_slice_in_dim(flags, first_row, lat_rows)
    row_cutoffs = lax.dynamic_slice_in_dim(cutoffs, first_row, lat_rows)
    result = filtered_or_kept(updated, row_flags, row_cutoffs, table, weights)
    return result


def solution(mesh):
    return jax.shard_map(
        local,
        mesh=mesh,
        in_specs=(
            P(("member", "lat"), None, None),
            P(("member", "lat"), None, None),
            P(("member", "lat"), None, None),
            P("member"),
            P("member"),
            P(),
            P(),
        ),
        out_specs=P(("member", "lat"), None, None),
        check_vma=False,
    )
```

profile of v0, /device:TPU:0, one launch (start us, length us, event | category | flops | bytes accessed | tf_op | source)
XLA Modules:
  0.0 101.5 jit_solution(3019089762479028692)
XLA Ops:
  0.0 0.0 copy-start
  0.0 0.0 copy-start.2
  0.0 2.8 %fusion.17 = (f32[2,2,32,1440]{3,2,1,0:T(8,128)}, f32[2,2,32,1440]{3,2,1,0:T(8,128)}) fusion(f32[1,4,32,1440]{3,2,1,0:T(8,128)} %bitcast.21, f32[1,4,32,1440]{3,2,1,0:T(8,128)} %bitcast.27), kind=kLoop, calls=%fused_computation.33 | loop fusion | flops 368640 | bytes 2949120 | tf_op jit(solution)/shard_map/stack | solution.py:102
  2.8 3.3 %collective-permute-start = (f32[2,2,32,1440]{3,2,1,0:T(8,128)}, f32[2,2,32,1440]{3,2,1,0:T(8,128)}, u32[]{:S(2)}, u32[]{:S(2)}) collective-permute-start(f32[2,2,32,1440]{3,2,1,0:T(8,128)} %get-tuple-element.115), channel_id=1, source_target_pairs={{0,1},{1,2},{2,3},{3,4},{4,5},{5,6},{6,7},{7,8},{8,9},{9,10},{10,1... | collective-permute-start | bytes 2211848 | tf_op jit(solution)/shard_map/ppermute | solution.py:15
  6.1 1.3 %collective-permute-start.1 = (f32[2,2,32,1440]{3,2,1,0:T(8,128)}, f32[2,2,32,1440]{3,2,1,0:T(8,128)}, u32[]{:S(2)}, u32[]{:S(2)}) collective-permute-start(f32[2,2,32,1440]{3,2,1,0:T(8,128)} %get-tuple-element.116), channel_id=1, source_target_pairs={{1,0},{2,1},{3,2},{4,3},{5,4},{6,5},{7,6},{8,7},{9,8},{10,9},{11,1... | collective-permute-start | bytes 2211848 | tf_op jit(solution)/shard_map/ppermute | solution.py:17
  7.3 2.8 %fusion.33 = (f32[4,32,1439]{2,1,0:T(8,128)}, f32[4,32,1439]{2,1,0:T(8,128)}) fusion(f32[4,32,1440]{2,1,0:T(8,128)} %param.9), kind=kLoop, calls=%fused_computation.63 | loop fusion | bytes 2947072 | tf_op jit(solution)/shard_map/jit(_roll_static)/slice | solution.py:104
  10.1 0.0 copy-done
  10.1 0.1 fusion.32
  10.2 0.3 slice.95
  10.5 0.0 copy-done.2
  10.5 1.2 %slice.89 = f32[4,32,1439]{2,1,0:T(8,128)} slice(f32[4,32,1440]{2,1,0:T(8,128)S(1)} %copy-done.2), slice={[0:4], [0:32], [1:1440]} | slice | bytes 1473536 | tf_op jit(solution)/shard_map/jit(_roll_static)/slice | solution.py:107
  11.8 0.7 sine_reduce_fusion
  12.4 0.0 slice-start
  12.4 0.0 copy-start.3
  12.4 0.0 copy-start.4
  12.4 0.0 copy-start.5
  12.4 0.0 copy-start.7
  12.5 19.6 %fusion.7 = (f32[1440,768]{1,0:T(8,128)}, f32[1440,768]{1,0:T(8,128)}) fusion(), kind=kLoop, calls=%fused_computation.15 | loop fusion | flops 9953280 | bytes 8847360 | tf_op jit(solution)/shard_map/sin | solution.py:29
  32.0 0.0 copy-done.9
  32.1 0.0 slice-done
  32.1 0.0 copy-done.3
  32.1 0.0 copy-done.4
  32.1 0.0 copy-done.5
  32.1 0.0 copy-done.7
  32.1 0.9 fusion.29
  33.0 0.1 multiply_reduce_fusion
  33.1 35.8 %psum.7 = f32[32]{0:T(128)S(1)} all-reduce(f32[32]{0:T(128)S(1)} %multiply_reduce_fusion), channel_id=1, replica_groups=mesh['member'=2,'lat'=16] {'lat'}, use_global_device_ids=true, to_apply=%region_3.4 | all-reduce | flops 32 | bytes 256 | tf_op jit(solution)/shard_map/psum | solution.py:112
  68.9 0.1 slice.109
  69.0 0.0 copy-done.8
  69.0 0.8 fusion.31
  69.8 0.0 copy-done.10
  69.8 0.1 dynamic-slice_convert_fusion
  71.2 0.0 copy-start.6
  71.2 8.2 %pad_maximum_fusion = f32[1440,1536]{1,0:T(8,128)} fusion(f32[1440,768]{1,0:T(8,128)} %get-tuple-element.123, f32[1440,768]{1,0:T(8,128)} %get-tuple-element.124), kind=kLoop, calls=%fused_computation.8 | loop fusion | flops 2211840 | bytes 17694720 | tf_op jit(solution)/shard_map/concatenate | solution.py:29
  79.4 0.0 collective-permute-done
  79.4 0.0 collective-permute-done.1
  79.4 0.0 copy-done.6
  79.4 1.9 %maximum_maximum_fusion = (f32[2,6,32,1440]{3,2,1,0:T(8,128)S(1)}, f32[2,6,32,1440]{3,2,1,0:T(8,128)S(1)}) fusion(f32[1,4,32,1440]{3,2,1,0:T(8,128)S(1)} %bitcast.28, f32[1,4,32,1440]{3,2,1,0:T(8,128)S(1)} %bitcast.22, f32[2,2,32,1440]{3,2,1,0:T(8,128)} %collective-permute-done, f32[2,2,32,1440]{3,2,1,0:T(8,128)} %collective-permute-done.1), kind=kLoop, calls=%fused_computation.18 | loop fusion | flops 2211840 | bytes 7372800 | tf_op jit(solution)/shard_map/concatenate | solution.py:13
  81.3 0.5 fusion.13
  81.8 0.7 fusion.22
  82.6 18.0 %conditional.1 = (f32[4,32,1440]{2,1,0:T(8,128)S(1)}) conditional(s32[]{:T(128)} %convert_element_type.42, f32[4,32,1440]{2,1,0:T(8,128)S(1)} %fusion.22, (f32[4,32,1440]{2,1,0:T(8,128)S(1)}, f32[1440,1536]{1,0:T(8,128)}, pred[4]{0:T(512)(128)(4,1)S(1)}, f32[4]{0:T(128)S(1)}, f32[1,768]{1,0:T(1,128)S(1)}, /*index=5*/s32[768]{0:T(1024)S(1)}) %tuple.45), branch_computations={%region_5.6_spmd, %region_6.7_spmd} | conditional | flops 6795468800 | bytes 25258016 | solution.py:72
  82.8 0.1 fusion.2
  82.9 7.6 %convolution_multiply_fusion = f32[128,1536]{1,0:T(8,128)S(1)} fusion(f32[128,1440]{1,0:T(8,128)S(1)} %bitcast.24, f32[1440,1536]{1,0:T(8,128)} %get-tuple-element.105, f32[128,768]{1,0:T(8,128)S(1)} %bitcast_multiply_fusion), kind=kOutput, calls=%fused_computation.1 | convolution fusion | flops 3397779456 | bytes 10764288 | tf_op jit(solution)/shard_map/cond/branch_1_fun/dot_general | solution.py:47
  90.6 0.3 copy.27
  90.8 9.5 %convolution_subtract_fusion = f32[128,1440]{0,1:T(8,128)S(1)} fusion(f32[128,1440]{0,1:T(8,128)S(1)} %copy.27, f32[128,1536]{1,0:T(8,128)S(1)} %convolution_multiply_fusion, f32[1440,1536]{1,0:T(8,128)} %get-tuple-element.105), kind=kOutput, calls=%fused_computation | convolution fusion | flops 3397570560 | bytes 11108352 | tf_op jit(solution)/shard_map/cond/branch_1_fun/dot_general | solution.py:51
  100.3 0.3 copy.28
  100.6 0.0 copy-start.1
  100.6 0.9 copy-done.1
  (13 shorter events, 0.2 us)
Async XLA Ops:
  0.0 10.1 %copy-start = (f32[4,32,1440]{2,1,0:T(8,128)S(1)}, f32[4,32,1440]{2,1,0:T(8,128)}, u32[]{:S(2)}) copy-start(f32[4,32,1440]{2,1,0:T(8,128)} %param.9) | copy-start | bytes 2211844
  0.0 10.5 %copy-start.2 = (f32[4,32,1440]{2,1,0:T(8,128)S(1)}, f32[4,32,1440]{2,1,0:T(8,128)}, u32[]{:S(2)}) copy-start(f32[4,32,1440]{2,1,0:T(8,128)} %param.10) | copy-start | bytes 2211844
  2.8 76.6 %collective-permute-start = (f32[2,2,32,1440]{3,2,1,0:T(8,128)}, f32[2,2,32,1440]{3,2,1,0:T(8,128)}, u32[]{:S(2)}, u32[]{:S(2)}) collective-permute-start(f32[2,2,32,1440]{3,2,1,0:T(8,128)} %get-tuple-element.115), channel_id=1, source_target_pairs={{0,1},{1,2},{2,3},{3,4},{4,5},{5,6},{6,7},{7,8},{8,9},{9,10},{10,1... | collective-permute-start | bytes 2211848 | tf_op jit(solution)/shard_map/ppermute | solution.py:15
  6.1 73.3 %collective-permute-start.1 = (f32[2,2,32,1440]{3,2,1,0:T(8,128)}, f32[2,2,32,1440]{3,2,1,0:T(8,128)}, u32[]{:S(2)}, u32[]{:S(2)}) collective-permute-start(f32[2,2,32,1440]{3,2,1,0:T(8,128)} %get-tuple-element.116), channel_id=1, source_target_pairs={{1,0},{2,1},{3,2},{4,3},{5,4},{6,5},{7,6},{8,7},{9,8},{10,9},{11,1... | collective-permute-start | bytes 2211848 | tf_op jit(solution)/shard_map/ppermute | solution.py:17
  12.4 19.6 %copy-start.9 = (f32[32]{0:T(128)S(1)}, f32[32]{0:T(128)}, u32[]{:S(2)}) copy-start(f32[32]{0:T(128)} %param.12) | copy-start | bytes 388
  12.4 19.6 %slice-start = ((f32[4,32,1440]{2,1,0:T(8,128)}), f32[4,32,1]{2,1,0:T(8,128)S(1)}, s32[]{:S(2)}) async-start(f32[4,32,1440]{2,1,0:T(8,128)} %param.10), calls=%async_computation | async-start | bytes 131072 | tf_op jit(solution)/shard_map/jit(_roll_static)/slice | solution.py:107
  12.4 19.7 %copy-start.3 = (f32[4,32,1439]{2,1,0:T(8,128)S(1)}, f32[4,32,1439]{2,1,0:T(8,128)}, u32[]{:S(2)}) copy-start(f32[4,32,1439]{2,1,0:T(8,128)} %slice.89) | copy-start | bytes 2210308
  12.4 19.7 %copy-start.4 = (f32[4,32,1439]{2,1,0:T(8,128)S(1)}, f32[4,32,1439]{2,1,0:T(8,128)}, u32[]{:S(2)}) copy-start(f32[4,32,1439]{2,1,0:T(8,128)} %get-tuple-element.121) | copy-start | bytes 2210308
  12.4 19.7 %copy-start.5 = (f32[4,32,1439]{2,1,0:T(8,128)S(1)}, f32[4,32,1439]{2,1,0:T(8,128)}, u32[]{:S(2)}) copy-start(f32[4,32,1439]{2,1,0:T(8,128)} %get-tuple-element.122) | copy-start | bytes 2210308
  12.4 19.7 %copy-start.7 = (f32[32]{0:T(128)S(1)}, f32[32]{0:T(128)}, u32[]{:S(2)}) copy-start(f32[32]{0:T(128)} %param.13) | copy-start | bytes 388
  32.0 37.0 %copy-start.8 = (s32[64]{0:T(128)S(1)}, s32[64]{0:T(128)}, u32[]{:S(2)}) copy-start(s32[64]{0:T(128)} %param.14) | copy-start | bytes 772
  32.0 37.8 %copy-start.10 = (s32[64]{0:T(128)S(1)}, s32[64]{0:T(128)}, u32[]{:S(2)}) copy-start(s32[64]{0:T(128)} %param.15) | copy-start | bytes 772
  71.2 8.2 %copy-start.6 = (f32[4,32,1440]{2,1,0:T(8,128)S(1)}, f32[4,32,1440]{2,1,0:T(8,128)}, u32[]{:S(2)}) copy-start(f32[4,32,1440]{2,1,0:T(8,128)} %param.11) | copy-start | bytes 2211844
  100.6 0.9 copy-start.1
where the time goes:
time: 102 us; the launch traced here: 101 us
  other arithmetic  36.4 us (36%)
  blocking collectives  35.8 us (35%)
  matrix products  17.1 us (17%)
  local copies, waits for them, and re-layouts  5.82 us (6%)
  starting transfers between devices  4.55 us (4%)
  between operations  1.52 us (1%)
    psum x1, blocking collectives, local(): totals = lax.psum(partial_sums, 'lat')  35.8 us
    sin x1, other arithmetic, transform_table(): return jnp.concatenate([jnp.cos(angle), jnp.sin(angle)], axis=1)  19.6 us
    dot_general x1, matrix products, filter_units(): lax.dot_general(scaled, table, dims, precision=highest, preferred_element...  9.48 us
    concatenate x1, other arithmetic, transform_table(): return jnp.concatenate([jnp.cos(angle), jnp.sin(angle)], axis=1)  8.16 us
    dot_general x1, matrix products, filter_units(): jnp.dot(flat, table, precision=highest, preferred_element_type=jnp.float32)  7.64 us
    ppermute x1, starting transfers between devices, padded_2(): lax.ppermute(tail, axis, [(i, (i + 1) % count) for i in range(ends)])  3.27 us
    slice x2, local copies, waits for them, and re-layouts, local(): west = jnp.roll(height, 1, axis=2)  2.85 us
    another operation x1, other arithmetic, local(): padded = padded_2(jnp.stack([height, merid_courant]), (('lat', 1),), 2)  2.78 us
  transfers between devices with their start and end apart: 2, of which 0 were waited for; matrix products, arithmetic and copies ran while one was open for 34% of the time, Pallas kernels for 0%

commit v1 on v0

v1 whole, which is shorter than its diff:
```python
import functools

import jax
import jax.numpy as jnp
import ml_dtypes
import numpy as np
from jax import lax
from jax.experimental import pallas as pl
from jax.experimental.pallas import tpu as pltpu
from jax.sharding import PartitionSpec as P

LANES = 128


def round_up(value, step):
    return -(-value // step) * step


def split(table):
    high = table.astype(ml_dtypes.bfloat16)
    low = (table - high.astype(np.float64)).astype(ml_dtypes.bfloat16)
    return high, low


@functools.cache
def filter_tables(nlon):
    half = nlon // 2
    width = round_up(half // 2 + 1, LANES)
    depth = round_up(half, LANES)
    n = np.arange(depth)
    m = np.arange(width)
    tables = []
    for odd in (0, 1):
        waves = 2 * m + odd
        angle = 2.0 * np.pi / nlon * (n[:, None] * waves[None, :] % nlon)
        valid = (n[:, None] < half) & (waves[None, :] <= half)
        table = np.concatenate([np.cos(angle) * valid, np.sin(angle) * valid], axis=1)
        tables += [*split(table), *split(np.ascontiguousarray(table.T))]
    return tables


def softplus(s):
    return jnp.maximum(s, 0.0) + jnp.log(1.0 + jnp.exp(-jnp.abs(s)))


def wrapped(row, nlon, full):
    base = nlon // LANES * LANES
    rest = nlon - base
    body, tail = row[:, :base], row[:, base:]
    tail = jnp.concatenate([tail, jnp.zeros((row.shape[0], full - nlon), row.dtype)], axis=1)
    lane = lax.broadcasted_iota(jnp.int32, tail.shape, 1)
    head = pltpu.roll(row[:, : full - base], rest, 1)
    end = pltpu.roll(tail, full - base - rest, 1)
    tail = jnp.where(lane < rest, tail, jnp.where(lane < full - base - 8, head, end))
    return jnp.concatenate([body, tail], axis=1)


def local_kernel(cos_ref, rates_ref, thresholds_ref, h_ref, u_ref, out_ref, sum_ref):
    j = pl.program_id(0)
    rows = pl.num_programs(0)
    nlon = h_ref.shape[2]
    full = round_up(nlon, LANES)
    first = lax.axis_index("lat") * rows
    h0 = h_ref[0]
    s = softplus(h0 - thresholds_ref[...])
    area = s * cos_ref[first + j]
    base = nlon // LANES * LANES
    acc = area[:, 0:LANES]
    for t in range(1, nlon // LANES):
        acc = acc + area[:, t * LANES : (t + 1) * LANES]
    acc = acc + jnp.concatenate(
        [area[:, base:], jnp.zeros((acc.shape[0], full - nlon), jnp.float32)], axis=1
    )
    acc = acc * -rates_ref[...]

    @pl.when(j == 0)
    def _():
        sum_ref[...] = acc

    @pl.when(j > 0)
    def _():
        sum_ref[...] += acc

    h = wrapped(h0, nlon, full)
    u = wrapped(u_ref[0], nlon, full)
    east = pltpu.roll(h, full - 1, 1)
    far_east = pltpu.roll(h, full - 2, 1)
    west = pltpu.roll(h, 1, 1)
    face = (7.0 * (h + east) - (west + far_east)) * (1.0 / 12.0)
    flux = 0.5 * (u + pltpu.roll(u, full - 1, 1)) * face
    div = flux - pltpu.roll(flux, 1, 1)
    out_ref[0] = h0 - div[:, :nlon] - rates_ref[...] * s


def finish_kernel(
    cos_row_ref,
    cos_face_ref,
    flags_ref,
    cutoffs_ref,
    sums_ref,
    h_ref,
    v_ref,
    part_ref,
    a_ref,
    b_ref,
    *rest,
):
    tables, (out_ref, u_ref) = rest[:8], rest[8:]
    rows, levels, nlon = h_ref.shape
    full = round_up(nlon, LANES)
    half = nlon // 2
    depth, cols = tables[0].shape
    width = cols // 2
    position = lax.axis_index("lat")
    first = position * rows
    odd = position % 2 == 1
    area = nlon * float(np.sum(np.sin(np.pi * (np.arange(cos_row_ref.shape[0]) + 0.5) / cos_row_ref.shape[0])))
    mean = jnp.sum(sums_ref[...], axis=1, keepdims=True) * (1.0 / area)

    below = [jnp.where(odd, a_ref[i], b_ref[i]) for i in range(3)]
    above = [jnp.where(odd, b_ref[i], a_ref[i]) for i in range(3)]
    height = [below[0], below[1]] + [h_ref[j] for j in range(rows)] + [above[0], above[1]]
    speed = [below[2]] + [v_ref[j] for j in range(rows)] + [above[2]]
    flux = []
    for f in range(rows + 1):
        p = 7.0 * (height[f + 1] + height[f + 2]) - (height[f] + height[f + 3])
        c = cos_face_ref[first + f] * (0.5 / 12.0)
        flux.append((speed[f] + speed[f + 1]) * c * p)
    marked = flags_ref[first]
    for j in range(1, rows):
        marked = jnp.maximum(marked, flags_ref[first + j])

    def updated(j):
        return part_ref[j] - (flux[j + 1] - flux[j]) * (1.0 / cos_row_ref[first + j])

    @pl.when(marked == 0)
    def _():
        for j in range(rows):
            out_ref[j] = updated(j) - mean

    @pl.when(marked > 0)
    def _():
        u_ref[:, base_of(nlon):] = jnp.zeros((rows * levels, full - base_of(nlon)), jnp.float32)
        for j in range(rows):
            u_ref[j * levels : (j + 1) * levels, :nlon] = updated(j)
        x = u_ref[...]
        near = x[:, :depth]
        far = pltpu.roll(x, full - half, 1)[:, :depth]
        removed = []
        lane = lax.broadcasted_iota(jnp.int32, (1, width), 1)
        for parity in (0, 1):
            y = near + far if parity == 0 else near - far
            fwd_high, fwd_low, inv_high, inv_low = (t[...] for t in tables[4 * parity : 4 * parity + 4])
            spectrum = product(y, fwd_high, fwd_low)
            waves = 2 * lane + parity
            weight = jnp.where((waves > 0) & (waves < half), 2.0 / nlon, 1.0 / nlon)
            inverse = 1.0 / jnp.maximum(waves, 1).astype(jnp.float32)
            pieces = []
            for j in range(rows):
                ratio = cutoffs_ref[first + j].astype(jnp.float32) * inverse
                factor = (1.0 - jnp.minimum(1.0, ratio * ratio)) * weight
                factor = jnp.where(flags_ref[first + j] > 0, factor, 0.0)
                factor = jnp.concatenate([factor, factor], axis=1)
                pieces.append(spectrum[j * levels : (j + 1) * levels] * factor)
            removed.append(product(jnp.concatenate(pieces, axis=0), inv_high, inv_low))
        zeros = jnp.zeros((rows * levels, full - depth), jnp.float32)
        r1 = jnp.concatenate([removed[0] + removed[1], zeros], axis=1)
        r2 = jnp.concatenate([removed[0] - removed[1], zeros], axis=1)
        y = x - r1 - pltpu.roll(r2, half, 1)
        for j in range(rows):
            cut = cutoffs_ref[first + j].astype(jnp.float32)
            kept = jnp.where(flags_ref[first + j] > 0, jnp.minimum(1.0, cut * cut), 1.0)
            out_ref[j] = y[j * levels : (j + 1) * levels, :nlon] - mean * kept


def base_of(nlon):
    return nlon // LANES * LANES


def product(y, high, low):
    y_high = y.astype(jnp.bfloat16)
    y_low = (y - y_high.astype(jnp.float32)).astype(jnp.bfloat16)
    count = y.shape[0]
    both = jnp.dot(
        jnp.concatenate([y_high, y_low], axis=0), high, preferred_element_type=jnp.float32
    )
    return both[:count] + both[count:] + jnp.dot(y_high, low, preferred_element_type=jnp.float32)


def local(height, zonal_courant, merid_courant, rates, thresholds, flags, cutoffs):
    rows, levels, nlon = height.shape
    count = lax.axis_size("lat")
    nlat = rows * count
    odd = lax.axis_index("lat") % 2 == 1
    full = round_up(nlon, LANES)

    def edge(upper):
        two = jnp.where(upper, rows - 2, 0)
        one = jnp.where(upper, rows - 1, 0)
        return jnp.concatenate(
            [
                lax.dynamic_slice_in_dim(height, two, 2, 0),
                lax.dynamic_slice_in_dim(merid_courant, one, 1, 0),
            ]
        )

    between = [(i, i + 1) for i in range(1, count - 1, 2)]
    within = [(i, i + 1) for i in range(0, count - 1, 2)]
    between = between + [(j, i) for i, j in between]
    within = within + [(j, i) for i, j in within]
    b = lax.ppermute(edge(odd), "lat", between)
    a = lax.ppermute(edge(~odd), "lat", within)

    cos_row = jnp.asarray(np.sin(np.pi * (np.arange(nlat) + 0.5) / nlat).astype(np.float32))
    faces = np.sin(np.pi * np.arange(nlat + 1) / nlat)
    faces[0] = faces[nlat] = 0.0
    cos_face = jnp.asarray(faces.astype(np.float32))
    smem = pl.BlockSpec(memory_space=pltpu.SMEM)
    vmem = pl.BlockSpec(memory_space=pltpu.VMEM)
    row_block = pl.BlockSpec((1, levels, nlon), lambda j: (j, 0, 0))
    level_block = pl.BlockSpec((levels, 1), lambda j: (0, 0))
    part, sums = pl.pallas_call(
        local_kernel,
        grid=(rows,),
        in_specs=[smem, level_block, level_block, row_block, row_block],
        out_specs=[row_block, pl.BlockSpec((levels, LANES), lambda j: (0, 0))],
        out_shape=[
            jax.ShapeDtypeStruct(height.shape, jnp.float32),
            jax.ShapeDtypeStruct((levels, LANES), jnp.float32),
        ],
        name="local_part",
    )(cos_row, rates[:, None], thresholds[:, None], height, zonal_courant)

    bits = [1 << i for i in range((count - 1).bit_length())]
    if count == 1 << len(bits):
        for d in [1] + bits[2:] + bits[1:2]:
            sums = sums + lax.ppermute(sums, "lat", [(i, i ^ d) for i in range(count)])
    else:
        sums = lax.psum(sums, "lat")

    return pl.pallas_call(
        finish_kernel,
        in_specs=[smem] * 4 + [vmem] * 14,
        out_specs=vmem,
        out_shape=jax.ShapeDtypeStruct(height.shape, jnp.float32),
        scratch_shapes=[pltpu.VMEM((rows * levels, full), jnp.float32)],
        name="finish",
    )(
        cos_row,
        cos_face,
        flags,
        cutoffs,
        sums,
        height,
        merid_courant,
        part,
        a,
        b,
        *[jnp.asarray(t) for t in filter_tables(nlon)],
    )


def solution(mesh):
    split_rows = P(("member", "lat"), None, None)
    return jax.shard_map(
        local,
        mesh=mesh,
        in_specs=(split_rows, split_rows, split_rows, P("member"), P("member"), P(), P()),
        out_specs=split_rows,
        check_vma=False,
    )
```

time: 102 us -> 37.3 us (0.37)
  blocking collectives: 35.8 us -> 0 us
  other arithmetic: 36.4 us -> 1.41 us
  matrix products: 17.1 us -> 0 us
  Pallas kernels: 0 us -> 13.4 us
  waiting for transfers between devices: 0.01 us -> 7.06 us
  starting transfers between devices: 4.55 us -> 11.2 us
  local copies, waits for them, and re-layouts: 5.82 us -> 3.81 us
  between operations: 1.52 us -> 0.08 us
    psum x1 -> x0, blocking collectives: 35.8 us -> none  [local(): totals = lax.psum(partial_sums, 'lat')]
    sin x2 -> x0, other arithmetic: 19.6 us -> none  [the longest x1 19.6 us: transform_table(): return jnp.concatenate([jnp.cos(angle), jnp.sin(angle)], axis=1)]
    dot_general x2 -> x0, matrix products: 17.1 us -> none  [the longest x1 9.48 us: filter_units(): lax.dot_general(scaled, table, dims, precision=highest, preferred_element...]
    pallas_call x0 -> x2, Pallas kernels: none -> 13.4 us  [the longest x1 8.83 us: local(): pl.pallas_call(finish_kernel, in_specs=[smem] * 4 + [vmem] * 14, out_spec...]
    concatenate x2, other arithmetic: 10.1 us -> 0.08 us  [edge(): jnp.concatenate([lax.dynamic_slice_in_dim(height, two, 2, 0), lax.dynamic...]
    ppermute x2 -> x6, waiting for transfers between devices: 0.01 us -> 7.06 us  [the longest x4 7.05 us: local(): sums = sums + lax.ppermute(sums, 'lat', [(i, i ^ d) for i in range(count)])]
    ppermute x2 -> x6, starting transfers between devices: 4.55 us -> 11.2 us  [the longest x4 9.96 us: local(): sums = sums + lax.ppermute(sums, 'lat', [(i, i ^ d) for i in range(count)])]
    slice x8 -> x0, local copies, waits for them, and re-layouts: 4.38 us -> none  [the longest x2 2.85 us: local(): west = jnp.roll(height, 1, axis=2)]
  transfers between devices with their start and end apart: 2 -> 6, of which waited for: 0 -> 4; matrix products, arithmetic and copies ran while one was open for 34% -> 7% of each run, Pallas kernels for 0% -> 12%
where the time goes in v1:
time: 37.3 us; the launch traced here: 37 us
  Pallas kernels  13.4 us (36%)
  starting transfers between devices  11.2 us (30%)
  waiting for transfers between devices  7.06 us (19%)
  local copies, waits for them, and re-layouts  3.81 us (10%)
  other arithmetic  1.41 us (4%)
    ppermute x4, starting transfers between devices, local(): sums = sums + lax.ppermute(sums, 'lat', [(i, i ^ d) for i in range(count)])  9.96 us
    pallas_call x1, Pallas kernels, local(): pl.pallas_call(finish_kernel, in_specs=[smem] * 4 + [vmem] * 14, out_spec...  8.83 us
    ppermute x4, waiting for transfers between devices, local(): sums = sums + lax.ppermute(sums, 'lat', [(i, i ^ d) for i in range(count)])  7.05 us
    pallas_call x1, Pallas kernels, local(): pl.pallas_call(local_kernel, grid=(rows,), in_specs=[smem, level_block, l...  4.59 us
    add x4, other arithmetic, local(): sums = sums + lax.ppermute(sums, 'lat', [(i, i ^ d) for i in range(count)])  1.33 us
    unnamed x10, local copies, waits for them, and re-layouts  1.26 us
    dynamic_slice x1, local copies, waits for them, and re-layouts, edge(): lax.dynamic_slice_in_dim(merid_courant, one, 1, 0)  1.12 us
  transfers between devices with their start and end apart: 6, of which 4 were waited for; matrix products, arithmetic and copies ran while one was open for 7% of the time, Pallas kernels for 12%

profile of v1, /device:TPU:0, one launch (start us, length us, event | category | flops | bytes accessed | tf_op | source)
XLA Modules:
  0.0 37.0 jit_solution(13107229038879135162)
XLA Ops:
  0.0 0.0 copy-start
  0.0 1.1 %constant_dynamic-slice_fusion = (f32[1,32,1440]{2,1,0:T(8,128)S(1)}, f32[1,32,1440]{2,1,0:T(8,128)S(1)}) fusion(f32[4,32,1440]{2,1,0:T(8,128)} %v_ref.1, s32[]{:T(128)S(6)} %select_n.28, s32[]{:T(128)S(6)} %select_n.26), kind=kLoop, calls=%fused_computation.2 | loop fusion | bytes 737288 | tf_op jit(solution)/shard_map/dynamic_slice | solution.py:203
  1.1 0.2 copy-done
  1.3 0.1 constant_dynamic-slice_fusion.1
  1.4 0.0 copy-start.3
  1.4 0.0 copy-start.4
  1.5 0.6 %collective-permute-start.4 = (f32[3,32,1440]{2,1,0:T(8,128)S(1)}, f32[3,32,1440]{2,1,0:T(8,128)S(1)}, u32[]{:S(2)}, u32[]{:S(2)}) collective-permute-start(f32[3,32,1440]{2,1,0:T(8,128)S(1)} %pad_maximum_fusion), channel_id=1, source_target_pairs={{0,1},{2,3},{4,5},{6,7},{8,9},{10,11},{12,13},{14,15},{1,0},{3,2},... | collective-permute-start | bytes 1658888 | tf_op jit(solution)/shard_map/ppermute | solution.py:212
  2.1 0.7 %collective-permute-start.5 = (f32[3,32,1440]{2,1,0:T(8,128)S(1)}, f32[3,32,1440]{2,1,0:T(8,128)S(1)}, u32[]{:S(2)}, u32[]{:S(2)}) collective-permute-start(f32[3,32,1440]{2,1,0:T(8,128)S(1)} %pad_maximum_fusion.1), channel_id=1, source_target_pairs={{1,2},{3,4},{5,6},{7,8},{9,10},{11,12},{13,14},{2,1},{4,3},{6,5},{... | collective-permute-start | bytes 1658888 | tf_op jit(solution)/shard_map/ppermute | solution.py:211
  2.8 0.0 copy-done.3
  2.8 0.7 %copy.18.rates_ref = f32[32,1]{1,0:T(8,128)} copy(f32[32,1]{0,1:T(1,128)S(1)} %bitcast.2) | data formatting | bytes 256 | tf_op jit(solution)/shard_map/broadcast_in_dim | solution.py:232
  3.5 0.0 copy-done.4
  3.5 0.7 %copy.19.thresholds_ref = f32[32,1]{1,0:T(8,128)} copy(f32[32,1]{0,1:T(1,128)S(1)} %bitcast.3) | data formatting | bytes 256 | tf_op jit(solution)/shard_map/broadcast_in_dim | solution.py:232
  4.2 4.6 %local_part.1 = (f32[4,32,1440]{2,1,0:T(8,128)}, f32[32,128]{1,0:T(8,128)}) custom-call(f32[64]{0:T(128)} %constant.46.clone.cos_ref.cos_row_ref, f32[32,1]{1,0:T(8,128)} %copy.18.rates_ref, f32[32,1]{1,0:T(8,128)} %copy.19.thresholds_ref, f32[4,32,1440]{2,1,0:T(8,128)} %h_ref.3, f32[4,32,1440]{2,1,0:T(8,128)} %u_ref.1), custom_call_target="tpu_custom_call" | custom-call | tf_op jit(solution)/shard_map/local_part/pallas_call | solution.py:222
  8.7 3.8 %collective-permute-start = (f32[32,128]{1,0:T(8,128)}, f32[32,128]{1,0:T(8,128)S(1)}, u32[]{:S(2)}, u32[]{:S(2)}) collective-permute-start(f32[32,128]{1,0:T(8,128)} %get-tuple-element.7), channel_id=1, source_target_pairs={{0,1},{1,0},{2,3},{3,2},{4,5},{5,4},{6,7},{7,6},{8,9},{9,8},{10,11... | collective-permute-start | bytes 49160 | tf_op jit(solution)/shard_map/ppermute | solution.py:237
  12.6 1.0 %collective-permute-done = f32[32,128]{1,0:T(8,128)S(1)} collective-permute-done((f32[32,128]{1,0:T(8,128)}, f32[32,128]{1,0:T(8,128)S(1)}, u32[]{:S(2)}, u32[]{:S(2)}) %collective-permute-start) | collective-permute-done | bytes 16416 | tf_op jit(solution)/shard_map/ppermute | solution.py:237
  13.6 0.7 %add.20 = f32[32,128]{1,0:T(8,128)S(1)} add(f32[32,128]{1,0:T(8,128)} %get-tuple-element.7, f32[32,128]{1,0:T(8,128)S(1)} %collective-permute-done) | non-fusion elementwise | flops 4096 | bytes 49152 | tf_op jit(solution)/shard_map/add | solution.py:237
  14.4 1.8 %collective-permute-start.1 = (f32[32,128]{1,0:T(8,128)S(1)}, f32[32,128]{1,0:T(8,128)S(1)}, u32[]{:S(2)}, u32[]{:S(2)}) collective-permute-start(f32[32,128]{1,0:T(8,128)S(1)} %add.20), channel_id=1, source_target_pairs={{0,4},{1,5},{2,6},{3,7},{4,0},{5,1},{6,2},{7,3},{8,12},{9,13},{10,... | collective-permute-start | bytes 49160 | tf_op jit(solution)/shard_map/ppermute | solution.py:237
  16.2 1.9 %collective-permute-done.1 = f32[32,128]{1,0:T(8,128)S(1)} collective-permute-done((f32[32,128]{1,0:T(8,128)S(1)}, f32[32,128]{1,0:T(8,128)S(1)}, u32[]{:S(2)}, u32[]{:S(2)}) %collective-permute-start.1) | collective-permute-done | bytes 16416 | tf_op jit(solution)/shard_map/ppermute | solution.py:237
  18.1 2.8 %collective-permute-start.2 = (f32[32,128]{1,0:T(8,128)S(1)}, f32[32,128]{1,0:T(8,128)S(1)}, u32[]{:S(2)}, u32[]{:S(2)}) collective-permute-start(f32[32,128]{1,0:T(8,128)S(1)} %add.21), channel_id=1, source_target_pairs={{0,8},{1,9},{2,10},{3,11},{4,12},{5,13},{6,14},{7,15},{8,0},{9,1},... | collective-permute-start | bytes 49160 | tf_op jit(solution)/shard_map/ppermute | solution.py:237
  20.9 1.8 %collective-permute-done.2 = f32[32,128]{1,0:T(8,128)S(1)} collective-permute-done((f32[32,128]{1,0:T(8,128)S(1)}, f32[32,128]{1,0:T(8,128)S(1)}, u32[]{:S(2)}, u32[]{:S(2)}) %collective-permute-start.2) | collective-permute-done | bytes 16416 | tf_op jit(solution)/shard_map/ppermute | solution.py:237
  22.8 1.5 %collective-permute-start.3 = (f32[32,128]{1,0:T(8,128)S(1)}, f32[32,128]{1,0:T(8,128)S(1)}, u32[]{:S(2)}, u32[]{:S(2)}) collective-permute-start(f32[32,128]{1,0:T(8,128)S(1)} %add.22), channel_id=1, source_target_pairs={{0,2},{1,3},{2,0},{3,1},{4,6},{5,7},{6,4},{7,5},{8,10},{9,11},{10,... | collective-permute-start | bytes 49160 | tf_op jit(solution)/shard_map/ppermute | solution.py:237
  24.3 2.2 %collective-permute-done.3 = f32[32,128]{1,0:T(8,128)S(1)} collective-permute-done((f32[32,128]{1,0:T(8,128)S(1)}, f32[32,128]{1,0:T(8,128)S(1)}, u32[]{:S(2)}, u32[]{:S(2)}) %collective-permute-start.3) | collective-permute-done | bytes 16416 | tf_op jit(solution)/shard_map/ppermute | solution.py:237
  26.5 0.6 %add.23.sums_ref = f32[32,128]{1,0:T(8,128)} add(f32[32,128]{1,0:T(8,128)S(1)} %add.22, f32[32,128]{1,0:T(8,128)S(1)} %collective-permute-done.3) | non-fusion elementwise | flops 4096 | bytes 49152 | tf_op jit(solution)/shard_map/add | solution.py:237
  27.1 0.0 collective-permute-done.4.a_ref
  27.1 0.0 copy-start.1
  27.1 0.0 collective-permute-done.5.b_ref
  27.1 0.0 copy-start.2
  27.1 0.8 %copy-done.1 = f32[3,32,1440]{2,1,0:T(8,128)} copy-done((f32[3,32,1440]{2,1,0:T(8,128)}, f32[3,32,1440]{2,1,0:T(8,128)S(1)}, u32[]{:S(2)}) %copy-start.1) | copy-done | bytes 552984
  27.9 0.2 copy-done.2
  28.2 8.8 %finish.1 = f32[4,32,1440]{2,1,0:T(8,128)} custom-call(f32[64]{0:T(128)} %constant.46.clone.cos_ref.cos_row_ref, f32[65]{0:T(128)} %constant.47.clone.cos_face_ref, s32[64]{0:T(128)} %flags_ref.1, s32[64]{0:T(128)} %cutoffs_ref.1, f32[32,128]{1,0:T(8,128)} %add.23.sums_ref, f32[4,32,1440]{2,1,0:T(8,128)} %h_ref.3, f32[4,32,1440]{2,1,0:T(8,128)} %v_ref.1, ...), custom_call_target="tpu_custom_call" | custom-call | tf_op jit(solution)/shard_map/finish/pallas_call | solution.py:241
  (4 shorter events, 0.1 us)
Async XLA Ops:
  0.0 1.3 %copy-start = (f32[4,32,1440]{2,1,0:T(8,128)S(1)}, f32[4,32,1440]{2,1,0:T(8,128)}, u32[]{:S(2)}) copy-start(f32[4,32,1440]{2,1,0:T(8,128)} %h_ref.3) | copy-start | bytes 2211844
  1.4 1.4 %copy-start.3 = (f32[32]{0:T(128)S(1)}, f32[32]{0:T(128)}, u32[]{:S(2)}) copy-start(f32[32]{0:T(128)} %param.20) | copy-start | bytes 388
  1.4 2.1 %copy-start.4 = (f32[32]{0:T(128)S(1)}, f32[32]{0:T(128)}, u32[]{:S(2)}) copy-start(f32[32]{0:T(128)} %param.21) | copy-start | bytes 388
  1.5 25.6 %collective-permute-start.4 = (f32[3,32,1440]{2,1,0:T(8,128)S(1)}, f32[3,32,1440]{2,1,0:T(8,128)S(1)}, u32[]{:S(2)}, u32[]{:S(2)}) collective-permute-start(f32[3,32,1440]{2,1,0:T(8,128)S(1)} %pad_maximum_fusion), channel_id=1, source_target_pairs={{0,1},{2,3},{4,5},{6,7},{8,9},{10,11},{12,13},{14,15},{1,0},{3,2},... | collective-permute-start | bytes 1658888 | tf_op jit(solution)/shard_map/ppermute | solution.py:212
  2.1 25.0 %collective-permute-start.5 = (f32[3,32,1440]{2,1,0:T(8,128)S(1)}, f32[3,32,1440]{2,1,0:T(8,128)S(1)}, u32[]{:S(2)}, u32[]{:S(2)}) collective-permute-start(f32[3,32,1440]{2,1,0:T(8,128)S(1)} %pad_maximum_fusion.1), channel_id=1, source_target_pairs={{1,2},{3,4},{5,6},{7,8},{9,10},{11,12},{13,14},{2,1},{4,3},{6,5},{... | collective-permute-start | bytes 1658888 | tf_op jit(solution)/shard_map/ppermute | solution.py:211
  8.7 4.9 %collective-permute-start = (f32[32,128]{1,0:T(8,128)}, f32[32,128]{1,0:T(8,128)S(1)}, u32[]{:S(2)}, u32[]{:S(2)}) collective-permute-start(f32[32,128]{1,0:T(8,128)} %get-tuple-element.7), channel_id=1, source_target_pairs={{0,1},{1,0},{2,3},{3,2},{4,5},{5,4},{6,7},{7,6},{8,9},{9,8},{10,11... | collective-permute-start | bytes 49160 | tf_op jit(solution)/shard_map/ppermute | solution.py:237
  14.4 3.7 %collective-permute-start.1 = (f32[32,128]{1,0:T(8,128)S(1)}, f32[32,128]{1,0:T(8,128)S(1)}, u32[]{:S(2)}, u32[]{:S(2)}) collective-permute-start(f32[32,128]{1,0:T(8,128)S(1)} %add.20), channel_id=1, source_target_pairs={{0,4},{1,5},{2,6},{3,7},{4,0},{5,1},{6,2},{7,3},{8,12},{9,13},{10,... | collective-permute-start | bytes 49160 | tf_op jit(solution)/shard_map/ppermute | solution.py:237
  18.1 4.6 %collective-permute-start.2 = (f32[32,128]{1,0:T(8,128)S(1)}, f32[32,128]{1,0:T(8,128)S(1)}, u32[]{:S(2)}, u32[]{:S(2)}) collective-permute-start(f32[32,128]{1,0:T(8,128)S(1)} %add.21), channel_id=1, source_target_pairs={{0,8},{1,9},{2,10},{3,11},{4,12},{5,13},{6,14},{7,15},{8,0},{9,1},... | collective-permute-start | bytes 49160 | tf_op jit(solution)/shard_map/ppermute | solution.py:237
  22.8 3.7 %collective-permute-start.3 = (f32[32,128]{1,0:T(8,128)S(1)}, f32[32,128]{1,0:T(8,128)S(1)}, u32[]{:S(2)}, u32[]{:S(2)}) collective-permute-start(f32[32,128]{1,0:T(8,128)S(1)} %add.22), channel_id=1, source_target_pairs={{0,2},{1,3},{2,0},{3,1},{4,6},{5,7},{6,4},{7,5},{8,10},{9,11},{10,... | collective-permute-start | bytes 49160 | tf_op jit(solution)/shard_map/ppermute | solution.py:237
  27.1 0.8 %copy-start.1 = (f32[3,32,1440]{2,1,0:T(8,128)}, f32[3,32,1440]{2,1,0:T(8,128)S(1)}, u32[]{:S(2)}) copy-start(f32[3,32,1440]{2,1,0:T(8,128)S(1)} %collective-permute-done.4.a_ref) | copy-start | bytes 1658884
  27.1 1.1 %copy-start.2 = (f32[3,32,1440]{2,1,0:T(8,128)}, f32[3,32,1440]{2,1,0:T(8,128)S(1)}, u32[]{:S(2)}) copy-start(f32[3,32,1440]{2,1,0:T(8,128)S(1)} %collective-permute-done.5.b_ref) | copy-start | bytes 1658884

commit v2 on v1

v2 whole, which is shorter than its diff:
```python
import functools

import jax
import jax.numpy as jnp
import numpy as np
from jax import lax
from jax.experimental import pallas as pl
from jax.experimental.pallas import tpu as pltpu
from jax.sharding import PartitionSpec as P

LANES = 128


def round_up(value, step):
    return -(-value // step) * step


@functools.cache
def phases(nlon):
    half = nlon // 2
    width = round_up(half // 2 + 1, LANES)
    depth = round_up(half, LANES)
    points = np.arange(depth)
    arrays = []
    for parity in (0, 1):
        waves = 2 * np.arange(width) + parity
        lanes = (waves <= half)[None, :]

        def both(steps, valid, axis):
            angle = 2.0 * np.pi / nlon * (steps % nlon)
            return np.concatenate([np.cos(angle) * valid, np.sin(angle) * valid], axis=axis)

        blocks = [
            both(points[::8, None] * waves[None, :], lanes & (points[::8, None] < half), 1),
            both(points[:8, None] * waves[None, :], True, 1),
            both(16 * np.arange(width // 8)[:, None] * points[None, :], (points < half)[None, :], 0),
            both(waves[:8, None] * points[None, :], True, 0),
        ]
        columns = max(x.shape[1] for x in blocks)
        arrays.append(
            np.concatenate([np.pad(x, ((0, 0), (0, columns - x.shape[1]))) for x in blocks]).astype(np.float32)
        )
    return arrays


def softplus(s):
    return jnp.maximum(s, 0.0) + jnp.log(1.0 + jnp.exp(-jnp.abs(s)))


def wrapped(row, nlon, full):
    base = nlon // LANES * LANES
    rest = nlon - base
    body, tail = row[:, :base], row[:, base:]
    tail = jnp.concatenate([tail, jnp.zeros((row.shape[0], full - nlon), row.dtype)], axis=1)
    lane = lax.broadcasted_iota(jnp.int32, tail.shape, 1)
    head = pltpu.roll(row[:, : full - base], rest, 1)
    end = pltpu.roll(tail, full - base - rest, 1)
    tail = jnp.where(lane < rest, tail, jnp.where(lane < full - base - 8, head, end))
    return jnp.concatenate([body, tail], axis=1)


def column(row):
    count = row.shape[1]
    same = lax.broadcasted_iota(jnp.int32, (count, count), 0) == lax.broadcasted_iota(
        jnp.int32, (count, count), 1
    )
    return jnp.sum(jnp.where(same, row, 0.0), axis=1, keepdims=True)


def dense_tiles(levels, nlon):
    rest = nlon % LANES
    shared = LANES // rest if rest else 1
    whole = levels // 8 * (nlon // LANES)
    return whole, shared, (-(-(levels // 8) // shared) if rest else 0)


def pack_row(row, out_ref, i):
    levels, nlon = row.shape
    whole, shared, extra = dense_tiles(levels, nlon)
    per = nlon // LANES
    rest = nlon % LANES
    for t in range(whole):
        g, k = divmod(t, per)
        out_ref[i, 8 * t : 8 * t + 8, :] = row[8 * g : 8 * g + 8, k * LANES : (k + 1) * LANES]
    for e in range(extra):
        parts = [
            row[8 * g : 8 * g + 8, per * LANES :]
            for g in range(e * shared, min((e + 1) * shared, levels // 8))
        ]
        parts.append(jnp.zeros((8, LANES - rest * len(parts)), row.dtype))
        t = whole + e
        out_ref[i, 8 * t : 8 * t + 8, :] = jnp.concatenate([p for p in parts if p.shape[1]], axis=1)


def unpack_row(ref, i, levels, nlon):
    whole, shared, _ = dense_tiles(levels, nlon)
    per = nlon // LANES
    rest = nlon % LANES
    groups = []
    for g in range(levels // 8):
        parts = [ref[i, 8 * t : 8 * t + 8, :] for t in range(g * per, (g + 1) * per)]
        if rest:
            t = whole + g // shared
            last = ref[i, 8 * t : 8 * t + 8, :]
            at = g % shared * rest
            parts.append((pltpu.roll(last, LANES - at, 1) if at else last)[:, :rest])
        groups.append(jnp.concatenate(parts, axis=1))
    return jnp.concatenate(groups, axis=0)


def pack_kernel(h_ref, v_ref, out_ref, edge_ref, sem):
    rows = h_ref.shape[0]
    odd = lax.axis_index("lat") % 2 == 1
    two = jnp.where(odd, rows - 2, 0)
    one = jnp.where(odd, rows - 1, 0)
    copies = [
        pltpu.make_async_copy(h_ref.at[pl.ds(two, 2)], edge_ref.at[pl.ds(0, 2)], sem.at[0]),
        pltpu.make_async_copy(v_ref.at[pl.ds(one, 1)], edge_ref.at[pl.ds(2, 1)], sem.at[1]),
    ]
    for c in copies:
        c.start()
    for c in copies:
        c.wait()
    for i in range(3):
        pack_row(edge_ref[i], out_ref, i)


def source_kernel(cos_ref, rates_ref, thresholds_ref, h_ref, v_ref, edge_ref, sum_ref, out_ref):
    rows, levels, nlon = h_ref.shape
    full = round_up(nlon, LANES)
    base = base_of(nlon)
    position = lax.axis_index("lat")
    first = position * rows
    rates = column(rates_ref[...])
    thresholds = column(thresholds_ref[...])
    total = jnp.zeros((levels, LANES), jnp.float32)
    for j in range(rows):
        s = softplus(h_ref[j] - thresholds) * -rates
        out_ref[j] = s
        acc = s[:, 0:LANES]
        for t in range(1, nlon // LANES):
            acc = acc + s[:, t * LANES : (t + 1) * LANES]
        if base < nlon:
            acc = acc + jnp.concatenate(
                [s[:, base:], jnp.zeros((levels, full - nlon), jnp.float32)], axis=1
            )
        total = total + acc * cos_ref[first + j]
    total = jnp.broadcast_to(jnp.sum(total, axis=1, keepdims=True), (levels, LANES))
    sum_ref[...] = total
    even = position % 2 == 0
    two = jnp.where(even, rows - 2, 0)
    one = jnp.where(even, rows - 1, 0)
    edge_ref[0, :, :nlon] = h_ref[two]
    edge_ref[1, :, :nlon] = h_ref[two + 1]
    edge_ref[2, :, :nlon] = v_ref[one]
    edge_ref[3, :, :LANES] = total


def zonal_kernel(h_ref, u_ref, s_ref, out_ref):
    rows, _, nlon = h_ref.shape
    full = round_up(nlon, LANES)
    for j in range(rows):
        h0 = h_ref[j]
        h = wrapped(h0, nlon, full)
        u = wrapped(u_ref[j], nlon, full)
        east = pltpu.roll(h, full - 1, 1)
        far_east = pltpu.roll(h, full - 2, 1)
        west = pltpu.roll(h, 1, 1)
        face = (7.0 * (h + east) - (west + far_east)) * (0.5 / 12.0)
        flux = (u + pltpu.roll(u, full - 1, 1)) * face
        div = flux - pltpu.roll(flux, 1, 1)
        out_ref[j] = h0 - div[:, :nlon] + s_ref[j]


def table_kernel(parity, half, source_ref, high_ref, low_ref, high_t_ref, low_t_ref):
    depth, cols = high_ref.shape
    width = cols // 2

    def put(high, low, at, cols, values):
        h = values.astype(jnp.bfloat16)
        high[at, cols] = h
        low[at, cols] = (values - h.astype(jnp.float32)).astype(jnp.bfloat16)

    def fill(coarse_cos, coarse_sin, fine_cos, fine_sin, count, store):
        for k in range(0, count, 2):
            pieces = []
            for q in (k, k + 1):
                cc, cs = coarse_cos(q), coarse_sin(q)
                pieces.append((cc * fine_cos - cs * fine_sin, cs * fine_cos + cc * fine_sin))
            store(k, *[jnp.concatenate(p, axis=0) for p in zip(*pieces)])

    def store(k, c, s):
        at = slice(8 * k, 8 * k + 16)
        put(high_ref, low_ref, at, slice(0, width), c)
        put(high_ref, low_ref, at, slice(width, cols), s)

    def store_t(k, c, s):
        if 2 * (8 * k + 15) + parity > half:
            waves = 2 * (8 * k + lax.broadcasted_iota(jnp.int32, c.shape, 0)) + parity
            c, s = jnp.where(waves <= half, c, 0.0), jnp.where(waves <= half, s, 0.0)
        put(high_t_ref, low_t_ref, slice(8 * k, 8 * k + 16), slice(None), c)
        put(high_t_ref, low_t_ref, slice(width + 8 * k, width + 8 * k + 16), slice(None), s)

    fine = depth // 8
    turned = fine + 8
    fine_t = turned + 2 * (width // 8)
    fill(
        lambda q: source_ref[q : q + 1, :width],
        lambda q: source_ref[q : q + 1, width:cols],
        source_ref[fine : fine + 8, :width],
        source_ref[fine : fine + 8, width:cols],
        depth // 8,
        store,
    )
    fill(
        lambda q: source_ref[turned + q : turned + q + 1, :depth],
        lambda q: source_ref[turned + width // 8 + q : turned + width // 8 + q + 1, :depth],
        source_ref[fine_t : fine_t + 8, :depth],
        source_ref[fine_t + 8 : fine_t + 16, :depth],
        width // 8,
        store_t,
    )


def finish_kernel(
    cos_row_ref,
    cos_face_ref,
    flags_ref,
    cutoffs_ref,
    sums_ref,
    h_ref,
    v_ref,
    part_ref,
    a_ref,
    b_ref,
    *rest,
):
    tables, (out_ref, u_ref) = rest[:8], rest[8:]
    rows, levels, nlon = h_ref.shape
    full = round_up(nlon, LANES)
    half = nlon // 2
    depth, cols = tables[0].shape
    width = cols // 2
    position = lax.axis_index("lat")
    first = position * rows
    odd = position % 2 == 1
    area = nlon * float(np.sum(np.sin(np.pi * (np.arange(cos_row_ref.shape[0]) + 0.5) / cos_row_ref.shape[0])))
    mean = sums_ref[:, :1] * (1.0 / area)

    b_rows = [unpack_row(b_ref, i, levels, nlon) for i in range(3)]
    below = [jnp.where(odd, a_ref[i], b_rows[i]) for i in range(3)]
    above = [jnp.where(odd, b_rows[i], a_ref[i]) for i in range(3)]
    height = [below[0], below[1]] + [h_ref[j] for j in range(rows)] + [above[0], above[1]]
    speed = [below[2]] + [v_ref[j] for j in range(rows)] + [above[2]]
    flux = []
    for f in range(rows + 1):
        p = 7.0 * (height[f + 1] + height[f + 2]) - (height[f] + height[f + 3])
        c = cos_face_ref[first + f] * (0.5 / 12.0)
        flux.append((speed[f] + speed[f + 1]) * c * p)
    marked = flags_ref[first]
    for j in range(1, rows):
        marked = jnp.maximum(marked, flags_ref[first + j])

    def updated(j):
        return part_ref[j] - (flux[j + 1] - flux[j]) * (1.0 / cos_row_ref[first + j])

    @pl.when(marked == 0)
    def _():
        for j in range(rows):
            out_ref[j] = updated(j) - mean

    @pl.when(marked > 0)
    def _():
        u_ref[:, base_of(nlon):] = jnp.zeros((rows * levels, full - base_of(nlon)), jnp.float32)
        for j in range(rows):
            u_ref[j * levels : (j + 1) * levels, :nlon] = updated(j)
        x = u_ref[...]
        near = x[:, :depth]
        far = pltpu.roll(x, full - half, 1)[:, :depth]
        removed = []
        lane = lax.broadcasted_iota(jnp.int32, (1, width), 1)
        for parity in (0, 1):
            y = near + far if parity == 0 else near - far
            fwd_high, fwd_low, inv_high, inv_low = (t[...] for t in tables[4 * parity : 4 * parity + 4])
            spectrum = product(y, fwd_high, fwd_low)
            waves = 2 * lane + parity
            weight = jnp.where((waves > 0) & (waves < half), 2.0 / nlon, 1.0 / nlon)
            inverse = 1.0 / jnp.maximum(waves, 1).astype(jnp.float32)
            pieces = []
            for j in range(rows):
                ratio = cutoffs_ref[first + j].astype(jnp.float32) * inverse
                factor = (1.0 - jnp.minimum(1.0, ratio * ratio)) * weight
                factor = jnp.where(flags_ref[first + j] > 0, factor, 0.0)
                factor = jnp.concatenate([factor, factor], axis=1)
                pieces.append(spectrum[j * levels : (j + 1) * levels] * factor)
            removed.append(product(jnp.concatenate(pieces, axis=0), inv_high, inv_low))
        zeros = jnp.zeros((rows * levels, full - depth), jnp.float32)
        r1 = jnp.concatenate([removed[0] + removed[1], zeros], axis=1)
        r2 = jnp.concatenate([removed[0] - removed[1], zeros], axis=1)
        y = x - r1 - pltpu.roll(r2, half, 1)
        for j in range(rows):
            cut = cutoffs_ref[first + j].astype(jnp.float32)
            kept = jnp.where(flags_ref[first + j] > 0, jnp.minimum(1.0, cut * cut), 1.0)
            out_ref[j] = y[j * levels : (j + 1) * levels, :nlon] - mean * kept


def base_of(nlon):
    return nlon // LANES * LANES


def product(y, high, low):
    y_high = y.astype(jnp.bfloat16)
    y_low = (y - y_high.astype(jnp.float32)).astype(jnp.bfloat16)
    count = y.shape[0]
    both = jnp.dot(
        jnp.concatenate([y_high, y_low], axis=0), high, preferred_element_type=jnp.float32
    )
    return both[:count] + both[count:] + jnp.dot(y_high, low, preferred_element_type=jnp.float32)


def call(kernel, ins, outs, megabytes, scratch=()):
    return pl.pallas_call(
        kernel,
        in_specs=[pl.BlockSpec(memory_space=space) for _, space in ins],
        out_specs=[pl.BlockSpec(memory_space=pltpu.VMEM) for _ in outs],
        out_shape=[jax.ShapeDtypeStruct(shape, dtype) for shape, dtype in outs],
        scratch_shapes=list(scratch),
        compiler_params=pltpu.CompilerParams(vmem_limit_bytes=megabytes << 20),
    )(*[x for x, _ in ins])


def permute(x, pairs):
    return lax.ppermute(x, "lat", pairs)


def step(height, zonal_courant, merid_courant, rates, thresholds, flags, cutoffs):
    rows, levels, nlon = height.shape
    count = lax.axis_size("lat")
    nlat = rows * count
    full = round_up(nlon, LANES)
    half = nlon // 2
    smem, vmem, hbm = pltpu.SMEM, pltpu.VMEM, pltpu.HBM
    f32 = jnp.float32

    between = [(i, i + 1) for i in range(1, count - 1, 2)]
    within = [(i, i + 1) for i in range(0, count - 1, 2)]
    between = between + [(j, i) for i, j in between]
    within = within + [(j, i) for i, j in within]
    whole, _, extra = dense_tiles(levels, nlon)
    (edge_b,) = call(
        pack_kernel,
        [(height, hbm), (merid_courant, hbm)],
        [((3, 8 * (whole + extra), LANES), f32)],
        4,
        [pltpu.VMEM((3, levels, nlon), f32), pltpu.SemaphoreType.DMA((2,))],
    )
    b = permute(edge_b, between)

    cos_row = jnp.asarray(np.sin(np.pi * (np.arange(nlat) + 0.5) / nlat).astype(np.float32))
    faces = np.sin(np.pi * np.arange(nlat + 1) / nlat)
    faces[0] = faces[nlat] = 0.0
    cos_face = jnp.asarray(faces.astype(np.float32))
    edge_a, sums, source = call(
        source_kernel,
        [(cos_row, smem), (rates[None], vmem), (thresholds[None], vmem), (height, vmem), (merid_courant, vmem)],
        [((4, levels, nlon), f32), ((levels, LANES), f32), (height.shape, f32)],
        8,
    )
    a = permute(edge_a, within)
    (part,) = call(zonal_kernel, [(height, vmem), (zonal_courant, vmem), (source, vmem)], [(height.shape, f32)], 8)
    depth = round_up(half, LANES)
    cols = 2 * round_up(half // 2 + 1, LANES)
    tables = []
    for parity in (0, 1):
        tables += call(
            functools.partial(table_kernel, parity, half),
            [(jnp.asarray(phases(nlon)[parity]), vmem)],
            [((depth, cols), jnp.bfloat16)] * 2 + [((cols, depth), jnp.bfloat16)] * 2,
            8,
        )

    bits = [1 << i for i in range((count - 1).bit_length())]
    if count == 1 << len(bits):
        sums = sums + a[3, :, :LANES]
        for d in bits[2:] + bits[1:2]:
            sums = sums + permute(sums, [(i, i ^ d) for i in range(count)])
    else:
        sums = lax.psum(sums, "lat")

    (out,) = call(
        finish_kernel,
        [(cos_row, smem), (cos_face, smem), (flags, smem), (cutoffs, smem)]
        + [(x, vmem) for x in (sums, height, merid_courant, part, a, b, *tables)],
        [(height.shape, f32)],
        24,
        [pltpu.VMEM((rows * levels, full), f32)],
    )
    return out


def solution(mesh):
    split_rows = P(("member", "lat"), None, None)
    return jax.shard_map(
        step,
        mesh=mesh,
        in_specs=(split_rows, split_rows, split_rows, P("member"), P("member"), P(), P()),
        out_specs=split_rows,
        check_vma=False,
    )
```

time: 37.3 us -> 33.9 us (0.909)
  Pallas kernels: 13.4 us -> 10 us
  waiting for transfers between devices: 7.06 us -> 10.3 us
  starting transfers between devices: 11.2 us -> 8.84 us
  other arithmetic: 1.41 us -> 0.02 us
  local copies, waits for them, and re-layouts: 3.81 us -> 4.28 us
    pallas_call x2 -> x6, Pallas kernels: 13.4 us -> 10 us  [call(): pl.pallas_call(kernel, in_specs=[pl.BlockSpec(memory_space=space) for _,...]
    ppermute x6 -> x5, waiting for transfers between devices: 7.06 us -> 10.3 us  [permute(): return lax.ppermute(x, 'lat', pairs)]
    unnamed x10 -> x28, local copies, waits for them, and re-layouts: 1.26 us -> 4.28 us
    ppermute x6 -> x5, starting transfers between devices: 11.2 us -> 8.84 us  [permute(): return lax.ppermute(x, 'lat', pairs)]
    broadcast_in_dim x2 -> x0, local copies, waits for them, and re-layouts: 1.38 us -> none  [the longest x1 0.69 us: local(): rates[:, None]]
    add x4, other arithmetic: 1.33 us -> 0.02 us  [the longest x3 0.01 us: step(): sums = sums + permute(sums, [(i, i ^ d) for i in range(count)])]
    dynamic_slice x2 -> x0, local copies, waits for them, and re-layouts: 1.17 us -> none  [the longest x1 1.12 us: edge(): lax.dynamic_slice_in_dim(merid_courant, one, 1, 0)]
  transfers between devices with their start and end apart: 6 -> 5, of which waited for: 4 -> 3; matrix products, arithmetic and copies ran while one was open for 7% -> 0% of each run, Pallas kernels for 12% -> 13%
where the time goes in v2:
time: 33.9 us; the launch traced here: 33.6 us
  waiting for transfers between devices  10.3 us (30%)
  Pallas kernels  10 us (29%)
  starting transfers between devices  8.84 us (26%)
  local copies, waits for them, and re-layouts  4.28 us (13%)
    ppermute x5, waiting for transfers between devices, permute(): return lax.ppermute(x, 'lat', pairs)  10.3 us
    pallas_call x6, Pallas kernels, call(): pl.pallas_call(kernel, in_specs=[pl.BlockSpec(memory_space=space) for _,...  10 us
    ppermute x5, starting transfers between devices, permute(): return lax.ppermute(x, 'lat', pairs)  8.84 us
    unnamed x28, local copies, waits for them, and re-layouts  4.28 us
  transfers between devices with their start and end apart: 5, of which 3 were waited for; matrix products, arithmetic and copies ran while one was open for 0% of the time, Pallas kernels for 13%

profile of v2, /device:TPU:0, one launch (start us, length us, event | category | flops | bytes accessed | tf_op | source)
XLA Modules:
  0.0 33.6 jit_solution(8854836250252237830)
XLA Ops:
  0.0 0.0 copy-start
  0.0 1.1 %copy-done = f32[4,32,1440]{2,1,0:T(8,128)S(1)} copy-done((f32[4,32,1440]{2,1,0:T(8,128)S(1)}, f32[4,32,1440]{2,1,0:T(8,128)}, u32[]{:S(2)}) %copy-start) | copy-done | bytes 737304
  1.1 0.0 copy-start.2
  1.1 1.1 %copy-done.2 = f32[4,32,1440]{2,1,0:T(8,128)S(1)} copy-done((f32[4,32,1440]{2,1,0:T(8,128)S(1)}, f32[4,32,1440]{2,1,0:T(8,128)}, u32[]{:S(2)}) %copy-start.2) | copy-done | bytes 737304
  2.3 0.0 copy-start.7
  2.3 0.7 %copy-done.7 = f32[64]{0:T(128)S(1)} copy-done((f32[64]{0:T(128)S(1)}, f32[64]{0:T(128)}, u32[]{:S(2)}) %copy-start.7) | copy-done | bytes 280
  2.9 0.0 copy-start.9
  2.9 0.7 %copy-done.9 = f32[32]{0:T(128)S(1)} copy-done((f32[32]{0:T(128)S(1)}, f32[32]{0:T(128)}, u32[]{:S(2)}) %copy-start.9) | copy-done | bytes 152
  3.6 0.0 copy-start.10
  3.6 0.7 %copy-done.10 = f32[32]{0:T(128)S(1)} copy-done((f32[32]{0:T(128)S(1)}, f32[32]{0:T(128)}, u32[]{:S(2)}) %copy-start.10) | copy-done | bytes 152
  4.2 1.0 %shard_map.109 = (f32[4,32,1440]{2,1,0:T(8,128)S(1)}, f32[32,128]{1,0:T(8,128)S(1)}, f32[4,32,1440]{2,1,0:T(8,128)S(1)}) custom-call(f32[64]{0:T(128)S(1)} %copy-done.7, f32[1,32]{1,0:T(1,128)S(1)} %bitcast.6, f32[1,32]{1,0:T(1,128)S(1)} %bitcast.7, f32[4,32,1440]{2,1,0:T(8,128)S(1)} %copy-done, f32[4,32,1440]{2,1,0:T(8,128)S(1)} %copy-done.2), custom_call_target="tpu_custom_call" | custom-call | tf_op jit(solution)/shard_map/pallas_call | solution.py:322
  5.3 0.0 copy-start.6
  5.3 0.0 copy-start.5
  5.3 0.5 %collective-permute-start = (f32[4,32,1440]{2,1,0:T(8,128)S(1)}, f32[4,32,1440]{2,1,0:T(8,128)S(1)}, u32[]{:S(2)}, u32[]{:S(2)}) collective-permute-start(f32[4,32,1440]{2,1,0:T(8,128)S(1)} %get-tuple-element.17), channel_id=1, source_target_pairs={{0,1},{2,3},{4,5},{6,7},{8,9},{10,11},{12,13},{14,15},{1,0},{3,2},... | collective-permute-start | bytes 2211848 | tf_op jit(solution)/shard_map/ppermute | solution.py:333
  5.8 0.0 copy-start.4
  5.8 0.6 %shard_map.111 = f32[3,360,128]{2,1,0:T(8,128)S(1)} custom-call(f32[4,32,1440]{2,1,0:T(8,128)S(1)} %copy-done, f32[4,32,1440]{2,1,0:T(8,128)S(1)} %copy-done.2), custom_call_target="tpu_custom_call" | custom-call | tf_op jit(solution)/shard_map/pallas_call | solution.py:322
  6.4 0.0 copy-start.1
  6.4 0.8 %collective-permute-start.4 = (f32[3,360,128]{2,1,0:T(8,128)S(1)}, f32[3,360,128]{2,1,0:T(8,128)S(1)}, u32[]{:S(2)}, u32[]{:S(2)}) collective-permute-start(f32[3,360,128]{2,1,0:T(8,128)S(1)} %shard_map.111), channel_id=1, source_target_pairs={{1,2},{3,4},{5,6},{7,8},{9,10},{11,12},{13,14},{2,1},{4,3},{6,5},{... | collective-permute-start | bytes 1658888 | tf_op jit(solution)/shard_map/ppermute | solution.py:333
  7.2 0.5 %collective-permute-done.a_ref = f32[4,32,1440]{2,1,0:T(8,128)S(1)} collective-permute-done((f32[4,32,1440]{2,1,0:T(8,128)S(1)}, f32[4,32,1440]{2,1,0:T(8,128)S(1)}, u32[]{:S(2)}, u32[]{:S(2)}) %collective-permute-start) | collective-permute-done | bytes 737312 | tf_op jit(solution)/shard_map/ppermute | solution.py:333
  7.7 4.9 %collective-permute-start.1 = (f32[32,128]{1,0:T(8,128)S(1)}, f32[32,128]{1,0:T(8,128)S(1)}, u32[]{:S(2)}, u32[]{:S(2)}) collective-permute-start(f32[32,128]{1,0:T(8,128)S(1)} %fusion), channel_id=1, source_target_pairs={{0,4},{1,5},{2,6},{3,7},{4,0},{5,1},{6,2},{7,3},{8,12},{9,13},{10,... | collective-permute-start | bytes 49160 | tf_op jit(solution)/shard_map/ppermute | solution.py:333
  12.6 7.7 %collective-permute-done.1 = f32[32,128]{1,0:T(8,128)S(1)} collective-permute-done((f32[32,128]{1,0:T(8,128)S(1)}, f32[32,128]{1,0:T(8,128)S(1)}, u32[]{:S(2)}, u32[]{:S(2)}) %collective-permute-start.1) | collective-permute-done | bytes 16416 | tf_op jit(solution)/shard_map/ppermute | solution.py:333
  20.4 2.6 %collective-permute-start.2 = (f32[32,128]{1,0:T(8,128)S(1)}, f32[32,128]{1,0:T(8,128)S(1)}, u32[]{:S(2)}, u32[]{:S(2)}) collective-permute-start(f32[32,128]{1,0:T(8,128)S(1)} %add.13), channel_id=1, source_target_pairs={{0,8},{1,9},{2,10},{3,11},{4,12},{5,13},{6,14},{7,15},{8,0},{9,1},... | collective-permute-start | bytes 49160 | tf_op jit(solution)/shard_map/ppermute | solution.py:333
  22.9 2.0 %collective-permute-done.2 = f32[32,128]{1,0:T(8,128)S(1)} collective-permute-done((f32[32,128]{1,0:T(8,128)S(1)}, f32[32,128]{1,0:T(8,128)S(1)}, u32[]{:S(2)}, u32[]{:S(2)}) %collective-permute-start.2) | collective-permute-done | bytes 16416 | tf_op jit(solution)/shard_map/ppermute | solution.py:333
  25.0 0.0 collective-permute-start.3
  25.0 0.0 copy-done.6
  25.0 1.2 %shard_map.112 = (bf16[768,768]{1,0:T(8,128)(2,1)S(1)}, bf16[768,768]{1,0:T(8,128)(2,1)S(1)}, bf16[768,768]{1,0:T(8,128)(2,1)S(1)}, bf16[768,768]{1,0:T(8,128)(2,1)S(1)}) custom-call(f32[216,768]{1,0:T(8,128)S(1)} %copy-done.6), custom_call_target="tpu_custom_call" | custom-call | tf_op jit(solution)/shard_map/pallas_call | solution.py:322
  26.2 0.0 copy-done.5
  26.2 1.2 %shard_map.113 = (bf16[768,768]{1,0:T(8,128)(2,1)S(1)}, bf16[768,768]{1,0:T(8,128)(2,1)S(1)}, bf16[768,768]{1,0:T(8,128)(2,1)S(1)}, bf16[768,768]{1,0:T(8,128)(2,1)S(1)}) custom-call(f32[216,768]{1,0:T(8,128)S(1)} %copy-done.5), custom_call_target="tpu_custom_call" | custom-call | tf_op jit(solution)/shard_map/pallas_call | solution.py:322
  27.4 0.0 copy-done.4
  27.4 0.0 copy-done.1
  27.4 0.0 copy-start.3
  27.4 0.0 copy-start.8
  27.4 0.0 copy-start.11
  27.4 0.0 copy-start.12
  27.5 0.0 copy-start.13
  27.5 1.3 %shard_map.110.part_ref = f32[4,32,1440]{2,1,0:T(8,128)S(1)} custom-call(f32[4,32,1440]{2,1,0:T(8,128)S(1)} %copy-done.1, f32[4,32,1440]{2,1,0:T(8,128)S(1)} %copy-done.4, f32[4,32,1440]{2,1,0:T(8,128)S(1)} %get-tuple-element.18.s_ref), custom_call_target="tpu_custom_call" | custom-call | tf_op jit(solution)/shard_map/pallas_call | solution.py:322
  28.8 0.0 collective-permute-done.3
  28.8 0.0 collective-permute-done.4.b_ref
  28.9 0.0 copy-done.3
  28.9 0.0 copy-done.8
  28.9 0.0 copy-done.11
  28.9 0.0 copy-done.12
  28.9 0.0 copy-done.13
  28.9 4.7 %shard_map.114 = f32[4,32,1440]{2,1,0:T(8,128)} custom-call(f32[64]{0:T(128)S(1)} %copy-done.8, f32[65]{0:T(128)S(1)} %copy-done.13, s32[64]{0:T(128)S(1)} %copy-done.11, s32[64]{0:T(128)S(1)} %copy-done.12, f32[32,128]{1,0:T(8,128)S(1)} %add.15.sums_ref, f32[4,32,1440]{2,1,0:T(8,128)S(1)} %copy-done.1, f32[4,32,1440]{2,1,0:T(8,128)S(1)} %copy-done.3, ...), custom_call_target="tpu_custom_call" | custom-call | tf_op jit(solution)/shard_map/pallas_call | solution.py:322
  (4 shorter events, 0.0 us)
Async XLA Ops:
  0.0 1.1 %copy-start = (f32[4,32,1440]{2,1,0:T(8,128)S(1)}, f32[4,32,1440]{2,1,0:T(8,128)}, u32[]{:S(2)}) copy-start(f32[4,32,1440]{2,1,0:T(8,128)} %h_ref.7) | copy-start | bytes 2211844
  1.1 1.1 %copy-start.2 = (f32[4,32,1440]{2,1,0:T(8,128)S(1)}, f32[4,32,1440]{2,1,0:T(8,128)}, u32[]{:S(2)}) copy-start(f32[4,32,1440]{2,1,0:T(8,128)} %v_ref.5) | copy-start | bytes 2211844
  2.3 0.7 %copy-start.7 = (f32[64]{0:T(128)S(1)}, f32[64]{0:T(128)}, u32[]{:S(2)}) copy-start(f32[64]{0:T(128)} %constant.8.clone.cos_ref.cos_row_ref) | copy-start | bytes 772
  2.9 0.7 %copy-start.9 = (f32[32]{0:T(128)S(1)}, f32[32]{0:T(128)}, u32[]{:S(2)}) copy-start(f32[32]{0:T(128)} %param.14) | copy-start | bytes 388
  3.6 0.7 %copy-start.10 = (f32[32]{0:T(128)S(1)}, f32[32]{0:T(128)}, u32[]{:S(2)}) copy-start(f32[32]{0:T(128)} %param.15) | copy-start | bytes 388
  5.3 19.8 %copy-start.6 = (f32[216,768]{1,0:T(8,128)S(1)}, f32[216,768]{1,0:T(8,128)}, u32[]{:S(2)}) copy-start(f32[216,768]{1,0:T(8,128)} %constant.10.clone.source_ref) | copy-start | bytes 1990660
  5.3 20.9 %copy-start.5 = (f32[216,768]{1,0:T(8,128)S(1)}, f32[216,768]{1,0:T(8,128)}, u32[]{:S(2)}) copy-start(f32[216,768]{1,0:T(8,128)} %constant.11.clone.source_ref) | copy-start | bytes 1990660
  5.3 2.4 %collective-permute-start = (f32[4,32,1440]{2,1,0:T(8,128)S(1)}, f32[4,32,1440]{2,1,0:T(8,128)S(1)}, u32[]{:S(2)}, u32[]{:S(2)}) collective-permute-start(f32[4,32,1440]{2,1,0:T(8,128)S(1)} %get-tuple-element.17), channel_id=1, source_target_pairs={{0,1},{2,3},{4,5},{6,7},{8,9},{10,11},{12,13},{14,15},{1,0},{3,2},... | collective-permute-start | bytes 2211848 | tf_op jit(solution)/shard_map/ppermute | solution.py:333
  5.8 21.6 %copy-start.4 = (f32[4,32,1440]{2,1,0:T(8,128)S(1)}, f32[4,32,1440]{2,1,0:T(8,128)}, u32[]{:S(2)}) copy-start(f32[4,32,1440]{2,1,0:T(8,128)} %u_ref.1) | copy-start | bytes 2211844
  6.4 21.0 %copy-start.1 = (f32[4,32,1440]{2,1,0:T(8,128)S(1)}, f32[4,32,1440]{2,1,0:T(8,128)}, u32[]{:S(2)}) copy-start(f32[4,32,1440]{2,1,0:T(8,128)} %h_ref.7) | copy-start | bytes 2211844
  6.4 22.5 %collective-permute-start.4 = (f32[3,360,128]{2,1,0:T(8,128)S(1)}, f32[3,360,128]{2,1,0:T(8,128)S(1)}, u32[]{:S(2)}, u32[]{:S(2)}) collective-permute-start(f32[3,360,128]{2,1,0:T(8,128)S(1)} %shard_map.111), channel_id=1, source_target_pairs={{1,2},{3,4},{5,6},{7,8},{9,10},{11,12},{13,14},{2,1},{4,3},{6,5},{... | collective-permute-start | bytes 1658888 | tf_op jit(solution)/shard_map/ppermute | solution.py:333
  7.7 12.6 %collective-permute-start.1 = (f32[32,128]{1,0:T(8,128)S(1)}, f32[32,128]{1,0:T(8,128)S(1)}, u32[]{:S(2)}, u32[]{:S(2)}) collective-permute-start(f32[32,128]{1,0:T(8,128)S(1)} %fusion), channel_id=1, source_target_pairs={{0,4},{1,5},{2,6},{3,7},{4,0},{5,1},{6,2},{7,3},{8,12},{9,13},{10,... | collective-permute-start | bytes 49160 | tf_op jit(solution)/shard_map/ppermute | solution.py:333
  20.4 4.6 %collective-permute-start.2 = (f32[32,128]{1,0:T(8,128)S(1)}, f32[32,128]{1,0:T(8,128)S(1)}, u32[]{:S(2)}, u32[]{:S(2)}) collective-permute-start(f32[32,128]{1,0:T(8,128)S(1)} %add.13), channel_id=1, source_target_pairs={{0,8},{1,9},{2,10},{3,11},{4,12},{5,13},{6,14},{7,15},{8,0},{9,1},... | collective-permute-start | bytes 49160 | tf_op jit(solution)/shard_map/ppermute | solution.py:333
  25.0 3.8 %collective-permute-start.3 = (f32[32,128]{1,0:T(8,128)S(1)}, f32[32,128]{1,0:T(8,128)S(1)}, u32[]{:S(2)}, u32[]{:S(2)}) collective-permute-start(f32[32,128]{1,0:T(8,128)S(1)} %add.14), channel_id=1, source_target_pairs={{0,2},{1,3},{2,0},{3,1},{4,6},{5,7},{6,4},{7,5},{8,10},{9,11},{10,... | collective-permute-start | bytes 49160 | tf_op jit(solution)/shard_map/ppermute | solution.py:333
  27.4 1.5 %copy-start.3 = (f32[4,32,1440]{2,1,0:T(8,128)S(1)}, f32[4,32,1440]{2,1,0:T(8,128)}, u32[]{:S(2)}) copy-start(f32[4,32,1440]{2,1,0:T(8,128)} %v_ref.5) | copy-start | bytes 2211844
  27.4 1.5 %copy-start.8 = (f32[64]{0:T(128)S(1)}, f32[64]{0:T(128)}, u32[]{:S(2)}) copy-start(f32[64]{0:T(128)} %constant.8.clone.cos_ref.cos_row_ref) | copy-start | bytes 772
  27.4 1.4 %copy-start.11 = (s32[64]{0:T(128)S(1)}, s32[64]{0:T(128)}, u32[]{:S(2)}) copy-start(s32[64]{0:T(128)} %flags_ref.1) | copy-start | bytes 772
  27.4 1.4 %copy-start.12 = (s32[64]{0:T(128)S(1)}, s32[64]{0:T(128)}, u32[]{:S(2)}) copy-start(s32[64]{0:T(128)} %cutoffs_ref.1) | copy-start | bytes 772
  27.5 1.4 %copy-start.13 = (f32[65]{0:T(128)S(1)}, f32[65]{0:T(128)}, u32[]{:S(2)}) copy-start(f32[65]{0:T(128)} %constant.9.clone.cos_face_ref) | copy-start | bytes 784

commit v3 on v2

--- a/solution.py
+++ b/solution.py
@@ -150,10 +150,9 @@
     even = position % 2 == 0
     two = jnp.where(even, rows - 2, 0)
     one = jnp.where(even, rows - 1, 0)
-    edge_ref[0, :, :nlon] = h_ref[two]
-    edge_ref[1, :, :nlon] = h_ref[two + 1]
-    edge_ref[2, :, :nlon] = v_ref[one]
-    edge_ref[3, :, :LANES] = total
+    edge_ref[0] = h_ref[two]
+    edge_ref[1] = h_ref[two + 1]
+    edge_ref[2] = v_ref[one]
 
 
 def zonal_kernel(h_ref, u_ref, s_ref, out_ref):
@@ -227,7 +226,6 @@
     cos_face_ref,
     flags_ref,
     cutoffs_ref,
-    sums_ref,
     h_ref,
     v_ref,
     part_ref,
@@ -235,7 +233,7 @@
     b_ref,
     *rest,
 ):
-    tables, (out_ref, u_ref) = rest[:8], rest[8:]
+    tables, (out_ref, kept_ref, u_ref) = rest[:8], rest[8:]
     rows, levels, nlon = h_ref.shape
     full = round_up(nlon, LANES)
     half = nlon // 2
@@ -244,9 +242,6 @@
     position = lax.axis_index("lat")
     first = position * rows
     odd = position % 2 == 1
-    area = nlon * float(np.sum(np.sin(np.pi * (np.arange(cos_row_ref.shape[0]) + 0.5) / cos_row_ref.shape[0])))
-    mean = sums_ref[:, :1] * (1.0 / area)
-
     b_rows = [unpack_row(b_ref, i, levels, nlon) for i in range(3)]
     below = [jnp.where(odd, a_ref[i], b_rows[i]) for i in range(3)]
     above = [jnp.where(odd, b_rows[i], a_ref[i]) for i in range(3)]
@@ -267,7 +262,7 @@
     @pl.when(marked == 0)
     def _():
         for j in range(rows):
-            out_ref[j] = updated(j) - mean
+            out_ref[j] = updated(j)
 
     @pl.when(marked > 0)
     def _():
@@ -299,9 +294,23 @@
         r2 = jnp.concatenate([removed[0] - removed[1], zeros], axis=1)
         y = x - r1 - pltpu.roll(r2, half, 1)
         for j in range(rows):
-            cut = cutoffs_ref[first + j].astype(jnp.float32)
-            kept = jnp.where(flags_ref[first + j] > 0, jnp.minimum(1.0, cut * cut), 1.0)
-            out_ref[j] = y[j * levels : (j + 1) * levels, :nlon] - mean * kept
+            out_ref[j] = y[j * levels : (j + 1) * levels, :nlon]
+
+    for j in range(rows):
+        cut = jnp.full((8, LANES), cutoffs_ref[first + j].astype(jnp.float32))
+        kept_ref[j] = jnp.where(flags_ref[first + j] > 0, jnp.minimum(1.0, cut * cut), 1.0)
+
+
+def mean_kernel(area, sums_ref, kept_ref, part_ref, out_ref, row_ref, sem):
+    rows = part_ref.shape[0]
+    mean = sums_ref[:, :1] * (1.0 / area)
+    copies = []
+    for j in range(rows):
+        row_ref[j] = part_ref[j] - mean * kept_ref[j, :1, :1]
+        copies.append(pltpu.make_async_copy(row_ref.at[j], out_ref.at[j], sem.at[j]))
+        copies[-1].start()
+    for c in copies:
+        c.wait()
 
 
 def base_of(nlon):
@@ -318,11 +327,11 @@
     return both[:count] + both[count:] + jnp.dot(y_high, low, preferred_element_type=jnp.float32)
 
 
-def call(kernel, ins, outs, megabytes, scratch=()):
+def call(kernel, ins, outs, megabytes, scratch=(), out_space=pltpu.VMEM):
     return pl.pallas_call(
         kernel,
         in_specs=[pl.BlockSpec(memory_space=space) for _, space in ins],
-        out_specs=[pl.BlockSpec(memory_space=pltpu.VMEM) for _ in outs],
+        out_specs=[pl.BlockSpec(memory_space=out_space) for _ in outs],
         out_shape=[jax.ShapeDtypeStruct(shape, dtype) for shape, dtype in outs],
         scratch_shapes=list(scratch),
         compiler_params=pltpu.CompilerParams(vmem_limit_bytes=megabytes << 20),
@@ -349,7 +358,10 @@
     whole, _, extra = dense_tiles(levels, nlon)
     (edge_b,) = call(
         pack_kernel,
-        [(height, hbm), (merid_courant, hbm)],
+        [
+            (pltpu.with_memory_space_constraint(height, hbm), hbm),
+            (pltpu.with_memory_space_constraint(merid_courant, hbm), hbm),
+        ],
         [((3, 8 * (whole + extra), LANES), f32)],
         4,
         [pltpu.VMEM((3, levels, nlon), f32), pltpu.SemaphoreType.DMA((2,))],
@@ -363,7 +375,7 @@
     edge_a, sums, source = call(
         source_kernel,
         [(cos_row, smem), (rates[None], vmem), (thresholds[None], vmem), (height, vmem), (merid_courant, vmem)],
-        [((4, levels, nlon), f32), ((levels, LANES), f32), (height.shape, f32)],
+        [((3, levels, nlon), f32), ((levels, LANES), f32), (height.shape, f32)],
         8,
     )
     a = permute(edge_a, within)
@@ -381,19 +393,27 @@
 
     bits = [1 << i for i in range((count - 1).bit_length())]
     if count == 1 << len(bits):
-        sums = sums + a[3, :, :LANES]
-        for d in bits[2:] + bits[1:2]:
+        for d in bits[:1] + bits[2:] + bits[1:2]:
             sums = sums + permute(sums, [(i, i ^ d) for i in range(count)])
     else:
         sums = lax.psum(sums, "lat")
 
-    (out,) = call(
+    part, kept = call(
         finish_kernel,
         [(cos_row, smem), (cos_face, smem), (flags, smem), (cutoffs, smem)]
-        + [(x, vmem) for x in (sums, height, merid_courant, part, a, b, *tables)],
-        [(height.shape, f32)],
+        + [(x, vmem) for x in (height, merid_courant, part, a, b, *tables)],
+        [(height.shape, f32), ((rows, 8, LANES), f32)],
         24,
         [pltpu.VMEM((rows * levels, full), f32)],
+    )
+    area = nlon * float(np.sum(np.sin(np.pi * (np.arange(nlat) + 0.5) / nlat)))
+    (out,) = call(
+        functools.partial(mean_kernel, area),
+        [(sums, vmem), (kept, vmem), (part, vmem)],
+        [(height.shape, f32)],
+        4,
+        [pltpu.VMEM(height.shape, f32), pltpu.SemaphoreType.DMA((rows,))],
+        hbm,
     )
     return out
 

time: 33.9 us -> 28.7 us (0.85)
  local copies, waits for them, and re-layouts: 4.28 us -> 0.06 us
  waiting for transfers between devices: 10.3 us -> 7.8 us
  Pallas kernels: 10 us -> 10.9 us
  starting transfers between devices: 8.84 us -> 9.53 us
    unnamed x28 -> x22, local copies, waits for them, and re-layouts: 4.28 us -> 0.06 us
    ppermute x5 -> x6, waiting for transfers between devices: 10.3 us -> 7.8 us  [permute(): return lax.ppermute(x, 'lat', pairs)]
    pallas_call x6 -> x7, Pallas kernels: 10 us -> 10.9 us  [call(): pl.pallas_call(kernel, in_specs=[pl.BlockSpec(memory_space=space) for _,...]
    ppermute x5 -> x6, starting transfers between devices: 8.84 us -> 9.53 us  [permute(): return lax.ppermute(x, 'lat', pairs)]
  transfers between devices with their start and end apart: 5 -> 6, of which waited for: 3 -> 3; matrix products, arithmetic and copies ran while one was open for 0% -> 0% of each run, Pallas kernels for 13% -> 17%
where the time goes in v3:
time: 28.7 us; the launch traced here: 28.5 us
  Pallas kernels  10.9 us (38%)
  starting transfers between devices  9.53 us (33%)
  waiting for transfers between devices  7.8 us (27%)
    pallas_call x7, Pallas kernels, call(): pl.pallas_call(kernel, in_specs=[pl.BlockSpec(memory_space=space) for _,...  10.9 us
    ppermute x6, starting transfers between devices, permute(): return lax.ppermute(x, 'lat', pairs)  9.53 us
    ppermute x6, waiting for transfers between devices, permute(): return lax.ppermute(x, 'lat', pairs)  7.8 us
  transfers between devices with their start and end apart: 6, of which 3 were waited for; matrix products, arithmetic and copies ran while one was open for 0% of the time, Pallas kernels for 17%

profile of v3, /device:TPU:0, one launch (start us, length us, event | category | flops | bytes accessed | tf_op | source)
XLA Modules:
  0.0 28.5 jit_solution(13921214044282339038)
XLA Ops:
  0.0 0.0 copy-start.5
  0.0 0.0 copy-start
  0.0 0.0 copy-start.1
  0.0 0.0 copy-start.7
  0.0 0.0 copy-start.6
  0.0 1.3 %shard_map.111 = f32[3,360,128]{2,1,0:T(8,128)S(1)} custom-call(f32[4,32,1440]{2,1,0:T(8,128)} %h_ref.7, f32[4,32,1440]{2,1,0:T(8,128)} %v_ref.5), custom_call_target="tpu_custom_call" | custom-call | tf_op jit(solution)/shard_map/pallas_call | solution.py:331
  1.3 0.0 copy-start.4
  1.3 0.8 %collective-permute-start.5 = (f32[3,360,128]{2,1,0:T(8,128)S(1)}, f32[3,360,128]{2,1,0:T(8,128)S(1)}, u32[]{:S(2)}, u32[]{:S(2)}) collective-permute-start(f32[3,360,128]{2,1,0:T(8,128)S(1)} %shard_map.111), channel_id=1, source_target_pairs={{1,2},{3,4},{5,6},{7,8},{9,10},{11,12},{13,14},{2,1},{4,3},{6,5},{... | collective-permute-start | bytes 1658888 | tf_op jit(solution)/shard_map/ppermute | solution.py:342
  2.2 0.0 copy-done.5
  2.2 0.0 copy-done
  2.2 0.0 copy-done.1
  2.2 0.0 copy-done.7
  2.2 0.0 copy-done.6
  2.2 0.0 copy-start.3
  2.2 0.0 copy-start.2
  2.3 1.0 %shard_map.109 = (f32[3,32,1440]{2,1,0:T(8,128)S(1)}, f32[32,128]{1,0:T(8,128)S(1)}, f32[4,32,1440]{2,1,0:T(8,128)S(1)}) custom-call(f32[64]{0:T(128)S(1)} %copy-done.5, f32[1,32]{1,0:T(1,128)S(1)} %bitcast.2, f32[1,32]{1,0:T(1,128)S(1)} %bitcast.3, f32[4,32,1440]{2,1,0:T(8,128)S(1)} %copy-done, f32[4,32,1440]{2,1,0:T(8,128)S(1)} %copy-done.1), custom_call_target="tpu_custom_call" | custom-call | tf_op jit(solution)/shard_map/pallas_call | solution.py:331
  3.3 4.4 %collective-permute-start.4 = (f32[3,32,1440]{2,1,0:T(8,128)S(1)}, f32[3,32,1440]{2,1,0:T(8,128)S(1)}, u32[]{:S(2)}, u32[]{:S(2)}) collective-permute-start(f32[3,32,1440]{2,1,0:T(8,128)S(1)} %get-tuple-element.20), channel_id=1, source_target_pairs={{0,1},{2,3},{4,5},{6,7},{8,9},{10,11},{12,13},{14,15},{1,0},{3,2},... | collective-permute-start | bytes 1658888 | tf_op jit(solution)/shard_map/ppermute | solution.py:342
  7.6 0.1 collective-permute-start
  7.7 1.6 %collective-permute-done = f32[32,128]{1,0:T(8,128)S(1)} collective-permute-done((f32[32,128]{1,0:T(8,128)S(1)}, f32[32,128]{1,0:T(8,128)S(1)}, u32[]{:S(2)}, u32[]{:S(2)}) %collective-permute-start) | collective-permute-done | bytes 16416 | tf_op jit(solution)/shard_map/ppermute | solution.py:342
  9.3 1.6 %collective-permute-start.1 = (f32[32,128]{1,0:T(8,128)S(1)}, f32[32,128]{1,0:T(8,128)S(1)}, u32[]{:S(2)}, u32[]{:S(2)}) collective-permute-start(f32[32,128]{1,0:T(8,128)S(1)} %add.12), channel_id=1, source_target_pairs={{0,4},{1,5},{2,6},{3,7},{4,0},{5,1},{6,2},{7,3},{8,12},{9,13},{10,... | collective-permute-start | bytes 49160 | tf_op jit(solution)/shard_map/ppermute | solution.py:342
  10.9 4.3 %collective-permute-done.1 = f32[32,128]{1,0:T(8,128)S(1)} collective-permute-done((f32[32,128]{1,0:T(8,128)S(1)}, f32[32,128]{1,0:T(8,128)S(1)}, u32[]{:S(2)}, u32[]{:S(2)}) %collective-permute-start.1) | collective-permute-done | bytes 16416 | tf_op jit(solution)/shard_map/ppermute | solution.py:342
  15.1 2.7 %collective-permute-start.2 = (f32[32,128]{1,0:T(8,128)S(1)}, f32[32,128]{1,0:T(8,128)S(1)}, u32[]{:S(2)}, u32[]{:S(2)}) collective-permute-start(f32[32,128]{1,0:T(8,128)S(1)} %add.13), channel_id=1, source_target_pairs={{0,8},{1,9},{2,10},{3,11},{4,12},{5,13},{6,14},{7,15},{8,0},{9,1},... | collective-permute-start | bytes 49160 | tf_op jit(solution)/shard_map/ppermute | solution.py:342
  17.8 1.9 %collective-permute-done.2 = f32[32,128]{1,0:T(8,128)S(1)} collective-permute-done((f32[32,128]{1,0:T(8,128)S(1)}, f32[32,128]{1,0:T(8,128)S(1)}, u32[]{:S(2)}, u32[]{:S(2)}) %collective-permute-start.2) | collective-permute-done | bytes 16416 | tf_op jit(solution)/shard_map/ppermute | solution.py:342
  19.8 0.0 collective-permute-start.3
  19.8 0.0 copy-done.4
  19.8 1.2 %shard_map.112 = (bf16[768,768]{1,0:T(8,128)(2,1)S(1)}, bf16[768,768]{1,0:T(8,128)(2,1)S(1)}, bf16[768,768]{1,0:T(8,128)(2,1)S(1)}, bf16[768,768]{1,0:T(8,128)(2,1)S(1)}) custom-call(f32[216,768]{1,0:T(8,128)S(1)} %copy-done.4), custom_call_target="tpu_custom_call" | custom-call | tf_op jit(solution)/shard_map/pallas_call | solution.py:331
  21.0 0.0 copy-done.3
  21.0 1.2 %shard_map.113 = (bf16[768,768]{1,0:T(8,128)(2,1)S(1)}, bf16[768,768]{1,0:T(8,128)(2,1)S(1)}, bf16[768,768]{1,0:T(8,128)(2,1)S(1)}, bf16[768,768]{1,0:T(8,128)(2,1)S(1)}) custom-call(f32[216,768]{1,0:T(8,128)S(1)} %copy-done.3), custom_call_target="tpu_custom_call" | custom-call | tf_op jit(solution)/shard_map/pallas_call | solution.py:331
  22.2 0.0 copy-done.2
  22.2 0.0 copy-start.8
  22.2 0.0 copy-start.9
  22.2 0.0 copy-start.10
  22.2 1.3 %shard_map.110.part_ref = f32[4,32,1440]{2,1,0:T(8,128)S(1)} custom-call(f32[4,32,1440]{2,1,0:T(8,128)S(1)} %copy-done, f32[4,32,1440]{2,1,0:T(8,128)S(1)} %copy-done.2, f32[4,32,1440]{2,1,0:T(8,128)S(1)} %get-tuple-element.19.s_ref), custom_call_target="tpu_custom_call" | custom-call | tf_op jit(solution)/shard_map/pallas_call | solution.py:331
  23.6 0.0 collective-permute-done.3
  23.6 0.0 collective-permute-done.5.b_ref
  23.6 0.0 collective-permute-done.4.a_ref
  23.6 0.0 copy-done.8
  23.6 0.0 copy-done.9
  23.6 0.0 copy-done.10
  23.7 3.9 %shard_map.114 = (f32[4,32,1440]{2,1,0:T(8,128)S(1)}, f32[4,8,128]{2,1,0:T(8,128)S(1)}) custom-call(f32[64]{0:T(128)S(1)} %copy-done.5, f32[65]{0:T(128)S(1)} %copy-done.10, s32[64]{0:T(128)S(1)} %copy-done.8, s32[64]{0:T(128)S(1)} %copy-done.9, f32[4,32,1440]{2,1,0:T(8,128)S(1)} %copy-done, f32[4,32,1440]{2,1,0:T(8,128)S(1)} %copy-done.1, ...), custom_call_target="tpu_custom_call" | custom-call | tf_op jit(solution)/shard_map/pallas_call | solution.py:331
  27.6 1.0 %shard_map.115 = f32[4,32,1440]{2,1,0:T(8,128)} custom-call(f32[32,128]{1,0:T(8,128)S(1)} %add.15.sums_ref, f32[4,8,128]{2,1,0:T(8,128)S(1)} %get-tuple-element.29.kept_ref, f32[4,32,1440]{2,1,0:T(8,128)S(1)} %get-tuple-element.30.part_ref), custom_call_target="tpu_custom_call" | custom-call | tf_op jit(solution)/shard_map/pallas_call | solution.py:331
  (4 shorter events, 0.0 us)
Async XLA Ops:
  0.0 2.2 %copy-start.5 = (f32[64]{0:T(128)S(1)}, f32[64]{0:T(128)}, u32[]{:S(2)}) copy-start(f32[64]{0:T(128)} %constant.8.clone.cos_ref.cos_row_ref) | copy-start | bytes 772
  0.0 2.2 %copy-start = (f32[4,32,1440]{2,1,0:T(8,128)S(1)}, f32[4,32,1440]{2,1,0:T(8,128)}, u32[]{:S(2)}) copy-start(f32[4,32,1440]{2,1,0:T(8,128)} %h_ref.7) | copy-start | bytes 2211844
  0.0 2.2 %copy-start.1 = (f32[4,32,1440]{2,1,0:T(8,128)S(1)}, f32[4,32,1440]{2,1,0:T(8,128)}, u32[]{:S(2)}) copy-start(f32[4,32,1440]{2,1,0:T(8,128)} %v_ref.5) | copy-start | bytes 2211844
  0.0 2.2 %copy-start.7 = (f32[32]{0:T(128)S(1)}, f32[32]{0:T(128)}, u32[]{:S(2)}) copy-start(f32[32]{0:T(128)} %param.15) | copy-start | bytes 388
  0.0 2.2 %copy-start.6 = (f32[32]{0:T(128)S(1)}, f32[32]{0:T(128)}, u32[]{:S(2)}) copy-start(f32[32]{0:T(128)} %param.14) | copy-start | bytes 388
  1.3 18.5 %copy-start.4 = (f32[216,768]{1,0:T(8,128)S(1)}, f32[216,768]{1,0:T(8,128)}, u32[]{:S(2)}) copy-start(f32[216,768]{1,0:T(8,128)} %constant.10.clone.source_ref) | copy-start | bytes 1990660
  1.3 22.3 %collective-permute-start.5 = (f32[3,360,128]{2,1,0:T(8,128)S(1)}, f32[3,360,128]{2,1,0:T(8,128)S(1)}, u32[]{:S(2)}, u32[]{:S(2)}) collective-permute-start(f32[3,360,128]{2,1,0:T(8,128)S(1)} %shard_map.111), channel_id=1, source_target_pairs={{1,2},{3,4},{5,6},{7,8},{9,10},{11,12},{13,14},{2,1},{4,3},{6,5},{... | collective-permute-start | bytes 1658888 | tf_op jit(solution)/shard_map/ppermute | solution.py:342
  2.2 18.8 %copy-start.3 = (f32[216,768]{1,0:T(8,128)S(1)}, f32[216,768]{1,0:T(8,128)}, u32[]{:S(2)}) copy-start(f32[216,768]{1,0:T(8,128)} %constant.11.clone.source_ref) | copy-start | bytes 1990660
  2.2 19.9 %copy-start.2 = (f32[4,32,1440]{2,1,0:T(8,128)S(1)}, f32[4,32,1440]{2,1,0:T(8,128)}, u32[]{:S(2)}) copy-start(f32[4,32,1440]{2,1,0:T(8,128)} %u_ref.1) | copy-start | bytes 2211844
  3.3 20.3 %collective-permute-start.4 = (f32[3,32,1440]{2,1,0:T(8,128)S(1)}, f32[3,32,1440]{2,1,0:T(8,128)S(1)}, u32[]{:S(2)}, u32[]{:S(2)}) collective-permute-start(f32[3,32,1440]{2,1,0:T(8,128)S(1)} %get-tuple-element.20), channel_id=1, source_target_pairs={{0,1},{2,3},{4,5},{6,7},{8,9},{10,11},{12,13},{14,15},{1,0},{3,2},... | collective-permute-start | bytes 1658888 | tf_op jit(solution)/shard_map/ppermute | solution.py:342
  7.6 1.7 %collective-permute-start = (f32[32,128]{1,0:T(8,128)S(1)}, f32[32,128]{1,0:T(8,128)S(1)}, u32[]{:S(2)}, u32[]{:S(2)}) collective-permute-start(f32[32,128]{1,0:T(8,128)S(1)} %get-tuple-element.18), channel_id=1, source_target_pairs={{0,1},{1,0},{2,3},{3,2},{4,5},{5,4},{6,7},{7,6},{8,9},{9,8},{10,11... | collective-permute-start | bytes 49160 | tf_op jit(solution)/shard_map/ppermute | solution.py:342
  9.3 5.8 %collective-permute-start.1 = (f32[32,128]{1,0:T(8,128)S(1)}, f32[32,128]{1,0:T(8,128)S(1)}, u32[]{:S(2)}, u32[]{:S(2)}) collective-permute-start(f32[32,128]{1,0:T(8,128)S(1)} %add.12), channel_id=1, source_target_pairs={{0,4},{1,5},{2,6},{3,7},{4,0},{5,1},{6,2},{7,3},{8,12},{9,13},{10,... | collective-permute-start | bytes 49160 | tf_op jit(solution)/shard_map/ppermute | solution.py:342
  15.1 4.6 %collective-permute-start.2 = (f32[32,128]{1,0:T(8,128)S(1)}, f32[32,128]{1,0:T(8,128)S(1)}, u32[]{:S(2)}, u32[]{:S(2)}) collective-permute-start(f32[32,128]{1,0:T(8,128)S(1)} %add.13), channel_id=1, source_target_pairs={{0,8},{1,9},{2,10},{3,11},{4,12},{5,13},{6,14},{7,15},{8,0},{9,1},... | collective-permute-start | bytes 49160 | tf_op jit(solution)/shard_map/ppermute | solution.py:342
  19.8 3.8 %collective-permute-start.3 = (f32[32,128]{1,0:T(8,128)S(1)}, f32[32,128]{1,0:T(8,128)S(1)}, u32[]{:S(2)}, u32[]{:S(2)}) collective-permute-start(f32[32,128]{1,0:T(8,128)S(1)} %add.14), channel_id=1, source_target_pairs={{0,2},{1,3},{2,0},{3,1},{4,6},{5,7},{6,4},{7,5},{8,10},{9,11},{10,... | collective-permute-start | bytes 49160 | tf_op jit(solution)/shard_map/ppermute | solution.py:342
  22.2 1.4 %copy-start.8 = (s32[64]{0:T(128)S(1)}, s32[64]{0:T(128)}, u32[]{:S(2)}) copy-start(s32[64]{0:T(128)} %flags_ref.1) | copy-start | bytes 772
  22.2 1.4 %copy-start.9 = (s32[64]{0:T(128)S(1)}, s32[64]{0:T(128)}, u32[]{:S(2)}) copy-start(s32[64]{0:T(128)} %cutoffs_ref.1) | copy-start | bytes 772
  22.2 1.4 %copy-start.10 = (f32[65]{0:T(128)S(1)}, f32[65]{0:T(128)}, u32[]{:S(2)}) copy-start(f32[65]{0:T(128)} %constant.9.clone.cos_face_ref) | copy-start | bytes 784

commit v4 on v3

--- a/solution.py
+++ b/solution.py
@@ -243,8 +243,9 @@
     first = position * rows
     odd = position % 2 == 1
     b_rows = [unpack_row(b_ref, i, levels, nlon) for i in range(3)]
-    below = [jnp.where(odd, a_ref[i], b_rows[i]) for i in range(3)]
-    above = [jnp.where(odd, b_rows[i], a_ref[i]) for i in range(3)]
+    last = lax.axis_size("lat") - 1
+    below = [jnp.where(odd, a_ref[i], jnp.where(position == 0, 0.0, b_rows[i])) for i in range(3)]
+    above = [jnp.where(odd, jnp.where(position == last, 0.0, b_rows[i]), a_ref[i]) for i in range(3)]
     height = [below[0], below[1]] + [h_ref[j] for j in range(rows)] + [above[0], above[1]]
     speed = [below[2]] + [v_ref[j] for j in range(rows)] + [above[2]]
     flux = []
@@ -338,8 +339,8 @@
     )(*[x for x, _ in ins])
 
 
-def permute(x, pairs):
-    return lax.ppermute(x, "lat", pairs)
+def permute(x, pairs, axes="lat"):
+    return lax.ppermute(x, axes, pairs)
 
 
 def step(height, zonal_courant, merid_courant, rates, thresholds, flags, cutoffs):
@@ -354,6 +355,11 @@
     between = [(i, i + 1) for i in range(1, count - 1, 2)]
     within = [(i, i + 1) for i in range(0, count - 1, 2)]
     between = between + [(j, i) for i, j in between]
+    parts = lax.axis_size("member")
+    between = [(p * count + i, p * count + j) for p in range(parts) for i, j in between]
+    ends = [0, count - 1] if count % 2 == 0 else [0]
+    if parts % 2 == 0:
+        between += [(p * count + e, (p ^ 1) * count + e) for p in range(parts) for e in ends]
     within = within + [(j, i) for i, j in within]
     whole, _, extra = dense_tiles(levels, nlon)
     (edge_b,) = call(
@@ -366,7 +372,7 @@
         4,
         [pltpu.VMEM((3, levels, nlon), f32), pltpu.SemaphoreType.DMA((2,))],
     )
-    b = permute(edge_b, between)
+    b = permute(edge_b, between, ("member", "lat"))
 
     cos_row = jnp.asarray(np.sin(np.pi * (np.arange(nlat) + 0.5) / nlat).astype(np.float32))
     faces = np.sin(np.pi * np.arange(nlat + 1) / nlat)

time: 28.7 us -> 26.8 us (0.934)
  starting transfers between devices: 9.53 us -> 7.67 us
    ppermute x6, starting transfers between devices: 9.53 us -> 7.67 us  [permute(): return lax.ppermute(x, axes, pairs)]
  transfers between devices with their start and end apart: 6 -> 6, of which waited for: 3 -> 3; matrix products, arithmetic and copies ran while one was open for 0% -> 0% of each run, Pallas kernels for 17% -> 18%
where the time goes in v4:
time: 26.8 us; the launch traced here: 26.6 us
  Pallas kernels  10.9 us (41%)
  waiting for transfers between devices  7.74 us (29%)
  starting transfers between devices  7.67 us (29%)
    pallas_call x7, Pallas kernels, call(): pl.pallas_call(kernel, in_specs=[pl.BlockSpec(memory_space=space) for _,...  10.9 us
    ppermute x6, waiting for transfers between devices, permute(): return lax.ppermute(x, axes, pairs)  7.74 us
    ppermute x6, starting transfers between devices, permute(): return lax.ppermute(x, axes, pairs)  7.67 us
  transfers between devices with their start and end apart: 6, of which 3 were waited for; matrix products, arithmetic and copies ran while one was open for 0% of the time, Pallas kernels for 18%

profile of v4, /device:TPU:0, one launch (start us, length us, event | category | flops | bytes accessed | tf_op | source)
XLA Modules:
  0.0 26.6 jit_solution(6697761300866298368)
XLA Ops:
  0.0 0.0 copy-start.5
  0.0 0.0 copy-start
  0.0 0.0 copy-start.1
  0.0 0.0 copy-start.7
  0.0 0.0 copy-start.6
  0.0 1.3 %shard_map.111 = f32[3,360,128]{2,1,0:T(8,128)S(1)} custom-call(f32[4,32,1440]{2,1,0:T(8,128)} %h_ref.7, f32[4,32,1440]{2,1,0:T(8,128)} %v_ref.5), custom_call_target="tpu_custom_call" | custom-call | tf_op jit(solution)/shard_map/pallas_call | solution.py:332
  1.3 0.0 copy-start.4
  1.3 3.0 %collective-permute-start.5 = (f32[3,360,128]{2,1,0:T(8,128)S(1)}, f32[3,360,128]{2,1,0:T(8,128)S(1)}, u32[]{:S(2)}, u32[]{:S(2)}) collective-permute-start(f32[3,360,128]{2,1,0:T(8,128)S(1)} %shard_map.111), channel_id=1, source_target_pairs={{1,2},{3,4},{5,6},{7,8},{9,10},{11,12},{13,14},{2,1},{4,3},{6,5},{... | collective-permute-start | bytes 1658888 | tf_op jit(solution)/shard_map/ppermute | solution.py:343
  4.4 0.0 copy-done.5
  4.4 0.0 copy-done
  4.4 0.0 copy-done.1
  4.4 0.0 copy-done.7
  4.4 0.0 copy-done.6
  4.4 0.0 copy-start.3
  4.4 0.0 copy-start.2
  4.4 1.0 %shard_map.109 = (f32[3,32,1440]{2,1,0:T(8,128)S(1)}, f32[32,128]{1,0:T(8,128)S(1)}, f32[4,32,1440]{2,1,0:T(8,128)S(1)}) custom-call(f32[64]{0:T(128)S(1)} %copy-done.5, f32[1,32]{1,0:T(1,128)S(1)} %bitcast.2, f32[1,32]{1,0:T(1,128)S(1)} %bitcast.3, f32[4,32,1440]{2,1,0:T(8,128)S(1)} %copy-done, f32[4,32,1440]{2,1,0:T(8,128)S(1)} %copy-done.1), custom_call_target="tpu_custom_call" | custom-call | tf_op jit(solution)/shard_map/pallas_call | solution.py:332
  5.5 0.2 collective-permute-start.4
  5.6 0.4 %collective-permute-start = (f32[32,128]{1,0:T(8,128)S(1)}, f32[32,128]{1,0:T(8,128)S(1)}, u32[]{:S(2)}, u32[]{:S(2)}) collective-permute-start(f32[32,128]{1,0:T(8,128)S(1)} %get-tuple-element.18), channel_id=1, source_target_pairs={{0,1},{1,0},{2,3},{3,2},{4,5},{5,4},{6,7},{7,6},{8,9},{9,8},{10,11... | collective-permute-start | bytes 49160 | tf_op jit(solution)/shard_map/ppermute | solution.py:343
  6.0 1.5 %collective-permute-done = f32[32,128]{1,0:T(8,128)S(1)} collective-permute-done((f32[32,128]{1,0:T(8,128)S(1)}, f32[32,128]{1,0:T(8,128)S(1)}, u32[]{:S(2)}, u32[]{:S(2)}) %collective-permute-start) | collective-permute-done | bytes 16416 | tf_op jit(solution)/shard_map/ppermute | solution.py:343
  7.5 1.3 %collective-permute-start.1 = (f32[32,128]{1,0:T(8,128)S(1)}, f32[32,128]{1,0:T(8,128)S(1)}, u32[]{:S(2)}, u32[]{:S(2)}) collective-permute-start(f32[32,128]{1,0:T(8,128)S(1)} %add.12), channel_id=1, source_target_pairs={{0,4},{1,5},{2,6},{3,7},{4,0},{5,1},{6,2},{7,3},{8,12},{9,13},{10,... | collective-permute-start | bytes 49160 | tf_op jit(solution)/shard_map/ppermute | solution.py:343
  8.9 4.3 %collective-permute-done.1 = f32[32,128]{1,0:T(8,128)S(1)} collective-permute-done((f32[32,128]{1,0:T(8,128)S(1)}, f32[32,128]{1,0:T(8,128)S(1)}, u32[]{:S(2)}, u32[]{:S(2)}) %collective-permute-start.1) | collective-permute-done | bytes 16416 | tf_op jit(solution)/shard_map/ppermute | solution.py:343
  13.2 2.7 %collective-permute-start.2 = (f32[32,128]{1,0:T(8,128)S(1)}, f32[32,128]{1,0:T(8,128)S(1)}, u32[]{:S(2)}, u32[]{:S(2)}) collective-permute-start(f32[32,128]{1,0:T(8,128)S(1)} %add.13), channel_id=1, source_target_pairs={{0,8},{1,9},{2,10},{3,11},{4,12},{5,13},{6,14},{7,15},{8,0},{9,1},... | collective-permute-start | bytes 49160 | tf_op jit(solution)/shard_map/ppermute | solution.py:343
  15.9 1.9 %collective-permute-done.2 = f32[32,128]{1,0:T(8,128)S(1)} collective-permute-done((f32[32,128]{1,0:T(8,128)S(1)}, f32[32,128]{1,0:T(8,128)S(1)}, u32[]{:S(2)}, u32[]{:S(2)}) %collective-permute-start.2) | collective-permute-done | bytes 16416 | tf_op jit(solution)/shard_map/ppermute | solution.py:343
  17.8 0.0 collective-permute-start.3
  17.8 0.0 copy-done.4
  17.8 1.2 %shard_map.112 = (bf16[768,768]{1,0:T(8,128)(2,1)S(1)}, bf16[768,768]{1,0:T(8,128)(2,1)S(1)}, bf16[768,768]{1,0:T(8,128)(2,1)S(1)}, bf16[768,768]{1,0:T(8,128)(2,1)S(1)}) custom-call(f32[216,768]{1,0:T(8,128)S(1)} %copy-done.4), custom_call_target="tpu_custom_call" | custom-call | tf_op jit(solution)/shard_map/pallas_call | solution.py:332
  19.0 0.0 copy-done.3
  19.0 1.2 %shard_map.113 = (bf16[768,768]{1,0:T(8,128)(2,1)S(1)}, bf16[768,768]{1,0:T(8,128)(2,1)S(1)}, bf16[768,768]{1,0:T(8,128)(2,1)S(1)}, bf16[768,768]{1,0:T(8,128)(2,1)S(1)}) custom-call(f32[216,768]{1,0:T(8,128)S(1)} %copy-done.3), custom_call_target="tpu_custom_call" | custom-call | tf_op jit(solution)/shard_map/pallas_call | solution.py:332
  20.2 0.0 copy-done.2
  20.2 0.0 copy-start.8
  20.2 0.0 copy-start.9
  20.3 0.0 copy-start.10
  20.3 1.3 %shard_map.110.part_ref = f32[4,32,1440]{2,1,0:T(8,128)S(1)} custom-call(f32[4,32,1440]{2,1,0:T(8,128)S(1)} %copy-done, f32[4,32,1440]{2,1,0:T(8,128)S(1)} %copy-done.2, f32[4,32,1440]{2,1,0:T(8,128)S(1)} %get-tuple-element.19.s_ref), custom_call_target="tpu_custom_call" | custom-call | tf_op jit(solution)/shard_map/pallas_call | solution.py:332
  21.6 0.0 collective-permute-done.3
  21.6 0.0 collective-permute-done.5.b_ref
  21.7 0.0 collective-permute-done.4.a_ref
  21.7 0.0 copy-done.8
  21.7 0.0 copy-done.9
  21.7 0.0 copy-done.10
  21.7 3.9 %shard_map.114 = (f32[4,32,1440]{2,1,0:T(8,128)S(1)}, f32[4,8,128]{2,1,0:T(8,128)S(1)}) custom-call(f32[64]{0:T(128)S(1)} %copy-done.5, f32[65]{0:T(128)S(1)} %copy-done.10, s32[64]{0:T(128)S(1)} %copy-done.8, s32[64]{0:T(128)S(1)} %copy-done.9, f32[4,32,1440]{2,1,0:T(8,128)S(1)} %copy-done, f32[4,32,1440]{2,1,0:T(8,128)S(1)} %copy-done.1, ...), custom_call_target="tpu_custom_call" | custom-call | tf_op jit(solution)/shard_map/pallas_call | solution.py:332
  25.6 1.0 %shard_map.115 = f32[4,32,1440]{2,1,0:T(8,128)} custom-call(f32[32,128]{1,0:T(8,128)S(1)} %add.15.sums_ref, f32[4,8,128]{2,1,0:T(8,128)S(1)} %get-tuple-element.29.kept_ref, f32[4,32,1440]{2,1,0:T(8,128)S(1)} %get-tuple-element.30.part_ref), custom_call_target="tpu_custom_call" | custom-call | tf_op jit(solution)/shard_map/pallas_call | solution.py:332
  (4 shorter events, 0.0 us)
Async XLA Ops:
  0.0 4.4 %copy-start.5 = (f32[64]{0:T(128)S(1)}, f32[64]{0:T(128)}, u32[]{:S(2)}) copy-start(f32[64]{0:T(128)} %constant.8.clone.cos_ref.cos_row_ref) | copy-start | bytes 772
  0.0 4.4 %copy-start = (f32[4,32,1440]{2,1,0:T(8,128)S(1)}, f32[4,32,1440]{2,1,0:T(8,128)}, u32[]{:S(2)}) copy-start(f32[4,32,1440]{2,1,0:T(8,128)} %h_ref.7) | copy-start | bytes 2211844
  0.0 4.4 %copy-start.1 = (f32[4,32,1440]{2,1,0:T(8,128)S(1)}, f32[4,32,1440]{2,1,0:T(8,128)}, u32[]{:S(2)}) copy-start(f32[4,32,1440]{2,1,0:T(8,128)} %v_ref.5) | copy-start | bytes 2211844
  0.0 4.4 %copy-start.7 = (f32[32]{0:T(128)S(1)}, f32[32]{0:T(128)}, u32[]{:S(2)}) copy-start(f32[32]{0:T(128)} %param.15) | copy-start | bytes 388
  0.0 4.4 %copy-start.6 = (f32[32]{0:T(128)S(1)}, f32[32]{0:T(128)}, u32[]{:S(2)}) copy-start(f32[32]{0:T(128)} %param.14) | copy-start | bytes 388
  1.3 16.5 %copy-start.4 = (f32[216,768]{1,0:T(8,128)S(1)}, f32[216,768]{1,0:T(8,128)}, u32[]{:S(2)}) copy-start(f32[216,768]{1,0:T(8,128)} %constant.10.clone.source_ref) | copy-start | bytes 1990660
  1.3 20.3 %collective-permute-start.5 = (f32[3,360,128]{2,1,0:T(8,128)S(1)}, f32[3,360,128]{2,1,0:T(8,128)S(1)}, u32[]{:S(2)}, u32[]{:S(2)}) collective-permute-start(f32[3,360,128]{2,1,0:T(8,128)S(1)} %shard_map.111), channel_id=1, source_target_pairs={{1,2},{3,4},{5,6},{7,8},{9,10},{11,12},{13,14},{2,1},{4,3},{6,5},{... | collective-permute-start | bytes 1658888 | tf_op jit(solution)/shard_map/ppermute | solution.py:343
  4.4 14.6 %copy-start.3 = (f32[216,768]{1,0:T(8,128)S(1)}, f32[216,768]{1,0:T(8,128)}, u32[]{:S(2)}) copy-start(f32[216,768]{1,0:T(8,128)} %constant.11.clone.source_ref) | copy-start | bytes 1990660
  4.4 15.8 %copy-start.2 = (f32[4,32,1440]{2,1,0:T(8,128)S(1)}, f32[4,32,1440]{2,1,0:T(8,128)}, u32[]{:S(2)}) copy-start(f32[4,32,1440]{2,1,0:T(8,128)} %u_ref.1) | copy-start | bytes 2211844
  5.5 16.2 %collective-permute-start.4 = (f32[3,32,1440]{2,1,0:T(8,128)S(1)}, f32[3,32,1440]{2,1,0:T(8,128)S(1)}, u32[]{:S(2)}, u32[]{:S(2)}) collective-permute-start(f32[3,32,1440]{2,1,0:T(8,128)S(1)} %get-tuple-element.20), channel_id=1, source_target_pairs={{0,1},{2,3},{4,5},{6,7},{8,9},{10,11},{12,13},{14,15},{1,0},{3,2},... | collective-permute-start | bytes 1658888 | tf_op jit(solution)/shard_map/ppermute | solution.py:343
  5.6 1.9 %collective-permute-start = (f32[32,128]{1,0:T(8,128)S(1)}, f32[32,128]{1,0:T(8,128)S(1)}, u32[]{:S(2)}, u32[]{:S(2)}) collective-permute-start(f32[32,128]{1,0:T(8,128)S(1)} %get-tuple-element.18), channel_id=1, source_target_pairs={{0,1},{1,0},{2,3},{3,2},{4,5},{5,4},{6,7},{7,6},{8,9},{9,8},{10,11... | collective-permute-start | bytes 49160 | tf_op jit(solution)/shard_map/ppermute | solution.py:343
  7.5 5.7 %collective-permute-start.1 = (f32[32,128]{1,0:T(8,128)S(1)}, f32[32,128]{1,0:T(8,128)S(1)}, u32[]{:S(2)}, u32[]{:S(2)}) collective-permute-start(f32[32,128]{1,0:T(8,128)S(1)} %add.12), channel_id=1, source_target_pairs={{0,4},{1,5},{2,6},{3,7},{4,0},{5,1},{6,2},{7,3},{8,12},{9,13},{10,... | collective-permute-start | bytes 49160 | tf_op jit(solution)/shard_map/ppermute | solution.py:343
  13.2 4.6 %collective-permute-start.2 = (f32[32,128]{1,0:T(8,128)S(1)}, f32[32,128]{1,0:T(8,128)S(1)}, u32[]{:S(2)}, u32[]{:S(2)}) collective-permute-start(f32[32,128]{1,0:T(8,128)S(1)} %add.13), channel_id=1, source_target_pairs={{0,8},{1,9},{2,10},{3,11},{4,12},{5,13},{6,14},{7,15},{8,0},{9,1},... | collective-permute-start | bytes 49160 | tf_op jit(solution)/shard_map/ppermute | solution.py:343
  17.8 3.8 %collective-permute-start.3 = (f32[32,128]{1,0:T(8,128)S(1)}, f32[32,128]{1,0:T(8,128)S(1)}, u32[]{:S(2)}, u32[]{:S(2)}) collective-permute-start(f32[32,128]{1,0:T(8,128)S(1)} %add.14), channel_id=1, source_target_pairs={{0,2},{1,3},{2,0},{3,1},{4,6},{5,7},{6,4},{7,5},{8,10},{9,11},{10,... | collective-permute-start | bytes 49160 | tf_op jit(solution)/shard_map/ppermute | solution.py:343
  20.2 1.4 %copy-start.8 = (s32[64]{0:T(128)S(1)}, s32[64]{0:T(128)}, u32[]{:S(2)}) copy-start(s32[64]{0:T(128)} %flags_ref.1) | copy-start | bytes 772
  20.2 1.4 %copy-start.9 = (s32[64]{0:T(128)S(1)}, s32[64]{0:T(128)}, u32[]{:S(2)}) copy-start(s32[64]{0:T(128)} %cutoffs_ref.1) | copy-start | bytes 772
  20.3 1.4 %copy-start.10 = (f32[65]{0:T(128)S(1)}, f32[65]{0:T(128)}, u32[]{:S(2)}) copy-start(f32[65]{0:T(128)} %constant.9.clone.cos_face_ref) | copy-start | bytes 784

commit v5 on v4

--- a/solution.py
+++ b/solution.py
@@ -92,20 +92,17 @@
         out_ref[i, 8 * t : 8 * t + 8, :] = jnp.concatenate([p for p in parts if p.shape[1]], axis=1)
 
 
-def unpack_row(ref, i, levels, nlon):
+def packed_tile(ref, i, g, k, levels, nlon):
     whole, shared, _ = dense_tiles(levels, nlon)
     per = nlon // LANES
     rest = nlon % LANES
-    groups = []
-    for g in range(levels // 8):
-        parts = [ref[i, 8 * t : 8 * t + 8, :] for t in range(g * per, (g + 1) * per)]
-        if rest:
-            t = whole + g // shared
-            last = ref[i, 8 * t : 8 * t + 8, :]
-            at = g % shared * rest
-            parts.append((pltpu.roll(last, LANES - at, 1) if at else last)[:, :rest])
-        groups.append(jnp.concatenate(parts, axis=1))
-    return jnp.concatenate(groups, axis=0)
+    if k < per:
+        t = g * per + k
+        return ref[i, 8 * t : 8 * t + 8, :]
+    t = whole + g // shared
+    last = ref[i, 8 * t : 8 * t + 8, :]
+    at = g % shared * rest
+    return (pltpu.roll(last, LANES - at, 1) if at else last)[:, :rest]
 
 
 def pack_kernel(h_ref, v_ref, out_ref, edge_ref, sem):
@@ -156,19 +153,19 @@
 
 
 def zonal_kernel(h_ref, u_ref, s_ref, out_ref):
-    rows, _, nlon = h_ref.shape
+    rows, levels, nlon = h_ref.shape
     full = round_up(nlon, LANES)
     for j in range(rows):
-        h0 = h_ref[j]
-        h = wrapped(h0, nlon, full)
-        u = wrapped(u_ref[j], nlon, full)
-        east = pltpu.roll(h, full - 1, 1)
-        far_east = pltpu.roll(h, full - 2, 1)
-        west = pltpu.roll(h, 1, 1)
-        face = (7.0 * (h + east) - (west + far_east)) * (0.5 / 12.0)
-        flux = (u + pltpu.roll(u, full - 1, 1)) * face
-        div = flux - pltpu.roll(flux, 1, 1)
-        out_ref[j] = h0 - div[:, :nlon] + s_ref[j]
+        for g in range(0, levels, 16):
+            at = slice(g, g + 16)
+            h0 = h_ref[j, at, :]
+            h = wrapped(h0, nlon, full)
+            u = wrapped(u_ref[j, at, :], nlon, full)
+            face = 7.0 * (h + pltpu.roll(h, full - 1, 1))
+            face = face - (pltpu.roll(h, 1, 1) + pltpu.roll(h, full - 2, 1))
+            flux = (u + pltpu.roll(u, full - 1, 1)) * (face * (0.5 / 12.0))
+            div = flux - pltpu.roll(flux, 1, 1)
+            out_ref[j, at, :] = h0 - div[:, :nlon] + s_ref[j, at, :]
 
 
 def table_kernel(parity, half, source_ref, high_ref, low_ref, high_t_ref, low_t_ref):
@@ -233,73 +230,105 @@
     b_ref,
     *rest,
 ):
-    tables, (out_ref, kept_ref, u_ref) = rest[:8], rest[8:]
+    tables, (out_ref, kept_ref, y_ref, s_ref, d_ref) = rest[:8], rest[8:]
     rows, levels, nlon = h_ref.shape
     full = round_up(nlon, LANES)
     half = nlon // 2
     depth, cols = tables[0].shape
     width = cols // 2
+    units = rows * levels
     position = lax.axis_index("lat")
+    last = lax.axis_size("lat") - 1
     first = position * rows
     odd = position % 2 == 1
-    b_rows = [unpack_row(b_ref, i, levels, nlon) for i in range(3)]
-    last = lax.axis_size("lat") - 1
-    below = [jnp.where(odd, a_ref[i], jnp.where(position == 0, 0.0, b_rows[i])) for i in range(3)]
-    above = [jnp.where(odd, jnp.where(position == last, 0.0, b_rows[i]), a_ref[i]) for i in range(3)]
-    height = [below[0], below[1]] + [h_ref[j] for j in range(rows)] + [above[0], above[1]]
-    speed = [below[2]] + [v_ref[j] for j in range(rows)] + [above[2]]
-    flux = []
-    for f in range(rows + 1):
-        p = 7.0 * (height[f + 1] + height[f + 2]) - (height[f] + height[f + 3])
-        c = cos_face_ref[first + f] * (0.5 / 12.0)
-        flux.append((speed[f] + speed[f + 1]) * c * p)
+    bottom, top = position == 0, position == last
     marked = flags_ref[first]
     for j in range(1, rows):
         marked = jnp.maximum(marked, flags_ref[first + j])
-
-    def updated(j):
-        return part_ref[j] - (flux[j + 1] - flux[j]) * (1.0 / cos_row_ref[first + j])
-
-    @pl.when(marked == 0)
-    def _():
-        for j in range(rows):
-            out_ref[j] = updated(j)
+    inverse_cos = [1.0 / jnp.full((8, LANES), cos_row_ref[first + j]) for j in range(rows)]
+    face_cos = [cos_face_ref[first + f] * (0.5 / 12.0) for f in range(rows + 1)]
+
+    for g in range(levels // 8):
+        at = slice(8 * g, 8 * g + 8)
+        for k in range(full // LANES):
+            lanes = slice(k * LANES, min((k + 1) * LANES, nlon))
+            wide = lanes.stop - lanes.start
+            near = [a_ref[i, at, lanes] for i in range(3)]
+            far = [packed_tile(b_ref, i, g, k, levels, nlon) for i in range(3)]
+            below = [jnp.where(odd, x, jnp.where(bottom, 0.0, y)) for x, y in zip(near, far)]
+            above = [jnp.where(odd, jnp.where(top, 0.0, y), x) for x, y in zip(near, far)]
+            height = [below[0], below[1], *(h_ref[j, at, lanes] for j in range(rows)), above[0], above[1]]
+            speed = [below[2], *(v_ref[j, at, lanes] for j in range(rows)), above[2]]
+            flux = []
+            for f in range(rows + 1):
+                p = 7.0 * (height[f + 1] + height[f + 2]) - (height[f] + height[f + 3])
+                flux.append((speed[f] + speed[f + 1]) * face_cos[f] * p)
+            for j in range(rows):
+                div = (flux[j + 1] - flux[j]) * inverse_cos[j][:, :wide]
+                out_ref[j, at, lanes] = part_ref[j, at, lanes] - div
+
+    for j in range(rows):
+        cut = jnp.full((8, LANES), cutoffs_ref[first + j].astype(jnp.float32))
+        kept_ref[j] = jnp.where(flags_ref[first + j] > 0, jnp.minimum(1.0, cut * cut), 1.0)
 
     @pl.when(marked > 0)
     def _():
-        u_ref[:, base_of(nlon):] = jnp.zeros((rows * levels, full - base_of(nlon)), jnp.float32)
-        for j in range(rows):
-            u_ref[j * levels : (j + 1) * levels, :nlon] = updated(j)
-        x = u_ref[...]
-        near = x[:, :depth]
-        far = pltpu.roll(x, full - half, 1)[:, :depth]
-        removed = []
-        lane = lax.broadcasted_iota(jnp.int32, (1, width), 1)
+        for r in range(0, units, 16):
+            j, q = divmod(r, levels)
+            x = out_ref[j, q : q + 16, :]
+            near = x[:, :depth]
+            x = jnp.concatenate([x, jnp.zeros((16, full - nlon), jnp.float32)], axis=1)
+            far = pltpu.roll(x, full - half, 1)[:, :depth]
+            for parity, y in ((0, near + far), (1, near - far)):
+                high = y.astype(jnp.bfloat16)
+                y_ref[parity, r : r + 16, :] = high
+                y_ref[parity, units + r : units + r + 16, :] = (y - high.astype(jnp.float32)).astype(jnp.bfloat16)
+        lane = lax.broadcasted_iota(jnp.int32, (8, width), 1)
+        chunk = 256 if cols % 256 == 0 and depth % 256 == 0 else LANES
         for parity in (0, 1):
-            y = near + far if parity == 0 else near - far
-            fwd_high, fwd_low, inv_high, inv_low = (t[...] for t in tables[4 * parity : 4 * parity + 4])
-            spectrum = product(y, fwd_high, fwd_low)
+            high_ref, low_ref = tables[4 * parity : 4 * parity + 2]
             waves = 2 * lane + parity
             weight = jnp.where((waves > 0) & (waves < half), 2.0 / nlon, 1.0 / nlon)
             inverse = 1.0 / jnp.maximum(waves, 1).astype(jnp.float32)
-            pieces = []
+            factors = []
             for j in range(rows):
                 ratio = cutoffs_ref[first + j].astype(jnp.float32) * inverse
                 factor = (1.0 - jnp.minimum(1.0, ratio * ratio)) * weight
                 factor = jnp.where(flags_ref[first + j] > 0, factor, 0.0)
-                factor = jnp.concatenate([factor, factor], axis=1)
-                pieces.append(spectrum[j * levels : (j + 1) * levels] * factor)
-            removed.append(product(jnp.concatenate(pieces, axis=0), inv_high, inv_low))
-        zeros = jnp.zeros((rows * levels, full - depth), jnp.float32)
-        r1 = jnp.concatenate([removed[0] + removed[1], zeros], axis=1)
-        r2 = jnp.concatenate([removed[0] - removed[1], zeros], axis=1)
-        y = x - r1 - pltpu.roll(r2, half, 1)
-        for j in range(rows):
-            out_ref[j] = y[j * levels : (j + 1) * levels, :nlon]
-
-    for j in range(rows):
-        cut = jnp.full((8, LANES), cutoffs_ref[first + j].astype(jnp.float32))
-        kept_ref[j] = jnp.where(flags_ref[first + j] > 0, jnp.minimum(1.0, cut * cut), 1.0)
+                factors.append(jnp.concatenate([factor, factor], axis=1))
+            for c in range(0, cols, chunk):
+                spectrum = products(y_ref.at[parity], high_ref, low_ref, c, chunk, units)
+                for r in range(0, units, 16):
+                    f = factors[r // levels][:, c : c + chunk]
+                    y = spectrum[r : r + 16] * jnp.concatenate([f, f], axis=0)
+                    high = y.astype(jnp.bfloat16)
+                    s_ref[parity, r : r + 16, c : c + chunk] = high
+                    s_ref[parity, units + r : units + r + 16, c : c + chunk] = (
+                        y - high.astype(jnp.float32)
+                    ).astype(jnp.bfloat16)
+        for c in range(0, depth, chunk):
+            even = products(s_ref.at[0], tables[2], tables[3], c, chunk, units)
+            uneven = products(s_ref.at[1], tables[6], tables[7], c, chunk, units)
+            for r in range(0, units, 16):
+                j, q = divmod(r, levels)
+                x, y = even[r : r + 16], uneven[r : r + 16]
+                out_ref[j, q : q + 16, c : c + chunk] -= x + y
+                d_ref[r : r + 16, c : c + chunk] = x - y
+        for r in range(0, units, 8):
+            j, q = divmod(r, levels)
+            d = jnp.concatenate([d_ref[r : r + 8, :], jnp.zeros((8, full - depth), jnp.float32)], axis=1)
+            start = half // LANES * LANES
+            out_ref[j, q : q + 8, start:] -= pltpu.roll(d, half, 1)[:, start:nlon]
+
+
+def products(y_ref, high_ref, low_ref, c, chunk, units):
+    both = jnp.dot(y_ref[...], high_ref[:, c : c + chunk], preferred_element_type=jnp.float32)
+    third = jnp.dot(y_ref[:units, :], low_ref[:, c : c + chunk], preferred_element_type=jnp.float32)
+    return both[:units] + both[units:] + third
+
+
+def base_of(nlon):
+    return nlon // LANES * LANES
 
 
 def mean_kernel(area, sums_ref, kept_ref, part_ref, out_ref, row_ref, sem):
@@ -318,16 +347,6 @@
     return nlon // LANES * LANES
 
 
-def product(y, high, low):
-    y_high = y.astype(jnp.bfloat16)
-    y_low = (y - y_high.astype(jnp.float32)).astype(jnp.bfloat16)
-    count = y.shape[0]
-    both = jnp.dot(
-        jnp.concatenate([y_high, y_low], axis=0), high, preferred_element_type=jnp.float32
-    )
-    return both[:count] + both[count:] + jnp.dot(y_high, low, preferred_element_type=jnp.float32)
-
-
 def call(kernel, ins, outs, megabytes, scratch=(), out_space=pltpu.VMEM):
     return pl.pallas_call(
         kernel,
@@ -347,7 +366,6 @@
     rows, levels, nlon = height.shape
     count = lax.axis_size("lat")
     nlat = rows * count
-    full = round_up(nlon, LANES)
     half = nlon // 2
     smem, vmem, hbm = pltpu.SMEM, pltpu.VMEM, pltpu.HBM
     f32 = jnp.float32
@@ -410,7 +428,11 @@
         + [(x, vmem) for x in (height, merid_courant, part, a, b, *tables)],
         [(height.shape, f32), ((rows, 8, LANES), f32)],
         24,
-        [pltpu.VMEM((rows * levels, full), f32)],
+        [
+            pltpu.VMEM((2, 2 * rows * levels, depth), jnp.bfloat16),
+            pltpu.VMEM((2, 2 * rows * levels, cols), jnp.bfloat16),
+            pltpu.VMEM((rows * levels, depth), f32),
+        ],
     )
     area = nlon * float(np.sum(np.sin(np.pi * (np.arange(nlat) + 0.5) / nlat)))
     (out,) = call(

time: 26.8 us -> 26.5 us (0.989)
  transfers between devices with their start and end apart: 6 -> 6, of which waited for: 3 -> 3; matrix products, arithmetic and copies ran while one was open for 0% -> 0% of each run, Pallas kernels for 18% -> 20%
where the time goes in v5:
time: 26.5 us; the launch traced here: 26.4 us
  Pallas kernels  10.7 us (40%)
  waiting for transfers between devices  7.74 us (29%)
  starting transfers between devices  7.67 us (29%)
    pallas_call x7, Pallas kernels, call(): pl.pallas_call(kernel, in_specs=[pl.BlockSpec(memory_space=space) for _,...  10.7 us
    ppermute x6, waiting for transfers between devices, permute(): return lax.ppermute(x, axes, pairs)  7.74 us
    ppermute x6, starting transfers between devices, permute(): return lax.ppermute(x, axes, pairs)  7.67 us
  transfers between devices with their start and end apart: 6, of which 3 were waited for; matrix products, arithmetic and copies ran while one was open for 0% of the time, Pallas kernels for 20%

profile of v5, /device:TPU:0, one launch (start us, length us, event | category | flops | bytes accessed | tf_op | source)
XLA Modules:
  0.0 26.4 jit_solution(8018176759627401926)
XLA Ops:
  0.0 0.0 copy-start.5
  0.0 0.0 copy-start
  0.0 0.0 copy-start.1
  0.0 0.0 copy-start.7
  0.0 0.0 copy-start.6
  0.0 1.3 %shard_map.111 = f32[3,360,128]{2,1,0:T(8,128)S(1)} custom-call(f32[4,32,1440]{2,1,0:T(8,128)} %h_ref.7, f32[4,32,1440]{2,1,0:T(8,128)} %v_ref.5), custom_call_target="tpu_custom_call" | custom-call | tf_op jit(solution)/shard_map/pallas_call | solution.py:351
  1.3 0.0 copy-start.4
  1.3 3.0 %collective-permute-start.5 = (f32[3,360,128]{2,1,0:T(8,128)S(1)}, f32[3,360,128]{2,1,0:T(8,128)S(1)}, u32[]{:S(2)}, u32[]{:S(2)}) collective-permute-start(f32[3,360,128]{2,1,0:T(8,128)S(1)} %shard_map.111), channel_id=1, source_target_pairs={{1,2},{3,4},{5,6},{7,8},{9,10},{11,12},{13,14},{2,1},{4,3},{6,5},{... | collective-permute-start | bytes 1658888 | tf_op jit(solution)/shard_map/ppermute | solution.py:362
  4.4 0.0 copy-done.5
  4.4 0.0 copy-done
  4.4 0.0 copy-done.1
  4.4 0.0 copy-done.7
  4.4 0.0 copy-done.6
  4.4 0.0 copy-start.3
  4.4 0.0 copy-start.2
  4.4 1.0 %shard_map.109 = (f32[3,32,1440]{2,1,0:T(8,128)S(1)}, f32[32,128]{1,0:T(8,128)S(1)}, f32[4,32,1440]{2,1,0:T(8,128)S(1)}) custom-call(f32[64]{0:T(128)S(1)} %copy-done.5, f32[1,32]{1,0:T(1,128)S(1)} %bitcast.2, f32[1,32]{1,0:T(1,128)S(1)} %bitcast.3, f32[4,32,1440]{2,1,0:T(8,128)S(1)} %copy-done, f32[4,32,1440]{2,1,0:T(8,128)S(1)} %copy-done.1), custom_call_target="tpu_custom_call" | custom-call | tf_op jit(solution)/shard_map/pallas_call | solution.py:351
  5.5 0.2 collective-permute-start.4
  5.6 0.4 %collective-permute-start = (f32[32,128]{1,0:T(8,128)S(1)}, f32[32,128]{1,0:T(8,128)S(1)}, u32[]{:S(2)}, u32[]{:S(2)}) collective-permute-start(f32[32,128]{1,0:T(8,128)S(1)} %get-tuple-element.18), channel_id=1, source_target_pairs={{0,1},{1,0},{2,3},{3,2},{4,5},{5,4},{6,7},{7,6},{8,9},{9,8},{10,11... | collective-permute-start | bytes 49160 | tf_op jit(solution)/shard_map/ppermute | solution.py:362
  6.0 1.5 %collective-permute-done = f32[32,128]{1,0:T(8,128)S(1)} collective-permute-done((f32[32,128]{1,0:T(8,128)S(1)}, f32[32,128]{1,0:T(8,128)S(1)}, u32[]{:S(2)}, u32[]{:S(2)}) %collective-permute-start) | collective-permute-done | bytes 16416 | tf_op jit(solution)/shard_map/ppermute | solution.py:362
  7.5 1.3 %collective-permute-start.1 = (f32[32,128]{1,0:T(8,128)S(1)}, f32[32,128]{1,0:T(8,128)S(1)}, u32[]{:S(2)}, u32[]{:S(2)}) collective-permute-start(f32[32,128]{1,0:T(8,128)S(1)} %add.12), channel_id=1, source_target_pairs={{0,4},{1,5},{2,6},{3,7},{4,0},{5,1},{6,2},{7,3},{8,12},{9,13},{10,... | collective-permute-start | bytes 49160 | tf_op jit(solution)/shard_map/ppermute | solution.py:362
  8.9 4.3 %collective-permute-done.1 = f32[32,128]{1,0:T(8,128)S(1)} collective-permute-done((f32[32,128]{1,0:T(8,128)S(1)}, f32[32,128]{1,0:T(8,128)S(1)}, u32[]{:S(2)}, u32[]{:S(2)}) %collective-permute-start.1) | collective-permute-done | bytes 16416 | tf_op jit(solution)/shard_map/ppermute | solution.py:362
  13.2 2.7 %collective-permute-start.2 = (f32[32,128]{1,0:T(8,128)S(1)}, f32[32,128]{1,0:T(8,128)S(1)}, u32[]{:S(2)}, u32[]{:S(2)}) collective-permute-start(f32[32,128]{1,0:T(8,128)S(1)} %add.13), channel_id=1, source_target_pairs={{0,8},{1,9},{2,10},{3,11},{4,12},{5,13},{6,14},{7,15},{8,0},{9,1},... | collective-permute-start | bytes 49160 | tf_op jit(solution)/shard_map/ppermute | solution.py:362
  15.9 1.9 %collective-permute-done.2 = f32[32,128]{1,0:T(8,128)S(1)} collective-permute-done((f32[32,128]{1,0:T(8,128)S(1)}, f32[32,128]{1,0:T(8,128)S(1)}, u32[]{:S(2)}, u32[]{:S(2)}) %collective-permute-start.2) | collective-permute-done | bytes 16416 | tf_op jit(solution)/shard_map/ppermute | solution.py:362
  17.8 0.0 collective-permute-start.3
  17.8 0.0 copy-done.4
  17.8 1.2 %shard_map.112 = (bf16[768,768]{1,0:T(8,128)(2,1)S(1)}, bf16[768,768]{1,0:T(8,128)(2,1)S(1)}, bf16[768,768]{1,0:T(8,128)(2,1)S(1)}, bf16[768,768]{1,0:T(8,128)(2,1)S(1)}) custom-call(f32[216,768]{1,0:T(8,128)S(1)} %copy-done.4), custom_call_target="tpu_custom_call" | custom-call | tf_op jit(solution)/shard_map/pallas_call | solution.py:351
  19.0 0.0 copy-done.3
  19.0 1.2 %shard_map.113 = (bf16[768,768]{1,0:T(8,128)(2,1)S(1)}, bf16[768,768]{1,0:T(8,128)(2,1)S(1)}, bf16[768,768]{1,0:T(8,128)(2,1)S(1)}, bf16[768,768]{1,0:T(8,128)(2,1)S(1)}) custom-call(f32[216,768]{1,0:T(8,128)S(1)} %copy-done.3), custom_call_target="tpu_custom_call" | custom-call | tf_op jit(solution)/shard_map/pallas_call | solution.py:351
  20.2 0.0 copy-done.2
  20.2 0.0 copy-start.8
  20.2 0.0 copy-start.9
  20.3 0.0 copy-start.10
  20.3 1.8 %shard_map.110.part_ref = f32[4,32,1440]{2,1,0:T(8,128)S(1)} custom-call(f32[4,32,1440]{2,1,0:T(8,128)S(1)} %copy-done, f32[4,32,1440]{2,1,0:T(8,128)S(1)} %copy-done.2, f32[4,32,1440]{2,1,0:T(8,128)S(1)} %get-tuple-element.19.s_ref), custom_call_target="tpu_custom_call" | custom-call | tf_op jit(solution)/shard_map/pallas_call | solution.py:351
  22.1 0.0 collective-permute-done.3
  22.1 0.0 collective-permute-done.5.b_ref
  22.1 0.0 collective-permute-done.4.a_ref
  22.1 0.0 copy-done.8
  22.1 0.0 copy-done.9
  22.2 0.0 copy-done.10
  22.2 3.2 %shard_map.114 = (f32[4,32,1440]{2,1,0:T(8,128)S(1)}, f32[4,8,128]{2,1,0:T(8,128)S(1)}) custom-call(f32[64]{0:T(128)S(1)} %copy-done.5, f32[65]{0:T(128)S(1)} %copy-done.10, s32[64]{0:T(128)S(1)} %copy-done.8, s32[64]{0:T(128)S(1)} %copy-done.9, f32[4,32,1440]{2,1,0:T(8,128)S(1)} %copy-done, f32[4,32,1440]{2,1,0:T(8,128)S(1)} %copy-done.1, ...), custom_call_target="tpu_custom_call" | custom-call | tf_op jit(solution)/shard_map/pallas_call | solution.py:351
  25.4 1.0 %shard_map.115 = f32[4,32,1440]{2,1,0:T(8,128)} custom-call(f32[32,128]{1,0:T(8,128)S(1)} %add.15.sums_ref, f32[4,8,128]{2,1,0:T(8,128)S(1)} %get-tuple-element.29.kept_ref, f32[4,32,1440]{2,1,0:T(8,128)S(1)} %get-tuple-element.30.part_ref), custom_call_target="tpu_custom_call" | custom-call | tf_op jit(solution)/shard_map/pallas_call | solution.py:351
  (4 shorter events, 0.0 us)
Async XLA Ops:
  0.0 4.4 %copy-start.5 = (f32[64]{0:T(128)S(1)}, f32[64]{0:T(128)}, u32[]{:S(2)}) copy-start(f32[64]{0:T(128)} %constant.8.clone.cos_ref.cos_row_ref) | copy-start | bytes 772
  0.0 4.4 %copy-start = (f32[4,32,1440]{2,1,0:T(8,128)S(1)}, f32[4,32,1440]{2,1,0:T(8,128)}, u32[]{:S(2)}) copy-start(f32[4,32,1440]{2,1,0:T(8,128)} %h_ref.7) | copy-start | bytes 2211844
  0.0 4.4 %copy-start.1 = (f32[4,32,1440]{2,1,0:T(8,128)S(1)}, f32[4,32,1440]{2,1,0:T(8,128)}, u32[]{:S(2)}) copy-start(f32[4,32,1440]{2,1,0:T(8,128)} %v_ref.5) | copy-start | bytes 2211844
  0.0 4.4 %copy-start.7 = (f32[32]{0:T(128)S(1)}, f32[32]{0:T(128)}, u32[]{:S(2)}) copy-start(f32[32]{0:T(128)} %param.15) | copy-start | bytes 388
  0.0 4.4 %copy-start.6 = (f32[32]{0:T(128)S(1)}, f32[32]{0:T(128)}, u32[]{:S(2)}) copy-start(f32[32]{0:T(128)} %param.14) | copy-start | bytes 388
  1.3 16.5 %copy-start.4 = (f32[216,768]{1,0:T(8,128)S(1)}, f32[216,768]{1,0:T(8,128)}, u32[]{:S(2)}) copy-start(f32[216,768]{1,0:T(8,128)} %constant.10.clone.source_ref) | copy-start | bytes 1990660
  1.3 20.8 %collective-permute-start.5 = (f32[3,360,128]{2,1,0:T(8,128)S(1)}, f32[3,360,128]{2,1,0:T(8,128)S(1)}, u32[]{:S(2)}, u32[]{:S(2)}) collective-permute-start(f32[3,360,128]{2,1,0:T(8,128)S(1)} %shard_map.111), channel_id=1, source_target_pairs={{1,2},{3,4},{5,6},{7,8},{9,10},{11,12},{13,14},{2,1},{4,3},{6,5},{... | collective-permute-start | bytes 1658888 | tf_op jit(solution)/shard_map/ppermute | solution.py:362
  4.4 14.6 %copy-start.3 = (f32[216,768]{1,0:T(8,128)S(1)}, f32[216,768]{1,0:T(8,128)}, u32[]{:S(2)}) copy-start(f32[216,768]{1,0:T(8,128)} %constant.11.clone.source_ref) | copy-start | bytes 1990660
  4.4 15.8 %copy-start.2 = (f32[4,32,1440]{2,1,0:T(8,128)S(1)}, f32[4,32,1440]{2,1,0:T(8,128)}, u32[]{:S(2)}) copy-start(f32[4,32,1440]{2,1,0:T(8,128)} %u_ref.1) | copy-start | bytes 2211844
  5.5 16.7 %collective-permute-start.4 = (f32[3,32,1440]{2,1,0:T(8,128)S(1)}, f32[3,32,1440]{2,1,0:T(8,128)S(1)}, u32[]{:S(2)}, u32[]{:S(2)}) collective-permute-start(f32[3,32,1440]{2,1,0:T(8,128)S(1)} %get-tuple-element.20), channel_id=1, source_target_pairs={{0,1},{2,3},{4,5},{6,7},{8,9},{10,11},{12,13},{14,15},{1,0},{3,2},... | collective-permute-start | bytes 1658888 | tf_op jit(solution)/shard_map/ppermute | solution.py:362
  5.6 1.9 %collective-permute-start = (f32[32,128]{1,0:T(8,128)S(1)}, f32[32,128]{1,0:T(8,128)S(1)}, u32[]{:S(2)}, u32[]{:S(2)}) collective-permute-start(f32[32,128]{1,0:T(8,128)S(1)} %get-tuple-element.18), channel_id=1, source_target_pairs={{0,1},{1,0},{2,3},{3,2},{4,5},{5,4},{6,7},{7,6},{8,9},{9,8},{10,11... | collective-permute-start | bytes 49160 | tf_op jit(solution)/shard_map/ppermute | solution.py:362
  7.5 5.7 %collective-permute-start.1 = (f32[32,128]{1,0:T(8,128)S(1)}, f32[32,128]{1,0:T(8,128)S(1)}, u32[]{:S(2)}, u32[]{:S(2)}) collective-permute-start(f32[32,128]{1,0:T(8,128)S(1)} %add.12), channel_id=1, source_target_pairs={{0,4},{1,5},{2,6},{3,7},{4,0},{5,1},{6,2},{7,3},{8,12},{9,13},{10,... | collective-permute-start | bytes 49160 | tf_op jit(solution)/shard_map/ppermute | solution.py:362
  13.2 4.6 %collective-permute-start.2 = (f32[32,128]{1,0:T(8,128)S(1)}, f32[32,128]{1,0:T(8,128)S(1)}, u32[]{:S(2)}, u32[]{:S(2)}) collective-permute-start(f32[32,128]{1,0:T(8,128)S(1)} %add.13), channel_id=1, source_target_pairs={{0,8},{1,9},{2,10},{3,11},{4,12},{5,13},{6,14},{7,15},{8,0},{9,1},... | collective-permute-start | bytes 49160 | tf_op jit(solution)/shard_map/ppermute | solution.py:362
  17.8 4.3 %collective-permute-start.3 = (f32[32,128]{1,0:T(8,128)S(1)}, f32[32,128]{1,0:T(8,128)S(1)}, u32[]{:S(2)}, u32[]{:S(2)}) collective-permute-start(f32[32,128]{1,0:T(8,128)S(1)} %add.14), channel_id=1, source_target_pairs={{0,2},{1,3},{2,0},{3,1},{4,6},{5,7},{6,4},{7,5},{8,10},{9,11},{10,... | collective-permute-start | bytes 49160 | tf_op jit(solution)/shard_map/ppermute | solution.py:362
  20.2 1.9 %copy-start.8 = (s32[64]{0:T(128)S(1)}, s32[64]{0:T(128)}, u32[]{:S(2)}) copy-start(s32[64]{0:T(128)} %flags_ref.1) | copy-start | bytes 772
  20.2 1.9 %copy-start.9 = (s32[64]{0:T(128)S(1)}, s32[64]{0:T(128)}, u32[]{:S(2)}) copy-start(s32[64]{0:T(128)} %cutoffs_ref.1) | copy-start | bytes 772
  20.3 1.9 %copy-start.10 = (f32[65]{0:T(128)S(1)}, f32[65]{0:T(128)}, u32[]{:S(2)}) copy-start(f32[65]{0:T(128)} %constant.9.clone.cos_face_ref) | copy-start | bytes 784

commit v6 on v5

--- a/solution.py
+++ b/solution.py
@@ -153,19 +153,19 @@
 
 
 def zonal_kernel(h_ref, u_ref, s_ref, out_ref):
-    rows, levels, nlon = h_ref.shape
+    rows, _, nlon = h_ref.shape
     full = round_up(nlon, LANES)
     for j in range(rows):
-        for g in range(0, levels, 16):
-            at = slice(g, g + 16)
-            h0 = h_ref[j, at, :]
-            h = wrapped(h0, nlon, full)
-            u = wrapped(u_ref[j, at, :], nlon, full)
-            face = 7.0 * (h + pltpu.roll(h, full - 1, 1))
-            face = face - (pltpu.roll(h, 1, 1) + pltpu.roll(h, full - 2, 1))
-            flux = (u + pltpu.roll(u, full - 1, 1)) * (face * (0.5 / 12.0))
-            div = flux - pltpu.roll(flux, 1, 1)
-            out_ref[j, at, :] = h0 - div[:, :nlon] + s_ref[j, at, :]
+        h0 = h_ref[j]
+        h = wrapped(h0, nlon, full)
+        u = wrapped(u_ref[j], nlon, full)
+        east = pltpu.roll(h, full - 1, 1)
+        far_east = pltpu.roll(h, full - 2, 1)
+        west = pltpu.roll(h, 1, 1)
+        face = (7.0 * (h + east) - (west + far_east)) * (0.5 / 12.0)
+        flux = (u + pltpu.roll(u, full - 1, 1)) * face
+        div = flux - pltpu.roll(flux, 1, 1)
+        out_ref[j] = h0 - div[:, :nlon] + s_ref[j]
 
 
 def table_kernel(parity, half, source_ref, high_ref, low_ref, high_t_ref, low_t_ref):
@@ -223,6 +223,7 @@
     cos_face_ref,
     flags_ref,
     cutoffs_ref,
+    sums_ref,
     h_ref,
     v_ref,
     part_ref,
@@ -230,7 +231,7 @@
     b_ref,
     *rest,
 ):
-    tables, (out_ref, kept_ref, y_ref, s_ref, d_ref) = rest[:8], rest[8:]
+    tables, (result_ref, out_ref, y_ref, s_ref, d_ref, sem) = rest[:8], rest[8:]
     rows, levels, nlon = h_ref.shape
     full = round_up(nlon, LANES)
     half = nlon // 2
@@ -248,7 +249,18 @@
     inverse_cos = [1.0 / jnp.full((8, LANES), cos_row_ref[first + j]) for j in range(rows)]
     face_cos = [cos_face_ref[first + f] * (0.5 / 12.0) for f in range(rows + 1)]
 
-    for g in range(levels // 8):
+    nlat = cos_row_ref.shape[0]
+    area = nlon * float(np.sum(np.sin(np.pi * (np.arange(nlat) + 0.5) / nlat)))
+    mean = sums_ref[:, :LANES] * (1.0 / area)
+    groups = levels // 8
+    sends = [
+        pltpu.make_async_copy(
+            out_ref.at[:, pl.ds(8 * g, 8), :], result_ref.at[:, pl.ds(8 * g, 8), :], sem.at[g]
+        )
+        for g in range(groups)
+    ]
+
+    def update(g, shift):
         at = slice(8 * g, 8 * g + 8)
         for k in range(full // LANES):
             lanes = slice(k * LANES, min((k + 1) * LANES, nlon))
@@ -265,14 +277,19 @@
                 flux.append((speed[f] + speed[f + 1]) * face_cos[f] * p)
             for j in range(rows):
                 div = (flux[j + 1] - flux[j]) * inverse_cos[j][:, :wide]
-                out_ref[j, at, lanes] = part_ref[j, at, lanes] - div
-
-    for j in range(rows):
-        cut = jnp.full((8, LANES), cutoffs_ref[first + j].astype(jnp.float32))
-        kept_ref[j] = jnp.where(flags_ref[first + j] > 0, jnp.minimum(1.0, cut * cut), 1.0)
+                new = part_ref[j, at, lanes] - div
+                out_ref[j, at, lanes] = new - mean[at, :wide] if shift else new
+
+    @pl.when(marked == 0)
+    def _():
+        for g in range(groups):
+            update(g, True)
+            sends[g].start()
 
     @pl.when(marked > 0)
     def _():
+        for g in range(groups):
+            update(g, False)
         for r in range(0, units, 16):
             j, q = divmod(r, levels)
             x = out_ref[j, q : q + 16, :]
@@ -314,33 +331,34 @@
                 x, y = even[r : r + 16], uneven[r : r + 16]
                 out_ref[j, q : q + 16, c : c + chunk] -= x + y
                 d_ref[r : r + 16, c : c + chunk] = x - y
-        for r in range(0, units, 8):
-            j, q = divmod(r, levels)
-            d = jnp.concatenate([d_ref[r : r + 8, :], jnp.zeros((8, full - depth), jnp.float32)], axis=1)
-            start = half // LANES * LANES
-            out_ref[j, q : q + 8, start:] -= pltpu.roll(d, half, 1)[:, start:nlon]
+        kept = []
+        for j in range(rows):
+            cut = jnp.full((8, LANES), cutoffs_ref[first + j].astype(jnp.float32))
+            kept.append(jnp.where(flags_ref[first + j] > 0, jnp.minimum(1.0, cut * cut), 1.0))
+        start = half // LANES * LANES
+        for g in range(groups):
+            at = slice(8 * g, 8 * g + 8)
+            for j in range(rows):
+                r = j * levels + 8 * g
+                d = jnp.concatenate([d_ref[r : r + 8, :], jnp.zeros((8, full - depth), jnp.float32)], axis=1)
+                d = pltpu.roll(d, half, 1)
+                shift = mean[at] * kept[j]
+                for k in range(full // LANES):
+                    lanes = slice(k * LANES, min((k + 1) * LANES, nlon))
+                    less = shift[:, : lanes.stop - lanes.start]
+                    if lanes.start >= start:
+                        less = less + d[:, lanes]
+                    out_ref[j, at, lanes] -= less
+            sends[g].start()
+
+    for send in sends:
+        send.wait()
 
 
 def products(y_ref, high_ref, low_ref, c, chunk, units):
     both = jnp.dot(y_ref[...], high_ref[:, c : c + chunk], preferred_element_type=jnp.float32)
     third = jnp.dot(y_ref[:units, :], low_ref[:, c : c + chunk], preferred_element_type=jnp.float32)
     return both[:units] + both[units:] + third
-
-
-def base_of(nlon):
-    return nlon // LANES * LANES
-
-
-def mean_kernel(area, sums_ref, kept_ref, part_ref, out_ref, row_ref, sem):
-    rows = part_ref.shape[0]
-    mean = sums_ref[:, :1] * (1.0 / area)
-    copies = []
-    for j in range(rows):
-        row_ref[j] = part_ref[j] - mean * kept_ref[j, :1, :1]
-        copies.append(pltpu.make_async_copy(row_ref.at[j], out_ref.at[j], sem.at[j]))
-        copies[-1].start()
-    for c in copies:
-        c.wait()
 
 
 def base_of(nlon):
@@ -417,30 +435,26 @@
 
     bits = [1 << i for i in range((count - 1).bit_length())]
     if count == 1 << len(bits):
-        for d in bits[:1] + bits[2:] + bits[1:2]:
-            sums = sums + permute(sums, [(i, i ^ d) for i in range(count)])
+        far = bits[2:]
+        rounds = [bits[:1], *([*far[i : i + 2], sum(far[i : i + 2])] for i in range(0, len(far), 2)), bits[1:2]]
+        for masks in rounds:
+            sums = sums + sum(permute(sums, [(p, p ^ mask) for p in range(count)]) for mask in dict.fromkeys(masks))
     else:
         sums = lax.psum(sums, "lat")
 
-    part, kept = call(
+    (out,) = call(
         finish_kernel,
         [(cos_row, smem), (cos_face, smem), (flags, smem), (cutoffs, smem)]
-        + [(x, vmem) for x in (height, merid_courant, part, a, b, *tables)],
-        [(height.shape, f32), ((rows, 8, LANES), f32)],
+        + [(x, vmem) for x in (sums, height, merid_courant, part, a, b, *tables)],
+        [(height.shape, f32)],
         24,
         [
+            pltpu.VMEM(height.shape, f32),
             pltpu.VMEM((2, 2 * rows * levels, depth), jnp.bfloat16),
             pltpu.VMEM((2, 2 * rows * levels, cols), jnp.bfloat16),
             pltpu.VMEM((rows * levels, depth), f32),
+            pltpu.SemaphoreType.DMA((levels // 8,)),
         ],
-    )
-    area = nlon * float(np.sum(np.sin(np.pi * (np.arange(nlat) + 0.5) / nlat)))
-    (out,) = call(
-        functools.partial(mean_kernel, area),
-        [(sums, vmem), (kept, vmem), (part, vmem)],
-        [(height.shape, f32)],
-        4,
-        [pltpu.VMEM(height.shape, f32), pltpu.SemaphoreType.DMA((rows,))],
         hbm,
     )
     return out

time: 26.5 us -> 24.7 us (0.932)
  waiting for transfers between devices: 7.74 us -> 5.36 us
  starting transfers between devices: 7.67 us -> 8.75 us
  Pallas kernels: 10.7 us -> 10.2 us
    ppermute x6 -> x7, waiting for transfers between devices: 7.74 us -> 5.36 us  [permute(): return lax.ppermute(x, axes, pairs)]
    ppermute x6 -> x7, starting transfers between devices: 7.67 us -> 8.75 us  [permute(): return lax.ppermute(x, axes, pairs)]
    pallas_call x7 -> x6, Pallas kernels: 10.7 us -> 10.2 us  [call(): pl.pallas_call(kernel, in_specs=[pl.BlockSpec(memory_space=space) for _,...]
  transfers between devices with their start and end apart: 6 -> 7, of which waited for: 3 -> 3; matrix products, arithmetic and copies ran while one was open for 0% -> 0% of each run, Pallas kernels for 20% -> 19%
where the time goes in v6:
time: 24.7 us; the launch traced here: 24.5 us
  Pallas kernels  10.2 us (41%)
  starting transfers between devices  8.75 us (35%)
  waiting for transfers between devices  5.36 us (22%)
    pallas_call x6, Pallas kernels, call(): pl.pallas_call(kernel, in_specs=[pl.BlockSpec(memory_space=space) for _,...  10.2 us
    ppermute x7, starting transfers between devices, permute(): return lax.ppermute(x, axes, pairs)  8.75 us
    ppermute x7, waiting for transfers between devices, permute(): return lax.ppermute(x, axes, pairs)  5.36 us
  transfers between devices with their start and end apart: 7, of which 3 were waited for; matrix products, arithmetic and copies ran while one was open for 0% of the time, Pallas kernels for 19%

profile of v6, /device:TPU:0, one launch (start us, length us, event | category | flops | bytes accessed | tf_op | source)
XLA Modules:
  0.0 24.5 jit_solution(5436342298481413856)
XLA Ops:
  0.0 0.0 copy-start.5
  0.0 0.0 copy-start
  0.0 0.0 copy-start.1
  0.0 0.0 copy-start.7
  0.0 0.0 copy-start.6
  0.0 1.3 %shard_map.111 = f32[3,360,128]{2,1,0:T(8,128)S(1)} custom-call(f32[4,32,1440]{2,1,0:T(8,128)} %h_ref.7, f32[4,32,1440]{2,1,0:T(8,128)} %v_ref.5), custom_call_target="tpu_custom_call" | custom-call | tf_op jit(solution)/shard_map/pallas_call | solution.py:369
  1.3 0.0 copy-start.4
  1.3 3.0 %collective-permute-start.6 = (f32[3,360,128]{2,1,0:T(8,128)S(1)}, f32[3,360,128]{2,1,0:T(8,128)S(1)}, u32[]{:S(2)}, u32[]{:S(2)}) collective-permute-start(f32[3,360,128]{2,1,0:T(8,128)S(1)} %shard_map.111), channel_id=1, source_target_pairs={{1,2},{3,4},{5,6},{7,8},{9,10},{11,12},{13,14},{2,1},{4,3},{6,5},{... | collective-permute-start | bytes 1658888 | tf_op jit(solution)/shard_map/ppermute | solution.py:380
  4.4 0.0 copy-done.5
  4.4 0.0 copy-done
  4.4 0.0 copy-done.1
  4.4 0.0 copy-done.7
  4.4 0.0 copy-done.6
  4.4 0.0 copy-start.3
  4.4 0.0 copy-start.2
  4.4 1.0 %shard_map.109 = (f32[3,32,1440]{2,1,0:T(8,128)S(1)}, f32[32,128]{1,0:T(8,128)S(1)}, f32[4,32,1440]{2,1,0:T(8,128)S(1)}) custom-call(f32[64]{0:T(128)S(1)} %copy-done.5, f32[1,32]{1,0:T(1,128)S(1)} %bitcast.2, f32[1,32]{1,0:T(1,128)S(1)} %bitcast.3, f32[4,32,1440]{2,1,0:T(8,128)S(1)} %copy-done, f32[4,32,1440]{2,1,0:T(8,128)S(1)} %copy-done.1), custom_call_target="tpu_custom_call" | custom-call | tf_op jit(solution)/shard_map/pallas_call | solution.py:369
  5.5 0.2 collective-permute-start.5
  5.6 0.4 %collective-permute-start = (f32[32,128]{1,0:T(8,128)S(1)}, f32[32,128]{1,0:T(8,128)S(1)}, u32[]{:S(2)}, u32[]{:S(2)}) collective-permute-start(f32[32,128]{1,0:T(8,128)S(1)} %get-tuple-element.16), channel_id=1, source_target_pairs={{0,1},{1,0},{2,3},{3,2},{4,5},{5,4},{6,7},{7,6},{8,9},{9,8},{10,11... | collective-permute-start | bytes 49160 | tf_op jit(solution)/shard_map/ppermute | solution.py:380
  6.0 1.5 %collective-permute-done = f32[32,128]{1,0:T(8,128)S(1)} collective-permute-done((f32[32,128]{1,0:T(8,128)S(1)}, f32[32,128]{1,0:T(8,128)S(1)}, u32[]{:S(2)}, u32[]{:S(2)}) %collective-permute-start) | collective-permute-done | bytes 16416 | tf_op jit(solution)/shard_map/ppermute | solution.py:380
  7.5 3.4 %collective-permute-start.3 = (f32[32,128]{1,0:T(8,128)S(1)}, f32[32,128]{1,0:T(8,128)S(1)}, u32[]{:S(2)}, u32[]{:S(2)}) collective-permute-start(f32[32,128]{1,0:T(8,128)S(1)} %add.15), channel_id=1, source_target_pairs={{0,12},{1,13},{2,14},{3,15},{4,8},{5,9},{6,10},{7,11},{8,4},{9,5},... | collective-permute-start | bytes 49160 | tf_op jit(solution)/shard_map/ppermute | solution.py:380
  10.9 0.0 collective-permute-start.2
  10.9 1.0 %collective-permute-start.1 = (f32[32,128]{1,0:T(8,128)S(1)}, f32[32,128]{1,0:T(8,128)S(1)}, u32[]{:S(2)}, u32[]{:S(2)}) collective-permute-start(f32[32,128]{1,0:T(8,128)S(1)} %add.15), channel_id=1, source_target_pairs={{0,4},{1,5},{2,6},{3,7},{4,0},{5,1},{6,2},{7,3},{8,12},{9,13},{10,... | collective-permute-start | bytes 49160 | tf_op jit(solution)/shard_map/ppermute | solution.py:380
  11.9 3.5 %collective-permute-done.3 = f32[32,128]{1,0:T(8,128)S(1)} collective-permute-done((f32[32,128]{1,0:T(8,128)S(1)}, f32[32,128]{1,0:T(8,128)S(1)}, u32[]{:S(2)}, u32[]{:S(2)}) %collective-permute-start.3) | collective-permute-done | bytes 16416 | tf_op jit(solution)/shard_map/ppermute | solution.py:380
  15.4 0.4 %collective-permute-done.2 = f32[32,128]{1,0:T(8,128)S(1)} collective-permute-done((f32[32,128]{1,0:T(8,128)S(1)}, f32[32,128]{1,0:T(8,128)S(1)}, u32[]{:S(2)}, u32[]{:S(2)}) %collective-permute-start.2) | collective-permute-done | bytes 16416 | tf_op jit(solution)/shard_map/ppermute | solution.py:380
  15.7 0.0 collective-permute-done.1
  15.7 0.8 %collective-permute-start.4 = (f32[32,128]{1,0:T(8,128)S(1)}, f32[32,128]{1,0:T(8,128)S(1)}, u32[]{:S(2)}, u32[]{:S(2)}) collective-permute-start(f32[32,128]{1,0:T(8,128)S(1)} %add_add_fusion), channel_id=1, source_target_pairs={{0,2},{1,3},{2,0},{3,1},{4,6},{5,7},{6,4},{7,5},{8,10},{9,11},{10,... | collective-permute-start | bytes 49160 | tf_op jit(solution)/shard_map/ppermute | solution.py:380
  16.5 0.0 copy-done.4
  16.5 1.2 %shard_map.112 = (bf16[768,768]{1,0:T(8,128)(2,1)S(1)}, bf16[768,768]{1,0:T(8,128)(2,1)S(1)}, bf16[768,768]{1,0:T(8,128)(2,1)S(1)}, bf16[768,768]{1,0:T(8,128)(2,1)S(1)}) custom-call(f32[216,768]{1,0:T(8,128)S(1)} %copy-done.4), custom_call_target="tpu_custom_call" | custom-call | tf_op jit(solution)/shard_map/pallas_call | solution.py:369
  17.7 0.0 copy-done.3
  17.7 1.2 %shard_map.113 = (bf16[768,768]{1,0:T(8,128)(2,1)S(1)}, bf16[768,768]{1,0:T(8,128)(2,1)S(1)}, bf16[768,768]{1,0:T(8,128)(2,1)S(1)}, bf16[768,768]{1,0:T(8,128)(2,1)S(1)}) custom-call(f32[216,768]{1,0:T(8,128)S(1)} %copy-done.3), custom_call_target="tpu_custom_call" | custom-call | tf_op jit(solution)/shard_map/pallas_call | solution.py:369
  18.9 0.0 copy-done.2
  18.9 0.0 copy-start.8
  18.9 0.0 copy-start.9
  18.9 0.0 copy-start.10
  18.9 1.3 %shard_map.110.part_ref = f32[4,32,1440]{2,1,0:T(8,128)S(1)} custom-call(f32[4,32,1440]{2,1,0:T(8,128)S(1)} %copy-done, f32[4,32,1440]{2,1,0:T(8,128)S(1)} %copy-done.2, f32[4,32,1440]{2,1,0:T(8,128)S(1)} %get-tuple-element.17.s_ref), custom_call_target="tpu_custom_call" | custom-call | tf_op jit(solution)/shard_map/pallas_call | solution.py:369
  20.3 0.0 collective-permute-done.4
  20.3 0.0 collective-permute-done.6.b_ref
  20.3 0.0 collective-permute-done.5.a_ref
  20.3 0.0 copy-done.8
  20.4 0.0 copy-done.9
  20.4 0.0 copy-done.10
  20.4 4.1 %shard_map.114 = f32[4,32,1440]{2,1,0:T(8,128)} custom-call(f32[64]{0:T(128)S(1)} %copy-done.5, f32[65]{0:T(128)S(1)} %copy-done.10, s32[64]{0:T(128)S(1)} %copy-done.8, s32[64]{0:T(128)S(1)} %copy-done.9, f32[32,128]{1,0:T(8,128)S(1)} %add.19.sums_ref, f32[4,32,1440]{2,1,0:T(8,128)S(1)} %copy-done, f32[4,32,1440]{2,1,0:T(8,128)S(1)} %copy-done.1, ...), custom_call_target="tpu_custom_call" | custom-call | tf_op jit(solution)/shard_map/pallas_call | solution.py:369
  (3 shorter events, 0.0 us)
Async XLA Ops:
  0.0 4.4 %copy-start.5 = (f32[64]{0:T(128)S(1)}, f32[64]{0:T(128)}, u32[]{:S(2)}) copy-start(f32[64]{0:T(128)} %constant.8.clone.cos_ref.cos_row_ref) | copy-start | bytes 772
  0.0 4.4 %copy-start = (f32[4,32,1440]{2,1,0:T(8,128)S(1)}, f32[4,32,1440]{2,1,0:T(8,128)}, u32[]{:S(2)}) copy-start(f32[4,32,1440]{2,1,0:T(8,128)} %h_ref.7) | copy-start | bytes 2211844
  0.0 4.4 %copy-start.1 = (f32[4,32,1440]{2,1,0:T(8,128)S(1)}, f32[4,32,1440]{2,1,0:T(8,128)}, u32[]{:S(2)}) copy-start(f32[4,32,1440]{2,1,0:T(8,128)} %v_ref.5) | copy-start | bytes 2211844
  0.0 4.4 %copy-start.7 = (f32[32]{0:T(128)S(1)}, f32[32]{0:T(128)}, u32[]{:S(2)}) copy-start(f32[32]{0:T(128)} %param.15) | copy-start | bytes 388
  0.0 4.4 %copy-start.6 = (f32[32]{0:T(128)S(1)}, f32[32]{0:T(128)}, u32[]{:S(2)}) copy-start(f32[32]{0:T(128)} %param.14) | copy-start | bytes 388
  1.3 15.2 %copy-start.4 = (f32[216,768]{1,0:T(8,128)S(1)}, f32[216,768]{1,0:T(8,128)}, u32[]{:S(2)}) copy-start(f32[216,768]{1,0:T(8,128)} %constant.10.clone.source_ref) | copy-start | bytes 1990660
  1.3 19.0 %collective-permute-start.6 = (f32[3,360,128]{2,1,0:T(8,128)S(1)}, f32[3,360,128]{2,1,0:T(8,128)S(1)}, u32[]{:S(2)}, u32[]{:S(2)}) collective-permute-start(f32[3,360,128]{2,1,0:T(8,128)S(1)} %shard_map.111), channel_id=1, source_target_pairs={{1,2},{3,4},{5,6},{7,8},{9,10},{11,12},{13,14},{2,1},{4,3},{6,5},{... | collective-permute-start | bytes 1658888 | tf_op jit(solution)/shard_map/ppermute | solution.py:380
  4.4 13.3 %copy-start.3 = (f32[216,768]{1,0:T(8,128)S(1)}, f32[216,768]{1,0:T(8,128)}, u32[]{:S(2)}) copy-start(f32[216,768]{1,0:T(8,128)} %constant.11.clone.source_ref) | copy-start | bytes 1990660
  4.4 14.5 %copy-start.2 = (f32[4,32,1440]{2,1,0:T(8,128)S(1)}, f32[4,32,1440]{2,1,0:T(8,128)}, u32[]{:S(2)}) copy-start(f32[4,32,1440]{2,1,0:T(8,128)} %u_ref.1) | copy-start | bytes 2211844
  5.5 14.9 %collective-permute-start.5 = (f32[3,32,1440]{2,1,0:T(8,128)S(1)}, f32[3,32,1440]{2,1,0:T(8,128)S(1)}, u32[]{:S(2)}, u32[]{:S(2)}) collective-permute-start(f32[3,32,1440]{2,1,0:T(8,128)S(1)} %get-tuple-element.18), channel_id=1, source_target_pairs={{0,1},{2,3},{4,5},{6,7},{8,9},{10,11},{12,13},{14,15},{1,0},{3,2},... | collective-permute-start | bytes 1658888 | tf_op jit(solution)/shard_map/ppermute | solution.py:380
  5.6 1.9 %collective-permute-start = (f32[32,128]{1,0:T(8,128)S(1)}, f32[32,128]{1,0:T(8,128)S(1)}, u32[]{:S(2)}, u32[]{:S(2)}) collective-permute-start(f32[32,128]{1,0:T(8,128)S(1)} %get-tuple-element.16), channel_id=1, source_target_pairs={{0,1},{1,0},{2,3},{3,2},{4,5},{5,4},{6,7},{7,6},{8,9},{9,8},{10,11... | collective-permute-start | bytes 49160 | tf_op jit(solution)/shard_map/ppermute | solution.py:380
  7.5 7.9 %collective-permute-start.3 = (f32[32,128]{1,0:T(8,128)S(1)}, f32[32,128]{1,0:T(8,128)S(1)}, u32[]{:S(2)}, u32[]{:S(2)}) collective-permute-start(f32[32,128]{1,0:T(8,128)S(1)} %add.15), channel_id=1, source_target_pairs={{0,12},{1,13},{2,14},{3,15},{4,8},{5,9},{6,10},{7,11},{8,4},{9,5},... | collective-permute-start | bytes 49160 | tf_op jit(solution)/shard_map/ppermute | solution.py:380
  10.9 4.8 %collective-permute-start.2 = (f32[32,128]{1,0:T(8,128)S(1)}, f32[32,128]{1,0:T(8,128)S(1)}, u32[]{:S(2)}, u32[]{:S(2)}) collective-permute-start(f32[32,128]{1,0:T(8,128)S(1)} %add.15), channel_id=1, source_target_pairs={{0,8},{1,9},{2,10},{3,11},{4,12},{5,13},{6,14},{7,15},{8,0},{9,1},... | collective-permute-start | bytes 49160 | tf_op jit(solution)/shard_map/ppermute | solution.py:380
  10.9 4.8 %collective-permute-start.1 = (f32[32,128]{1,0:T(8,128)S(1)}, f32[32,128]{1,0:T(8,128)S(1)}, u32[]{:S(2)}, u32[]{:S(2)}) collective-permute-start(f32[32,128]{1,0:T(8,128)S(1)} %add.15), channel_id=1, source_target_pairs={{0,4},{1,5},{2,6},{3,7},{4,0},{5,1},{6,2},{7,3},{8,12},{9,13},{10,... | collective-permute-start | bytes 49160 | tf_op jit(solution)/shard_map/ppermute | solution.py:380
  15.7 4.6 %collective-permute-start.4 = (f32[32,128]{1,0:T(8,128)S(1)}, f32[32,128]{1,0:T(8,128)S(1)}, u32[]{:S(2)}, u32[]{:S(2)}) collective-permute-start(f32[32,128]{1,0:T(8,128)S(1)} %add_add_fusion), channel_id=1, source_target_pairs={{0,2},{1,3},{2,0},{3,1},{4,6},{5,7},{6,4},{7,5},{8,10},{9,11},{10,... | collective-permute-start | bytes 49160 | tf_op jit(solution)/shard_map/ppermute | solution.py:380
  18.9 1.4 %copy-start.8 = (s32[64]{0:T(128)S(1)}, s32[64]{0:T(128)}, u32[]{:S(2)}) copy-start(s32[64]{0:T(128)} %flags_ref.1) | copy-start | bytes 772
  18.9 1.4 %copy-start.9 = (s32[64]{0:T(128)S(1)}, s32[64]{0:T(128)}, u32[]{:S(2)}) copy-start(s32[64]{0:T(128)} %cutoffs_ref.1) | copy-start | bytes 772
  18.9 1.4 %copy-start.10 = (f32[65]{0:T(128)S(1)}, f32[65]{0:T(128)}, u32[]{:S(2)}) copy-start(f32[65]{0:T(128)} %constant.9.clone.cos_face_ref) | copy-start | bytes 784

commit v7 on v6

--- a/solution.py
+++ b/solution.py
@@ -218,55 +218,44 @@
     )
 
 
-def finish_kernel(
-    cos_row_ref,
-    cos_face_ref,
-    flags_ref,
-    cutoffs_ref,
-    sums_ref,
-    h_ref,
-    v_ref,
-    part_ref,
-    a_ref,
-    b_ref,
-    *rest,
-):
-    tables, (result_ref, out_ref, y_ref, s_ref, d_ref, sem) = rest[:8], rest[8:]
-    rows, levels, nlon = h_ref.shape
-    full = round_up(nlon, LANES)
-    half = nlon // 2
-    depth, cols = tables[0].shape
-    width = cols // 2
-    units = rows * levels
-    position = lax.axis_index("lat")
-    last = lax.axis_size("lat") - 1
-    first = position * rows
+def zoned(position, count):
+    edge = -(-count // 4)
+    return (position < edge) | (position >= count - edge)
+
+
+def early(position, count):
     odd = position % 2 == 1
-    bottom, top = position == 0, position == last
-    marked = flags_ref[first]
-    for j in range(1, rows):
-        marked = jnp.maximum(marked, flags_ref[first + j])
-    inverse_cos = [1.0 / jnp.full((8, LANES), cos_row_ref[first + j]) for j in range(rows)]
-    face_cos = [cos_face_ref[first + f] * (0.5 / 12.0) for f in range(rows + 1)]
-
-    nlat = cos_row_ref.shape[0]
-    area = nlon * float(np.sum(np.sin(np.pi * (np.arange(nlat) + 0.5) / nlat)))
-    mean = sums_ref[:, :LANES] * (1.0 / area)
-    groups = levels // 8
-    sends = [
-        pltpu.make_async_copy(
-            out_ref.at[:, pl.ds(8 * g, 8), :], result_ref.at[:, pl.ds(8 * g, 8), :], sem.at[g]
-        )
-        for g in range(groups)
-    ]
-
-    def update(g, shift):
-        at = slice(8 * g, 8 * g + 8)
-        for k in range(full // LANES):
-            lanes = slice(k * LANES, min((k + 1) * LANES, nlon))
+    upper = odd * (position + 1) + (1 - odd) * position
+    both = zoned(upper - 1, count) | zoned(upper, count)
+    return zoned(position, count) | (((upper & 3) == 0) & (both == False))
+
+
+class Rows:
+    def __init__(self, cos_row_ref, cos_face_ref, h_ref, v_ref, part_ref, a_ref):
+        self.refs = h_ref, v_ref, part_ref, a_ref
+        self.rows, self.levels, self.nlon = h_ref.shape
+        self.full = round_up(self.nlon, LANES)
+        self.position = lax.axis_index("lat")
+        self.last = lax.axis_size("lat") - 1
+        self.first = self.position * self.rows
+        self.inverse_cos = [
+            1.0 / jnp.full((8, LANES), cos_row_ref[self.first + j]) for j in range(self.rows)
+        ]
+        self.face_cos = [cos_face_ref[self.first + f] * (0.5 / 12.0) for f in range(self.rows + 1)]
+
+    def tiles(self, g):
+        for k in range(self.full // LANES):
+            yield k, slice(8 * g, 8 * g + 8), slice(k * LANES, min((k + 1) * LANES, self.nlon))
+
+    def update(self, g, far_tile, store):
+        h_ref, v_ref, part_ref, a_ref = self.refs
+        rows = self.rows
+        odd = self.position % 2 == 1
+        bottom, top = self.position == 0, self.position == self.last
+        for k, at, lanes in self.tiles(g):
             wide = lanes.stop - lanes.start
             near = [a_ref[i, at, lanes] for i in range(3)]
-            far = [packed_tile(b_ref, i, g, k, levels, nlon) for i in range(3)]
+            far = [far_tile(i, g, k) for i in range(3)]
             below = [jnp.where(odd, x, jnp.where(bottom, 0.0, y)) for x, y in zip(near, far)]
             above = [jnp.where(odd, jnp.where(top, 0.0, y), x) for x, y in zip(near, far)]
             height = [below[0], below[1], *(h_ref[j, at, lanes] for j in range(rows)), above[0], above[1]]
@@ -274,22 +263,37 @@
             flux = []
             for f in range(rows + 1):
                 p = 7.0 * (height[f + 1] + height[f + 2]) - (height[f] + height[f + 3])
-                flux.append((speed[f] + speed[f + 1]) * face_cos[f] * p)
+                flux.append((speed[f] + speed[f + 1]) * self.face_cos[f] * p)
             for j in range(rows):
-                div = (flux[j + 1] - flux[j]) * inverse_cos[j][:, :wide]
-                new = part_ref[j, at, lanes] - div
-                out_ref[j, at, lanes] = new - mean[at, :wide] if shift else new
-
-    @pl.when(marked == 0)
+                div = (flux[j + 1] - flux[j]) * self.inverse_cos[j][:, :wide]
+                store(j, at, lanes, part_ref[j, at, lanes] - div)
+
+
+def any_marked(flags_ref, first, rows):
+    marked = flags_ref[first]
+    for j in range(1, rows):
+        marked = jnp.maximum(marked, flags_ref[first + j])
+    return marked
+
+
+def filter_kernel(cos_row_ref, cos_face_ref, flags_ref, cutoffs_ref, h_ref, v_ref, part_ref, a_ref, b_ref, *rest):
+    tables, (out_ref, y_ref, s_ref, d_ref) = rest[:8], rest[8:]
+    rows, levels, nlon = h_ref.shape
+    full = round_up(nlon, LANES)
+    half = nlon // 2
+    depth, cols = tables[0].shape
+    width = cols // 2
+    units = rows * levels
+    first = lax.axis_index("lat") * rows
+
+    def store(j, at, lanes, value):
+        out_ref[j, at, lanes] = value
+
+    @pl.when(any_marked(flags_ref, first, rows) > 0)
     def _():
-        for g in range(groups):
-            update(g, True)
-            sends[g].start()
-
-    @pl.when(marked > 0)
-    def _():
-        for g in range(groups):
-            update(g, False)
+        state = Rows(cos_row_ref, cos_face_ref, h_ref, v_ref, part_ref, a_ref)
+        for g in range(levels // 8):
+            state.update(g, lambda i, g, k: packed_tile(b_ref, i, g, k, levels, nlon), store)
         for r in range(0, units, 16):
             j, q = divmod(r, levels)
             x = out_ref[j, q : q + 16, :]
@@ -331,24 +335,71 @@
                 x, y = even[r : r + 16], uneven[r : r + 16]
                 out_ref[j, q : q + 16, c : c + chunk] -= x + y
                 d_ref[r : r + 16, c : c + chunk] = x - y
+        start = half // LANES * LANES
+        for r in range(0, units, 8):
+            j, q = divmod(r, levels)
+            d = jnp.concatenate([d_ref[r : r + 8, :], jnp.zeros((8, full - depth), jnp.float32)], axis=1)
+            out_ref[j, q : q + 8, start:] -= pltpu.roll(d, half, 1)[:, start:nlon]
+
+
+def finish_kernel(
+    cos_row_ref,
+    cos_face_ref,
+    flags_ref,
+    cutoffs_ref,
+    sums_ref,
+    h_ref,
+    v_ref,
+    part_ref,
+    a_ref,
+    b_ref,
+    c_ref,
+    filtered_ref,
+    result_ref,
+    out_ref,
+    sem,
+):
+    rows, levels, nlon = h_ref.shape
+    first = lax.axis_index("lat") * rows
+    nlat = cos_row_ref.shape[0]
+    area = nlon * float(np.sum(np.sin(np.pi * (np.arange(nlat) + 0.5) / nlat)))
+    mean = sums_ref[:, :LANES] * (1.0 / area)
+    groups = levels // 8
+    sends = [
+        pltpu.make_async_copy(
+            out_ref.at[:, pl.ds(8 * g, 8), :], result_ref.at[:, pl.ds(8 * g, 8), :], sem.at[g]
+        )
+        for g in range(groups)
+    ]
+    marked = any_marked(flags_ref, first, rows)
+    state = Rows(cos_row_ref, cos_face_ref, h_ref, v_ref, part_ref, a_ref)
+
+    @pl.when(marked == 0)
+    def _():
+        soon = early(state.position, state.last + 1)
+
+        def far_tile(i, g, k):
+            x = packed_tile(b_ref, i, g, k, levels, nlon)
+            return jnp.where(soon, x, packed_tile(c_ref, i, g, k, levels, nlon))
+
+        def store(j, at, lanes, value):
+            out_ref[j, at, lanes] = value - mean[at, : lanes.stop - lanes.start]
+
+        for g in range(groups):
+            state.update(g, far_tile, store)
+            sends[g].start()
+
+    @pl.when(marked > 0)
+    def _():
         kept = []
         for j in range(rows):
             cut = jnp.full((8, LANES), cutoffs_ref[first + j].astype(jnp.float32))
             kept.append(jnp.where(flags_ref[first + j] > 0, jnp.minimum(1.0, cut * cut), 1.0))
-        start = half // LANES * LANES
         for g in range(groups):
-            at = slice(8 * g, 8 * g + 8)
-            for j in range(rows):
-                r = j * levels + 8 * g
-                d = jnp.concatenate([d_ref[r : r + 8, :], jnp.zeros((8, full - depth), jnp.float32)], axis=1)
-                d = pltpu.roll(d, half, 1)
-                shift = mean[at] * kept[j]
-                for k in range(full // LANES):
-                    lanes = slice(k * LANES, min((k + 1) * LANES, nlon))
-                    less = shift[:, : lanes.stop - lanes.start]
-                    if lanes.start >= start:
-                        less = less + d[:, lanes]
-                    out_ref[j, at, lanes] -= less
+            for k, at, lanes in state.tiles(g):
+                for j in range(rows):
+                    shift = (mean[at] * kept[j])[:, : lanes.stop - lanes.start]
+                    out_ref[j, at, lanes] = filtered_ref[j, at, lanes] - shift
             sends[g].start()
 
     for send in sends:
@@ -380,6 +431,27 @@
     return lax.ppermute(x, axes, pairs)
 
 
+def exchanges(parts, count):
+    flows = [(i, i + 1) for i in range(1, count - 1, 2)]
+    flows += [(j, i) for i, j in flows]
+    groups = []
+    for first in (True, False):
+        real = [(i, j) for i, j in flows if bool(early(j, count)) == first]
+        senders = set(range(count)) - {i for i, _ in real}
+        receivers = set(range(count)) - {j for _, j in real}
+        pairs = [(p * count + i, p * count + j) for p in range(parts) for i, j in real]
+        if parts % 2 == 0 and len(senders) == len(receivers):
+            spare = senders & receivers
+            local = {i for i in spare if i ^ 1 in spare}
+            away = [(i, i) for i in sorted(spare - local)]
+            away += zip(sorted(senders - spare), sorted(receivers - spare, reverse=True))
+            for p in range(parts):
+                pairs += [(p * count + i, p * count + (i ^ 1)) for i in sorted(local)]
+                pairs += [(p * count + i, (p ^ 1) * count + j) for i, j in away]
+        groups.append(pairs)
+    return groups
+
+
 def step(height, zonal_courant, merid_courant, rates, thresholds, flags, cutoffs):
     rows, levels, nlon = height.shape
     count = lax.axis_size("lat")
@@ -388,14 +460,7 @@
     smem, vmem, hbm = pltpu.SMEM, pltpu.VMEM, pltpu.HBM
     f32 = jnp.float32
 
-    between = [(i, i + 1) for i in range(1, count - 1, 2)]
     within = [(i, i + 1) for i in range(0, count - 1, 2)]
-    between = between + [(j, i) for i, j in between]
-    parts = lax.axis_size("member")
-    between = [(p * count + i, p * count + j) for p in range(parts) for i, j in between]
-    ends = [0, count - 1] if count % 2 == 0 else [0]
-    if parts % 2 == 0:
-        between += [(p * count + e, (p ^ 1) * count + e) for p in range(parts) for e in ends]
     within = within + [(j, i) for i, j in within]
     whole, _, extra = dense_tiles(levels, nlon)
     (edge_b,) = call(
@@ -408,7 +473,11 @@
         4,
         [pltpu.VMEM((3, levels, nlon), f32), pltpu.SemaphoreType.DMA((2,))],
     )
-    b = permute(edge_b, between, ("member", "lat"))
+    parts = lax.axis_size("member")
+    b, c = (
+        permute(edge_b, pairs, ("member", "lat"))
+        for pairs in exchanges(parts, count)
+    )
 
     cos_row = jnp.asarray(np.sin(np.pi * (np.arange(nlat) + 0.5) / nlat).astype(np.float32))
     faces = np.sin(np.pi * np.arange(nlat + 1) / nlat)
@@ -442,19 +511,25 @@
     else:
         sums = lax.psum(sums, "lat")
 
-    (out,) = call(
-        finish_kernel,
-        [(cos_row, smem), (cos_face, smem), (flags, smem), (cutoffs, smem)]
-        + [(x, vmem) for x in (sums, height, merid_courant, part, a, b, *tables)],
+    scalars = [(x, smem) for x in (cos_row, cos_face, flags, cutoffs)]
+    rows_and_edges = [(x, vmem) for x in (height, merid_courant, part, a, b)]
+    (filtered,) = call(
+        filter_kernel,
+        scalars + rows_and_edges + [(x, vmem) for x in tables],
         [(height.shape, f32)],
         24,
         [
-            pltpu.VMEM(height.shape, f32),
             pltpu.VMEM((2, 2 * rows * levels, depth), jnp.bfloat16),
             pltpu.VMEM((2, 2 * rows * levels, cols), jnp.bfloat16),
             pltpu.VMEM((rows * levels, depth), f32),
-            pltpu.SemaphoreType.DMA((levels // 8,)),
         ],
+    )
+    (out,) = call(
+        finish_kernel,
+        [*scalars, (sums, vmem), *rows_and_edges, (c, vmem), (filtered, vmem)],
+        [(height.shape, f32)],
+        8,
+        [pltpu.VMEM(height.shape, f32), pltpu.SemaphoreType.DMA((levels // 8,))],
         hbm,
     )
     return out

time: 24.7 us -> 34.5 us (1.40)
  waiting for transfers between devices: 5.36 us -> 14.5 us
  Pallas kernels: 10.2 us -> 10.8 us
    ppermute x7 -> x8, waiting for transfers between devices: 5.36 us -> 14.5 us  [permute(): return lax.ppermute(x, axes, pairs)]
    pallas_call x6 -> x7, Pallas kernels: 10.2 us -> 10.8 us  [call(): pl.pallas_call(kernel, in_specs=[pl.BlockSpec(memory_space=space) for _,...]
    ppermute x7 -> x8, starting transfers between devices: 8.75 us -> 8.78 us  [permute(): return lax.ppermute(x, axes, pairs)]
  transfers between devices with their start and end apart: 7 -> 8, of which waited for: 3 -> 3; matrix products, arithmetic and copies ran while one was open for 0% -> 0% of each run, Pallas kernels for 19% -> 23%
where the time goes in v7:
time: 34.5 us; the launch traced here: 34.3 us
  waiting for transfers between devices  14.5 us (42%)
  Pallas kernels  10.8 us (31%)
  starting transfers between devices  8.78 us (25%)
    ppermute x8, waiting for transfers between devices, permute(): return lax.ppermute(x, axes, pairs)  14.5 us
    pallas_call x7, Pallas kernels, call(): pl.pallas_call(kernel, in_specs=[pl.BlockSpec(memory_space=space) for _,...  10.8 us
    ppermute x8, starting transfers between devices, permute(): return lax.ppermute(x, axes, pairs)  8.78 us
  transfers between devices with their start and end apart: 8, of which 3 were waited for; matrix products, arithmetic and copies ran while one was open for 0% of the time, Pallas kernels for 23%

profile of v7, /device:TPU:0, one launch (start us, length us, event | category | flops | bytes accessed | tf_op | source)
XLA Modules:
  0.0 34.3 jit_solution(11336594199163998459)
XLA Ops:
  0.0 0.0 copy-start.5
  0.0 0.0 copy-start
  0.0 0.0 copy-start.1
  0.0 0.0 copy-start.10
  0.0 0.0 copy-start.9
  0.0 1.3 %shard_map.111 = f32[3,360,128]{2,1,0:T(8,128)S(1)} custom-call(f32[4,32,1440]{2,1,0:T(8,128)} %h_ref.9, f32[4,32,1440]{2,1,0:T(8,128)} %v_ref.7), custom_call_target="tpu_custom_call" | custom-call | tf_op jit(solution)/shard_map/pallas_call | solution.py:420
  1.3 0.0 copy-start.4
  1.3 3.0 %collective-permute-start.6 = (f32[3,360,128]{2,1,0:T(8,128)S(1)}, f32[3,360,128]{2,1,0:T(8,128)S(1)}, u32[]{:S(2)}, u32[]{:S(2)}) collective-permute-start(f32[3,360,128]{2,1,0:T(8,128)S(1)} %shard_map.111), channel_id=1, source_target_pairs={{1,2},{7,8},{11,12},{13,14},{2,1},{4,3},{8,7},{14,13},{17,18},{23,... | collective-permute-start | bytes 1658888 | tf_op jit(solution)/shard_map/ppermute | solution.py:431
  4.4 0.0 copy-done.5
  4.4 0.0 copy-done
  4.4 0.0 copy-done.1
  4.4 0.0 copy-done.10
  4.4 0.0 copy-done.9
  4.4 0.0 copy-start.3
  4.4 0.0 copy-start.2
  4.4 1.0 %shard_map.109 = (f32[3,32,1440]{2,1,0:T(8,128)S(1)}, f32[32,128]{1,0:T(8,128)S(1)}, f32[4,32,1440]{2,1,0:T(8,128)S(1)}) custom-call(f32[64]{0:T(128)S(1)} %copy-done.5, f32[1,32]{1,0:T(1,128)S(1)} %bitcast.2, f32[1,32]{1,0:T(1,128)S(1)} %bitcast.3, f32[4,32,1440]{2,1,0:T(8,128)S(1)} %copy-done, f32[4,32,1440]{2,1,0:T(8,128)S(1)} %copy-done.1), custom_call_target="tpu_custom_call" | custom-call | tf_op jit(solution)/shard_map/pallas_call | solution.py:420
  5.4 0.2 collective-permute-start.5
  5.6 0.4 %collective-permute-start.7 = (f32[3,360,128]{2,1,0:T(8,128)S(1)}, f32[3,360,128]{2,1,0:T(8,128)S(1)}, u32[]{:S(2)}, u32[]{:S(2)}) collective-permute-start(f32[3,360,128]{2,1,0:T(8,128)S(1)} %shard_map.111), channel_id=1, source_target_pairs={{3,4},{5,6},{9,10},{6,5},{10,9},{12,11},{19,20},{21,22},{25,26},{2... | collective-permute-start | bytes 1658888 | tf_op jit(solution)/shard_map/ppermute | solution.py:431
  6.0 0.1 collective-permute-start
  6.1 2.2 %collective-permute-done = f32[32,128]{1,0:T(8,128)S(1)} collective-permute-done((f32[32,128]{1,0:T(8,128)S(1)}, f32[32,128]{1,0:T(8,128)S(1)}, u32[]{:S(2)}, u32[]{:S(2)}) %collective-permute-start) | collective-permute-done | bytes 16416 | tf_op jit(solution)/shard_map/ppermute | solution.py:431
  8.3 3.5 %collective-permute-start.3 = (f32[32,128]{1,0:T(8,128)S(1)}, f32[32,128]{1,0:T(8,128)S(1)}, u32[]{:S(2)}, u32[]{:S(2)}) collective-permute-start(f32[32,128]{1,0:T(8,128)S(1)} %add.15), channel_id=1, source_target_pairs={{0,12},{1,13},{2,14},{3,15},{4,8},{5,9},{6,10},{7,11},{8,4},{9,5},... | collective-permute-start | bytes 49160 | tf_op jit(solution)/shard_map/ppermute | solution.py:431
  11.8 1.6 %collective-permute-start.2 = (f32[32,128]{1,0:T(8,128)S(1)}, f32[32,128]{1,0:T(8,128)S(1)}, u32[]{:S(2)}, u32[]{:S(2)}) collective-permute-start(f32[32,128]{1,0:T(8,128)S(1)} %add.15), channel_id=1, source_target_pairs={{0,8},{1,9},{2,10},{3,11},{4,12},{5,13},{6,14},{7,15},{8,0},{9,1},... | collective-permute-start | bytes 49160 | tf_op jit(solution)/shard_map/ppermute | solution.py:431
  13.4 8.6 %collective-permute-done.3 = f32[32,128]{1,0:T(8,128)S(1)} collective-permute-done((f32[32,128]{1,0:T(8,128)S(1)}, f32[32,128]{1,0:T(8,128)S(1)}, u32[]{:S(2)}, u32[]{:S(2)}) %collective-permute-start.3) | collective-permute-done | bytes 16416 | tf_op jit(solution)/shard_map/ppermute | solution.py:431
  21.9 0.0 collective-permute-start.1
  21.9 0.0 collective-permute-done.2
  21.9 3.7 %collective-permute-done.1 = f32[32,128]{1,0:T(8,128)S(1)} collective-permute-done((f32[32,128]{1,0:T(8,128)S(1)}, f32[32,128]{1,0:T(8,128)S(1)}, u32[]{:S(2)}, u32[]{:S(2)}) %collective-permute-start.1) | collective-permute-done | bytes 16416 | tf_op jit(solution)/shard_map/ppermute | solution.py:431
  25.7 0.0 collective-permute-start.4
  25.7 0.0 copy-done.4
  25.7 1.2 %shard_map.112 = (bf16[768,768]{1,0:T(8,128)(2,1)S(1)}, bf16[768,768]{1,0:T(8,128)(2,1)S(1)}, bf16[768,768]{1,0:T(8,128)(2,1)S(1)}, bf16[768,768]{1,0:T(8,128)(2,1)S(1)}) custom-call(f32[216,768]{1,0:T(8,128)S(1)} %copy-done.4), custom_call_target="tpu_custom_call" | custom-call | tf_op jit(solution)/shard_map/pallas_call | solution.py:420
  26.9 0.0 copy-done.3
  26.9 1.2 %shard_map.113 = (bf16[768,768]{1,0:T(8,128)(2,1)S(1)}, bf16[768,768]{1,0:T(8,128)(2,1)S(1)}, bf16[768,768]{1,0:T(8,128)(2,1)S(1)}, bf16[768,768]{1,0:T(8,128)(2,1)S(1)}) custom-call(f32[216,768]{1,0:T(8,128)S(1)} %copy-done.3), custom_call_target="tpu_custom_call" | custom-call | tf_op jit(solution)/shard_map/pallas_call | solution.py:420
  28.1 0.0 copy-done.2
  28.1 0.0 copy-start.6
  28.1 0.0 copy-start.7
  28.1 0.0 copy-start.8
  28.1 1.3 %shard_map.110.part_ref = f32[4,32,1440]{2,1,0:T(8,128)S(1)} custom-call(f32[4,32,1440]{2,1,0:T(8,128)S(1)} %copy-done, f32[4,32,1440]{2,1,0:T(8,128)S(1)} %copy-done.2, f32[4,32,1440]{2,1,0:T(8,128)S(1)} %get-tuple-element.17.s_ref), custom_call_target="tpu_custom_call" | custom-call | tf_op jit(solution)/shard_map/pallas_call | solution.py:420
  29.5 0.0 collective-permute-done.4
  29.5 0.0 collective-permute-done.6.b_ref
  29.5 0.0 collective-permute-done.5.a_ref
  29.5 0.0 copy-done.6
  29.5 0.0 copy-done.7
  29.5 0.0 copy-done.8
  29.5 3.3 %shard_map.114.filtered_ref = f32[4,32,1440]{2,1,0:T(8,128)S(1)} custom-call(f32[64]{0:T(128)S(1)} %copy-done.5, f32[65]{0:T(128)S(1)} %copy-done.8, s32[64]{0:T(128)S(1)} %copy-done.6, s32[64]{0:T(128)S(1)} %copy-done.7, f32[4,32,1440]{2,1,0:T(8,128)S(1)} %copy-done, f32[4,32,1440]{2,1,0:T(8,128)S(1)} %copy-done.1, f32[4,32,1440]{2,1,0:T(8,128)S(1)} %shard_map.110.part_ref, ...), custom_call_target="tpu_custom_call" | custom-call | tf_op jit(solution)/shard_map/pallas_call | solution.py:420
  32.8 0.0 collective-permute-done.7.c_ref
  32.8 1.5 %shard_map.115 = f32[4,32,1440]{2,1,0:T(8,128)} custom-call(f32[64]{0:T(128)S(1)} %copy-done.5, f32[65]{0:T(128)S(1)} %copy-done.8, s32[64]{0:T(128)S(1)} %copy-done.6, s32[64]{0:T(128)S(1)} %copy-done.7, f32[32,128]{1,0:T(8,128)S(1)} %add.19.sums_ref, f32[4,32,1440]{2,1,0:T(8,128)S(1)} %copy-done, f32[4,32,1440]{2,1,0:T(8,128)S(1)} %copy-done.1, ...), custom_call_target="tpu_custom_call" | custom-call | tf_op jit(solution)/shard_map/pallas_call | solution.py:420
  (3 shorter events, 0.0 us)
Async XLA Ops:
  0.0 4.4 %copy-start.5 = (f32[64]{0:T(128)S(1)}, f32[64]{0:T(128)}, u32[]{:S(2)}) copy-start(f32[64]{0:T(128)} %constant.8.clone.cos_ref.cos_row_ref) | copy-start | bytes 772
  0.0 4.4 %copy-start = (f32[4,32,1440]{2,1,0:T(8,128)S(1)}, f32[4,32,1440]{2,1,0:T(8,128)}, u32[]{:S(2)}) copy-start(f32[4,32,1440]{2,1,0:T(8,128)} %h_ref.9) | copy-start | bytes 2211844
  0.0 4.4 %copy-start.1 = (f32[4,32,1440]{2,1,0:T(8,128)S(1)}, f32[4,32,1440]{2,1,0:T(8,128)}, u32[]{:S(2)}) copy-start(f32[4,32,1440]{2,1,0:T(8,128)} %v_ref.7) | copy-start | bytes 2211844
  0.0 4.4 %copy-start.10 = (f32[32]{0:T(128)S(1)}, f32[32]{0:T(128)}, u32[]{:S(2)}) copy-start(f32[32]{0:T(128)} %param.15) | copy-start | bytes 388
  0.0 4.4 %copy-start.9 = (f32[32]{0:T(128)S(1)}, f32[32]{0:T(128)}, u32[]{:S(2)}) copy-start(f32[32]{0:T(128)} %param.14) | copy-start | bytes 388
  1.3 24.4 %copy-start.4 = (f32[216,768]{1,0:T(8,128)S(1)}, f32[216,768]{1,0:T(8,128)}, u32[]{:S(2)}) copy-start(f32[216,768]{1,0:T(8,128)} %constant.10.clone.source_ref) | copy-start | bytes 1990660
  1.3 28.2 %collective-permute-start.6 = (f32[3,360,128]{2,1,0:T(8,128)S(1)}, f32[3,360,128]{2,1,0:T(8,128)S(1)}, u32[]{:S(2)}, u32[]{:S(2)}) collective-permute-start(f32[3,360,128]{2,1,0:T(8,128)S(1)} %shard_map.111), channel_id=1, source_target_pairs={{1,2},{7,8},{11,12},{13,14},{2,1},{4,3},{8,7},{14,13},{17,18},{23,... | collective-permute-start | bytes 1658888 | tf_op jit(solution)/shard_map/ppermute | solution.py:431
  4.4 22.5 %copy-start.3 = (f32[216,768]{1,0:T(8,128)S(1)}, f32[216,768]{1,0:T(8,128)}, u32[]{:S(2)}) copy-start(f32[216,768]{1,0:T(8,128)} %constant.11.clone.source_ref) | copy-start | bytes 1990660
  4.4 23.7 %copy-start.2 = (f32[4,32,1440]{2,1,0:T(8,128)S(1)}, f32[4,32,1440]{2,1,0:T(8,128)}, u32[]{:S(2)}) copy-start(f32[4,32,1440]{2,1,0:T(8,128)} %u_ref.1) | copy-start | bytes 2211844
  5.4 24.1 %collective-permute-start.5 = (f32[3,32,1440]{2,1,0:T(8,128)S(1)}, f32[3,32,1440]{2,1,0:T(8,128)S(1)}, u32[]{:S(2)}, u32[]{:S(2)}) collective-permute-start(f32[3,32,1440]{2,1,0:T(8,128)S(1)} %get-tuple-element.18), channel_id=1, source_target_pairs={{0,1},{2,3},{4,5},{6,7},{8,9},{10,11},{12,13},{14,15},{1,0},{3,2},... | collective-permute-start | bytes 1658888 | tf_op jit(solution)/shard_map/ppermute | solution.py:431
  5.6 27.2 %collective-permute-start.7 = (f32[3,360,128]{2,1,0:T(8,128)S(1)}, f32[3,360,128]{2,1,0:T(8,128)S(1)}, u32[]{:S(2)}, u32[]{:S(2)}) collective-permute-start(f32[3,360,128]{2,1,0:T(8,128)S(1)} %shard_map.111), channel_id=1, source_target_pairs={{3,4},{5,6},{9,10},{6,5},{10,9},{12,11},{19,20},{21,22},{25,26},{2... | collective-permute-start | bytes 1658888 | tf_op jit(solution)/shard_map/ppermute | solution.py:431
  6.0 2.3 %collective-permute-start = (f32[32,128]{1,0:T(8,128)S(1)}, f32[32,128]{1,0:T(8,128)S(1)}, u32[]{:S(2)}, u32[]{:S(2)}) collective-permute-start(f32[32,128]{1,0:T(8,128)S(1)} %get-tuple-element.16), channel_id=1, source_target_pairs={{0,1},{1,0},{2,3},{3,2},{4,5},{5,4},{6,7},{7,6},{8,9},{9,8},{10,11... | collective-permute-start | bytes 49160 | tf_op jit(solution)/shard_map/ppermute | solution.py:431
  8.3 13.6 %collective-permute-start.3 = (f32[32,128]{1,0:T(8,128)S(1)}, f32[32,128]{1,0:T(8,128)S(1)}, u32[]{:S(2)}, u32[]{:S(2)}) collective-permute-start(f32[32,128]{1,0:T(8,128)S(1)} %add.15), channel_id=1, source_target_pairs={{0,12},{1,13},{2,14},{3,15},{4,8},{5,9},{6,10},{7,11},{8,4},{9,5},... | collective-permute-start | bytes 49160 | tf_op jit(solution)/shard_map/ppermute | solution.py:431
  11.8 10.2 %collective-permute-start.2 = (f32[32,128]{1,0:T(8,128)S(1)}, f32[32,128]{1,0:T(8,128)S(1)}, u32[]{:S(2)}, u32[]{:S(2)}) collective-permute-start(f32[32,128]{1,0:T(8,128)S(1)} %add.15), channel_id=1, source_target_pairs={{0,8},{1,9},{2,10},{3,11},{4,12},{5,13},{6,14},{7,15},{8,0},{9,1},... | collective-permute-start | bytes 49160 | tf_op jit(solution)/shard_map/ppermute | solution.py:431
  21.9 3.7 %collective-permute-start.1 = (f32[32,128]{1,0:T(8,128)S(1)}, f32[32,128]{1,0:T(8,128)S(1)}, u32[]{:S(2)}, u32[]{:S(2)}) collective-permute-start(f32[32,128]{1,0:T(8,128)S(1)} %add.15), channel_id=1, source_target_pairs={{0,4},{1,5},{2,6},{3,7},{4,0},{5,1},{6,2},{7,3},{8,12},{9,13},{10,... | collective-permute-start | bytes 49160 | tf_op jit(solution)/shard_map/ppermute | solution.py:431
  25.7 3.8 %collective-permute-start.4 = (f32[32,128]{1,0:T(8,128)S(1)}, f32[32,128]{1,0:T(8,128)S(1)}, u32[]{:S(2)}, u32[]{:S(2)}) collective-permute-start(f32[32,128]{1,0:T(8,128)S(1)} %add_add_fusion), channel_id=1, source_target_pairs={{0,2},{1,3},{2,0},{3,1},{4,6},{5,7},{6,4},{7,5},{8,10},{9,11},{10,... | collective-permute-start | bytes 49160 | tf_op jit(solution)/shard_map/ppermute | solution.py:431
  28.1 1.4 %copy-start.6 = (s32[64]{0:T(128)S(1)}, s32[64]{0:T(128)}, u32[]{:S(2)}) copy-start(s32[64]{0:T(128)} %flags_ref.3) | copy-start | bytes 772
  28.1 1.4 %copy-start.7 = (s32[64]{0:T(128)S(1)}, s32[64]{0:T(128)}, u32[]{:S(2)}) copy-start(s32[64]{0:T(128)} %cutoffs_ref.3) | copy-start | bytes 772
  28.1 1.4 %copy-start.8 = (f32[65]{0:T(128)S(1)}, f32[65]{0:T(128)}, u32[]{:S(2)}) copy-start(f32[65]{0:T(128)} %constant.9.clone.cos_face_ref) | copy-start | bytes 784

commit v8 on v6

--- a/solution.py
+++ b/solution.py
@@ -105,14 +105,15 @@
     return (pltpu.roll(last, LANES - at, 1) if at else last)[:, :rest]
 
 
+def edge_rows(upper, rows):
+    return jnp.where(upper, rows - 2, 1), jnp.where(upper, rows - 1, 0)
+
+
 def pack_kernel(h_ref, v_ref, out_ref, edge_ref, sem):
-    rows = h_ref.shape[0]
-    odd = lax.axis_index("lat") % 2 == 1
-    two = jnp.where(odd, rows - 2, 0)
-    one = jnp.where(odd, rows - 1, 0)
+    far, near = edge_rows(lax.axis_index("lat") % 2 == 1, h_ref.shape[0])
     copies = [
-        pltpu.make_async_copy(h_ref.at[pl.ds(two, 2)], edge_ref.at[pl.ds(0, 2)], sem.at[0]),
-        pltpu.make_async_copy(v_ref.at[pl.ds(one, 1)], edge_ref.at[pl.ds(2, 1)], sem.at[1]),
+        pltpu.make_async_copy(ref.at[row], edge_ref.at[i], sem.at[i])
+        for i, (ref, row) in enumerate([(h_ref, far), (h_ref, near), (v_ref, near)])
     ]
     for c in copies:
         c.start()
@@ -144,12 +145,10 @@
         total = total + acc * cos_ref[first + j]
     total = jnp.broadcast_to(jnp.sum(total, axis=1, keepdims=True), (levels, LANES))
     sum_ref[...] = total
-    even = position % 2 == 0
-    two = jnp.where(even, rows - 2, 0)
-    one = jnp.where(even, rows - 1, 0)
-    edge_ref[0] = h_ref[two]
-    edge_ref[1] = h_ref[two + 1]
-    edge_ref[2] = v_ref[one]
+    far, near = edge_rows(position % 2 == 0, rows)
+    edge_ref[0] = h_ref[far]
+    edge_ref[1] = h_ref[near]
+    edge_ref[2] = v_ref[near]
 
 
 def zonal_kernel(h_ref, u_ref, s_ref, out_ref):
@@ -218,78 +217,62 @@
     )
 
 
-def finish_kernel(
-    cos_row_ref,
-    cos_face_ref,
-    flags_ref,
-    cutoffs_ref,
-    sums_ref,
-    h_ref,
-    v_ref,
-    part_ref,
-    a_ref,
-    b_ref,
-    *rest,
-):
-    tables, (result_ref, out_ref, y_ref, s_ref, d_ref, sem) = rest[:8], rest[8:]
-    rows, levels, nlon = h_ref.shape
-    full = round_up(nlon, LANES)
-    half = nlon // 2
-    depth, cols = tables[0].shape
-    width = cols // 2
-    units = rows * levels
-    position = lax.axis_index("lat")
-    last = lax.axis_size("lat") - 1
-    first = position * rows
-    odd = position % 2 == 1
-    bottom, top = position == 0, position == last
-    marked = flags_ref[first]
-    for j in range(1, rows):
-        marked = jnp.maximum(marked, flags_ref[first + j])
-    inverse_cos = [1.0 / jnp.full((8, LANES), cos_row_ref[first + j]) for j in range(rows)]
-    face_cos = [cos_face_ref[first + f] * (0.5 / 12.0) for f in range(rows + 1)]
-
-    nlat = cos_row_ref.shape[0]
-    area = nlon * float(np.sum(np.sin(np.pi * (np.arange(nlat) + 0.5) / nlat)))
-    mean = sums_ref[:, :LANES] * (1.0 / area)
-    groups = levels // 8
-    sends = [
-        pltpu.make_async_copy(
-            out_ref.at[:, pl.ds(8 * g, 8), :], result_ref.at[:, pl.ds(8 * g, 8), :], sem.at[g]
-        )
-        for g in range(groups)
-    ]
-
-    def update(g, shift):
-        at = slice(8 * g, 8 * g + 8)
-        for k in range(full // LANES):
-            lanes = slice(k * LANES, min((k + 1) * LANES, nlon))
-            wide = lanes.stop - lanes.start
-            near = [a_ref[i, at, lanes] for i in range(3)]
-            far = [packed_tile(b_ref, i, g, k, levels, nlon) for i in range(3)]
-            below = [jnp.where(odd, x, jnp.where(bottom, 0.0, y)) for x, y in zip(near, far)]
-            above = [jnp.where(odd, jnp.where(top, 0.0, y), x) for x, y in zip(near, far)]
-            height = [below[0], below[1], *(h_ref[j, at, lanes] for j in range(rows)), above[0], above[1]]
-            speed = [below[2], *(v_ref[j, at, lanes] for j in range(rows)), above[2]]
-            flux = []
-            for f in range(rows + 1):
-                p = 7.0 * (height[f + 1] + height[f + 2]) - (height[f] + height[f + 3])
-                flux.append((speed[f] + speed[f + 1]) * face_cos[f] * p)
-            for j in range(rows):
-                div = (flux[j + 1] - flux[j]) * inverse_cos[j][:, :wide]
-                new = part_ref[j, at, lanes] - div
-                out_ref[j, at, lanes] = new - mean[at, :wide] if shift else new
-
-    @pl.when(marked == 0)
-    def _():
-        for g in range(groups):
-            update(g, True)
-            sends[g].start()
-
-    @pl.when(marked > 0)
-    def _():
-        for g in range(groups):
-            update(g, False)
+class Side:
+    def __init__(self, lower, scalars, arrays):
+        self.cos_row_ref, self.cos_face_ref, self.flags_ref, self.cutoffs_ref = scalars
+        self.h_ref, self.v_ref, self.part_ref = arrays
+        self.rows, self.levels, self.nlon = self.h_ref.shape
+        self.full = round_up(self.nlon, LANES)
+        self.lower = lower
+        position = lax.axis_index("lat")
+        self.first = position * self.rows
+        self.outermost = position == jnp.where(lower, 0, lax.axis_size("lat") - 1)
+
+    def row(self, i):
+        return jnp.where(self.lower, i, self.rows - 1 - i)
+
+    def tiles(self, g):
+        for k in range(self.full // LANES):
+            yield k, slice(8 * g, 8 * g + 8), slice(k * LANES, min((k + 1) * LANES, self.nlon))
+
+    def any_marked(self):
+        marked = self.flags_ref[self.first]
+        for j in range(1, self.rows):
+            marked = jnp.maximum(marked, self.flags_ref[self.first + j])
+        return marked > 0
+
+    def kept(self, i):
+        row = self.first + self.row(i)
+        cut = jnp.full((8, LANES), self.cutoffs_ref[row].astype(jnp.float32))
+        return jnp.where(self.flags_ref[row] > 0, jnp.minimum(1.0, cut * cut), 1.0)
+
+    def update(self, count, halo_tile, out_ref):
+        sign = jnp.where(self.lower, 1.0, -1.0)
+        scale = [sign / jnp.full((8, LANES), self.cos_row_ref[self.first + self.row(i)]) for i in range(count)]
+        face_cos = [
+            self.cos_face_ref[self.first + jnp.where(self.lower, i, self.rows - i)] * (0.5 / 12.0)
+            for i in range(count + 1)
+        ]
+        for g in range(self.levels // 8):
+            for k, at, lanes in self.tiles(g):
+                wide = lanes.stop - lanes.start
+                far, near, beyond = (jnp.where(self.outermost, 0.0, halo_tile(i, g, k)) for i in range(3))
+                height = [far, near, *(self.h_ref[self.row(i), at, lanes] for i in range(count + 2))]
+                speed = [beyond, *(self.v_ref[self.row(i), at, lanes] for i in range(count + 1))]
+                flux = []
+                for f in range(count + 1):
+                    p = 7.0 * (height[f + 1] + height[f + 2]) - (height[f] + height[f + 3])
+                    flux.append((speed[f] + speed[f + 1]) * face_cos[f] * p)
+                for i in range(count):
+                    div = (flux[i + 1] - flux[i]) * scale[i][:, :wide]
+                    out_ref[i, at, lanes] = self.part_ref[self.row(i), at, lanes] - div
+
+    def filter(self, count, tables, y_ref, s_ref, d_ref, out_ref):
+        levels, nlon, full = self.levels, self.nlon, self.full
+        half = nlon // 2
+        depth, cols = tables[0].shape
+        width = cols // 2
+        units = count * levels
         for r in range(0, units, 16):
             j, q = divmod(r, levels)
             x = out_ref[j, q : q + 16, :]
@@ -297,9 +280,7 @@
             x = jnp.concatenate([x, jnp.zeros((16, full - nlon), jnp.float32)], axis=1)
             far = pltpu.roll(x, full - half, 1)[:, :depth]
             for parity, y in ((0, near + far), (1, near - far)):
-                high = y.astype(jnp.bfloat16)
-                y_ref[parity, r : r + 16, :] = high
-                y_ref[parity, units + r : units + r + 16, :] = (y - high.astype(jnp.float32)).astype(jnp.bfloat16)
+                put_parts(y_ref, parity, r, units, slice(None), y)
         lane = lax.broadcasted_iota(jnp.int32, (8, width), 1)
         chunk = 256 if cols % 256 == 0 and depth % 256 == 0 else LANES
         for parity in (0, 1):
@@ -308,21 +289,18 @@
             weight = jnp.where((waves > 0) & (waves < half), 2.0 / nlon, 1.0 / nlon)
             inverse = 1.0 / jnp.maximum(waves, 1).astype(jnp.float32)
             factors = []
-            for j in range(rows):
-                ratio = cutoffs_ref[first + j].astype(jnp.float32) * inverse
+            for j in range(count):
+                row = self.first + self.row(j)
+                ratio = self.cutoffs_ref[row].astype(jnp.float32) * inverse
                 factor = (1.0 - jnp.minimum(1.0, ratio * ratio)) * weight
-                factor = jnp.where(flags_ref[first + j] > 0, factor, 0.0)
+                factor = jnp.where(self.flags_ref[row] > 0, factor, 0.0)
                 factors.append(jnp.concatenate([factor, factor], axis=1))
             for c in range(0, cols, chunk):
                 spectrum = products(y_ref.at[parity], high_ref, low_ref, c, chunk, units)
                 for r in range(0, units, 16):
                     f = factors[r // levels][:, c : c + chunk]
                     y = spectrum[r : r + 16] * jnp.concatenate([f, f], axis=0)
-                    high = y.astype(jnp.bfloat16)
-                    s_ref[parity, r : r + 16, c : c + chunk] = high
-                    s_ref[parity, units + r : units + r + 16, c : c + chunk] = (
-                        y - high.astype(jnp.float32)
-                    ).astype(jnp.bfloat16)
+                    put_parts(s_ref, parity, r, units, slice(c, c + chunk), y)
         for c in range(0, depth, chunk):
             even = products(s_ref.at[0], tables[2], tables[3], c, chunk, units)
             uneven = products(s_ref.at[1], tables[6], tables[7], c, chunk, units)
@@ -331,28 +309,91 @@
                 x, y = even[r : r + 16], uneven[r : r + 16]
                 out_ref[j, q : q + 16, c : c + chunk] -= x + y
                 d_ref[r : r + 16, c : c + chunk] = x - y
-        kept = []
-        for j in range(rows):
-            cut = jnp.full((8, LANES), cutoffs_ref[first + j].astype(jnp.float32))
-            kept.append(jnp.where(flags_ref[first + j] > 0, jnp.minimum(1.0, cut * cut), 1.0))
-        start = half // LANES * LANES
-        for g in range(groups):
-            at = slice(8 * g, 8 * g + 8)
-            for j in range(rows):
-                r = j * levels + 8 * g
-                d = jnp.concatenate([d_ref[r : r + 8, :], jnp.zeros((8, full - depth), jnp.float32)], axis=1)
-                d = pltpu.roll(d, half, 1)
-                shift = mean[at] * kept[j]
-                for k in range(full // LANES):
-                    lanes = slice(k * LANES, min((k + 1) * LANES, nlon))
-                    less = shift[:, : lanes.stop - lanes.start]
-                    if lanes.start >= start:
-                        less = less + d[:, lanes]
-                    out_ref[j, at, lanes] -= less
-            sends[g].start()
-
-    for send in sends:
-        send.wait()
+
+
+def put_parts(ref, parity, r, units, lanes, y):
+    high = y.astype(jnp.bfloat16)
+    ref[parity, r : r + 16, lanes] = high
+    ref[parity, units + r : units + r + 16, lanes] = (y - high.astype(jnp.float32)).astype(jnp.bfloat16)
+
+
+def near_kernel(*refs):
+    scalars, arrays, a_ref, tables = refs[:4], refs[4:7], refs[7], refs[8:16]
+    out_ref, y_ref, s_ref, d_ref = refs[16:]
+    side = Side(lax.axis_index("lat") % 2 == 1, scalars, arrays)
+    count = out_ref.shape[0]
+
+    def halo_tile(i, g, k):
+        return a_ref[i, 8 * g : 8 * g + 8, k * LANES : min((k + 1) * LANES, side.nlon)]
+
+    side.update(count, halo_tile, out_ref)
+
+    @pl.when(side.any_marked())
+    def _():
+        side.filter(count, tables, y_ref, s_ref, d_ref, out_ref)
+        start = side.nlon // 2 // LANES * LANES
+        for r in range(0, count * side.levels, 8):
+            j, q = divmod(r, side.levels)
+            out_ref[j, q : q + 8, start:] -= shifted(d_ref, r, side)[:, start:]
+
+
+def shifted(d_ref, r, side):
+    depth = d_ref.shape[1]
+    d = jnp.concatenate([d_ref[r : r + 8, :], jnp.zeros((8, side.full - depth), jnp.float32)], axis=1)
+    return pltpu.roll(d, side.nlon // 2, 1)[:, : side.nlon]
+
+
+def finish_kernel(*refs):
+    scalars, sums_ref, arrays, b_ref, done_ref, tables = refs[:4], refs[4], refs[5:8], refs[8], refs[9], refs[10:18]
+    result_ref, out_ref, y_ref, s_ref, d_ref, sem = refs[18:]
+    odd = lax.axis_index("lat") % 2 == 1
+    side, other = Side(odd == False, scalars, arrays), Side(odd, scalars, arrays)
+    levels, nlon = side.levels, side.nlon
+    done = done_ref.shape[0]
+    count = side.rows - done
+    nlat = scalars[0].shape[0]
+    area = nlon * float(np.sum(np.sin(np.pi * (np.arange(nlat) + 0.5) / nlat)))
+    mean = sums_ref[:, :LANES] * (1.0 / area)
+    sends = []
+
+    def send(view, i):
+        n = len(sends)
+        sends.append(pltpu.make_async_copy(out_ref.at[n], result_ref.at[view.row(i)], sem.at[n]))
+        sends[-1].start()
+
+    for i in range(done):
+        kept = other.kept(i)
+        for g in range(levels // 8):
+            for _, at, lanes in side.tiles(g):
+                shift = (mean[at] * kept)[:, : lanes.stop - lanes.start]
+                out_ref[i, at, lanes] = done_ref[i, at, lanes] - shift
+        send(other, i)
+
+    new_ref = out_ref.at[pl.ds(done, count)]
+    side.update(count, lambda i, g, k: packed_tile(b_ref, i, g, k, levels, nlon), new_ref)
+    marked = side.any_marked()
+
+    @pl.when(marked)
+    def _():
+        side.filter(count, tables, y_ref, s_ref, d_ref, new_ref)
+
+    @pl.when(marked == False)
+    def _():
+        d_ref[...] = jnp.zeros_like(d_ref)
+
+    start = nlon // 2 // LANES * LANES
+    for i in range(count):
+        kept = side.kept(i)
+        for g in range(levels // 8):
+            d = shifted(d_ref, i * levels + 8 * g, side)
+            for _, at, lanes in side.tiles(g):
+                less = (mean[at] * kept)[:, : lanes.stop - lanes.start]
+                if lanes.start >= start:
+                    less = less + d[:, lanes]
+                new_ref[i, at, lanes] -= less
+        send(side, i)
+    for copy in sends:
+        copy.wait()
 
 
 def products(y_ref, high_ref, low_ref, c, chunk, units):
@@ -406,7 +447,7 @@
         ],
         [((3, 8 * (whole + extra), LANES), f32)],
         4,
-        [pltpu.VMEM((3, levels, nlon), f32), pltpu.SemaphoreType.DMA((2,))],
+        [pltpu.VMEM((3, levels, nlon), f32), pltpu.SemaphoreType.DMA((3,))],
     )
     b = permute(edge_b, between, ("member", "lat"))
 
@@ -442,19 +483,25 @@
     else:
         sums = lax.psum(sums, "lat")
 
-    (out,) = call(
-        finish_kernel,
-        [(cos_row, smem), (cos_face, smem), (flags, smem), (cutoffs, smem)]
-        + [(x, vmem) for x in (sums, height, merid_courant, part, a, b, *tables)],
-        [(height.shape, f32)],
-        24,
-        [
-            pltpu.VMEM(height.shape, f32),
+    scalars = [(x, smem) for x in (cos_row, cos_face, flags, cutoffs)]
+    arrays = [(x, vmem) for x in (height, merid_courant, part)]
+    held = [(x, vmem) for x in tables]
+
+    def scratch(rows):
+        return [
             pltpu.VMEM((2, 2 * rows * levels, depth), jnp.bfloat16),
             pltpu.VMEM((2, 2 * rows * levels, cols), jnp.bfloat16),
             pltpu.VMEM((rows * levels, depth), f32),
-            pltpu.SemaphoreType.DMA((levels // 8,)),
-        ],
+        ]
+
+    done = rows - 2
+    (near,) = call(near_kernel, [*scalars, *arrays, (a, vmem), *held], [((done, levels, nlon), f32)], 16, scratch(done))
+    (out,) = call(
+        finish_kernel,
+        [*scalars, (sums, vmem), *arrays, (b, vmem), (near, vmem), *held],
+        [(height.shape, f32)],
+        16,
+        [pltpu.VMEM(height.shape, f32), *scratch(2), pltpu.SemaphoreType.DMA((rows,))],
         hbm,
     )
     return out

time: 24.7 us -> 31.7 us (1.28)
  local copies, waits for them, and re-layouts: 0.06 us -> 4.28 us
  waiting for transfers between devices: 5.36 us -> 7.17 us
  Pallas kernels: 10.2 us -> 12 us
  starting transfers between devices: 8.75 us -> 7.78 us
    unnamed x22 -> x28, local copies, waits for them, and re-layouts: 0.06 us -> 4.28 us
    ppermute x7, waiting for transfers between devices: 5.36 us -> 7.17 us  [permute(): return lax.ppermute(x, axes, pairs)]
    pallas_call x6 -> x7, Pallas kernels: 10.2 us -> 12 us  [call(): pl.pallas_call(kernel, in_specs=[pl.BlockSpec(memory_space=space) for _,...]
    ppermute x7, starting transfers between devices: 8.75 us -> 7.78 us  [permute(): return lax.ppermute(x, axes, pairs)]
  transfers between devices with their start and end apart: 7 -> 7, of which waited for: 3 -> 2; matrix products, arithmetic and copies ran while one was open for 0% -> 0% of each run, Pallas kernels for 19% -> 24%
where the time goes in v8:
time: 31.7 us; the launch traced here: 31.4 us
  Pallas kernels  12 us (38%)
  starting transfers between devices  7.78 us (25%)
  waiting for transfers between devices  7.17 us (23%)
  local copies, waits for them, and re-layouts  4.28 us (14%)
    pallas_call x7, Pallas kernels, call(): pl.pallas_call(kernel, in_specs=[pl.BlockSpec(memory_space=space) for _,...  12 us
    ppermute x7, starting transfers between devices, permute(): return lax.ppermute(x, axes, pairs)  7.78 us
    ppermute x7, waiting for transfers between devices, permute(): return lax.ppermute(x, axes, pairs)  7.17 us
    unnamed x28, local copies, waits for them, and re-layouts  4.28 us
  transfers between devices with their start and end apart: 7, of which 2 were waited for; matrix products, arithmetic and copies ran while one was open for 0% of the time, Pallas kernels for 24%

profile of v8, /device:TPU:0, one launch (start us, length us, event | category | flops | bytes accessed | tf_op | source)
XLA Modules:
  0.0 31.4 jit_solution(731888457025321680)
XLA Ops:
  0.0 0.0 copy-start
  0.0 1.1 %copy-done = f32[4,32,1440]{2,1,0:T(8,128)S(1)} copy-done((f32[4,32,1440]{2,1,0:T(8,128)S(1)}, f32[4,32,1440]{2,1,0:T(8,128)}, u32[]{:S(2)}) %copy-start) | copy-done | bytes 737304
  1.1 0.0 copy-start.2
  1.1 1.1 %copy-done.2 = f32[4,32,1440]{2,1,0:T(8,128)S(1)} copy-done((f32[4,32,1440]{2,1,0:T(8,128)S(1)}, f32[4,32,1440]{2,1,0:T(8,128)}, u32[]{:S(2)}) %copy-start.2) | copy-done | bytes 737304
  2.3 0.0 copy-start.7
  2.3 0.7 %copy-done.7 = f32[64]{0:T(128)S(1)} copy-done((f32[64]{0:T(128)S(1)}, f32[64]{0:T(128)}, u32[]{:S(2)}) %copy-start.7) | copy-done | bytes 280
  2.9 0.0 copy-start.12
  2.9 0.7 %copy-done.12 = f32[32]{0:T(128)S(1)} copy-done((f32[32]{0:T(128)S(1)}, f32[32]{0:T(128)}, u32[]{:S(2)}) %copy-start.12) | copy-done | bytes 152
  3.6 0.0 copy-start.13
  3.6 0.7 %copy-done.13 = f32[32]{0:T(128)S(1)} copy-done((f32[32]{0:T(128)S(1)}, f32[32]{0:T(128)}, u32[]{:S(2)}) %copy-start.13) | copy-done | bytes 152
  4.2 1.0 %shard_map.109 = (f32[3,32,1440]{2,1,0:T(8,128)S(1)}, f32[32,128]{1,0:T(8,128)S(1)}, f32[4,32,1440]{2,1,0:T(8,128)S(1)}) custom-call(f32[64]{0:T(128)S(1)} %copy-done.7, f32[1,32]{1,0:T(1,128)S(1)} %bitcast.2, f32[1,32]{1,0:T(1,128)S(1)} %bitcast.3, f32[4,32,1440]{2,1,0:T(8,128)S(1)} %copy-done, f32[4,32,1440]{2,1,0:T(8,128)S(1)} %copy-done.2), custom_call_target="tpu_custom_call" | custom-call | tf_op jit(solution)/shard_map/pallas_call | solution.py:410
  5.3 0.0 copy-start.6
  5.3 0.0 copy-start.5
  5.3 0.5 %collective-permute-start.6 = (f32[3,32,1440]{2,1,0:T(8,128)S(1)}, f32[3,32,1440]{2,1,0:T(8,128)S(1)}, u32[]{:S(2)}, u32[]{:S(2)}) collective-permute-start(f32[3,32,1440]{2,1,0:T(8,128)S(1)} %get-tuple-element.18), channel_id=1, source_target_pairs={{0,1},{2,3},{4,5},{6,7},{8,9},{10,11},{12,13},{14,15},{1,0},{3,2},... | collective-permute-start | bytes 1658888 | tf_op jit(solution)/shard_map/ppermute | solution.py:421
  5.8 1.3 %shard_map.111 = f32[3,360,128]{2,1,0:T(8,128)S(1)} custom-call(f32[4,32,1440]{2,1,0:T(8,128)} %refs_5_.3, f32[4,32,1440]{2,1,0:T(8,128)} %refs_6_.1), custom_call_target="tpu_custom_call" | custom-call | tf_op jit(solution)/shard_map/pallas_call | solution.py:410
  7.1 0.0 copy-start.1
  7.1 2.6 %collective-permute-start.5 = (f32[3,360,128]{2,1,0:T(8,128)S(1)}, f32[3,360,128]{2,1,0:T(8,128)S(1)}, u32[]{:S(2)}, u32[]{:S(2)}) collective-permute-start(f32[3,360,128]{2,1,0:T(8,128)S(1)} %shard_map.111), channel_id=1, source_target_pairs={{1,2},{3,4},{5,6},{7,8},{9,10},{11,12},{13,14},{2,1},{4,3},{6,5},{... | collective-permute-start | bytes 1658888 | tf_op jit(solution)/shard_map/ppermute | solution.py:421
  9.8 0.1 collective-permute-start
  9.9 1.0 %collective-permute-done = f32[32,128]{1,0:T(8,128)S(1)} collective-permute-done((f32[32,128]{1,0:T(8,128)S(1)}, f32[32,128]{1,0:T(8,128)S(1)}, u32[]{:S(2)}, u32[]{:S(2)}) %collective-permute-start) | collective-permute-done | bytes 16416 | tf_op jit(solution)/shard_map/ppermute | solution.py:421
  11.0 3.5 %collective-permute-start.3 = (f32[32,128]{1,0:T(8,128)S(1)}, f32[32,128]{1,0:T(8,128)S(1)}, u32[]{:S(2)}, u32[]{:S(2)}) collective-permute-start(f32[32,128]{1,0:T(8,128)S(1)} %add.15), channel_id=1, source_target_pairs={{0,12},{1,13},{2,14},{3,15},{4,8},{5,9},{6,10},{7,11},{8,4},{9,5},... | collective-permute-start | bytes 49160 | tf_op jit(solution)/shard_map/ppermute | solution.py:421
  14.5 0.0 collective-permute-start.2
  14.5 0.9 %collective-permute-start.1 = (f32[32,128]{1,0:T(8,128)S(1)}, f32[32,128]{1,0:T(8,128)S(1)}, u32[]{:S(2)}, u32[]{:S(2)}) collective-permute-start(f32[32,128]{1,0:T(8,128)S(1)} %add.15), channel_id=1, source_target_pairs={{0,4},{1,5},{2,6},{3,7},{4,0},{5,1},{6,2},{7,3},{8,12},{9,13},{10,... | collective-permute-start | bytes 49160 | tf_op jit(solution)/shard_map/ppermute | solution.py:421
  15.4 6.1 %collective-permute-done.3 = f32[32,128]{1,0:T(8,128)S(1)} collective-permute-done((f32[32,128]{1,0:T(8,128)S(1)}, f32[32,128]{1,0:T(8,128)S(1)}, u32[]{:S(2)}, u32[]{:S(2)}) %collective-permute-start.3) | collective-permute-done | bytes 16416 | tf_op jit(solution)/shard_map/ppermute | solution.py:421
  21.5 0.0 collective-permute-done.2
  21.5 0.0 collective-permute-done.1
  21.5 0.1 collective-permute-start.4
  21.6 0.0 copy-done.6
  21.6 1.2 %shard_map.112 = (bf16[768,768]{1,0:T(8,128)(2,1)S(1)}, bf16[768,768]{1,0:T(8,128)(2,1)S(1)}, bf16[768,768]{1,0:T(8,128)(2,1)S(1)}, bf16[768,768]{1,0:T(8,128)(2,1)S(1)}) custom-call(f32[216,768]{1,0:T(8,128)S(1)} %copy-done.6), custom_call_target="tpu_custom_call" | custom-call | tf_op jit(solution)/shard_map/pallas_call | solution.py:410
  22.8 0.0 copy-done.5
  22.8 1.2 %shard_map.113 = (bf16[768,768]{1,0:T(8,128)(2,1)S(1)}, bf16[768,768]{1,0:T(8,128)(2,1)S(1)}, bf16[768,768]{1,0:T(8,128)(2,1)S(1)}, bf16[768,768]{1,0:T(8,128)(2,1)S(1)}) custom-call(f32[216,768]{1,0:T(8,128)S(1)} %copy-done.5), custom_call_target="tpu_custom_call" | custom-call | tf_op jit(solution)/shard_map/pallas_call | solution.py:410
  24.0 0.0 copy-done.4
  24.0 0.0 copy-done.1
  24.0 0.0 copy-start.3
  24.0 0.0 copy-start.8
  24.0 0.0 copy-start.9
  24.0 0.0 copy-start.10
  24.0 0.0 copy-start.11
  24.0 1.3 %shard_map.110.refs_6_.refs_7_ = f32[4,32,1440]{2,1,0:T(8,128)S(1)} custom-call(f32[4,32,1440]{2,1,0:T(8,128)S(1)} %copy-done.1, f32[4,32,1440]{2,1,0:T(8,128)S(1)} %copy-done.4, f32[4,32,1440]{2,1,0:T(8,128)S(1)} %get-tuple-element.17.s_ref), custom_call_target="tpu_custom_call" | custom-call | tf_op jit(solution)/shard_map/pallas_call | solution.py:410
  25.4 0.0 collective-permute-done.4
  25.4 0.0 collective-permute-done.6.refs_7_
  25.4 0.0 copy-done.3
  25.4 0.0 copy-done.8
  25.4 0.0 copy-done.9
  25.4 0.0 copy-done.10
  25.5 0.0 copy-done.11
  25.5 2.6 %shard_map.114.refs_9_ = f32[2,32,1440]{2,1,0:T(8,128)S(1)} custom-call(f32[64]{0:T(128)S(1)} %copy-done.8, f32[65]{0:T(128)S(1)} %copy-done.11, s32[64]{0:T(128)S(1)} %copy-done.9, s32[64]{0:T(128)S(1)} %copy-done.10, f32[4,32,1440]{2,1,0:T(8,128)S(1)} %copy-done.1, f32[4,32,1440]{2,1,0:T(8,128)S(1)} %copy-done.3, ...), custom_call_target="tpu_custom_call" | custom-call | tf_op jit(solution)/shard_map/pallas_call | solution.py:410
  28.0 0.0 collective-permute-done.5.refs_8_
  28.1 3.4 %shard_map.115 = f32[4,32,1440]{2,1,0:T(8,128)} custom-call(f32[64]{0:T(128)S(1)} %copy-done.8, f32[65]{0:T(128)S(1)} %copy-done.11, s32[64]{0:T(128)S(1)} %copy-done.9, s32[64]{0:T(128)S(1)} %copy-done.10, f32[32,128]{1,0:T(8,128)S(1)} %add.19.refs_4_, f32[4,32,1440]{2,1,0:T(8,128)S(1)} %copy-done.1, f32[4,32,1440]{2,1,0:T(8,128)S(1)} %copy-done.3, ...), custom_call_target="tpu_custom_call" | custom-call | tf_op jit(solution)/shard_map/pallas_call | solution.py:410
  (4 shorter events, 0.0 us)
Async XLA Ops:
  0.0 1.1 %copy-start = (f32[4,32,1440]{2,1,0:T(8,128)S(1)}, f32[4,32,1440]{2,1,0:T(8,128)}, u32[]{:S(2)}) copy-start(f32[4,32,1440]{2,1,0:T(8,128)} %refs_5_.3) | copy-start | bytes 2211844
  1.1 1.1 %copy-start.2 = (f32[4,32,1440]{2,1,0:T(8,128)S(1)}, f32[4,32,1440]{2,1,0:T(8,128)}, u32[]{:S(2)}) copy-start(f32[4,32,1440]{2,1,0:T(8,128)} %refs_6_.1) | copy-start | bytes 2211844
  2.3 0.7 %copy-start.7 = (f32[64]{0:T(128)S(1)}, f32[64]{0:T(128)}, u32[]{:S(2)}) copy-start(f32[64]{0:T(128)} %constant.8.clone.cos_ref.refs_0_) | copy-start | bytes 772
  2.9 0.7 %copy-start.12 = (f32[32]{0:T(128)S(1)}, f32[32]{0:T(128)}, u32[]{:S(2)}) copy-start(f32[32]{0:T(128)} %param.14) | copy-start | bytes 388
  3.6 0.7 %copy-start.13 = (f32[32]{0:T(128)S(1)}, f32[32]{0:T(128)}, u32[]{:S(2)}) copy-start(f32[32]{0:T(128)} %param.15) | copy-start | bytes 388
  5.3 16.3 %copy-start.6 = (f32[216,768]{1,0:T(8,128)S(1)}, f32[216,768]{1,0:T(8,128)}, u32[]{:S(2)}) copy-start(f32[216,768]{1,0:T(8,128)} %constant.10.clone.source_ref) | copy-start | bytes 1990660
  5.3 17.5 %copy-start.5 = (f32[216,768]{1,0:T(8,128)S(1)}, f32[216,768]{1,0:T(8,128)}, u32[]{:S(2)}) copy-start(f32[216,768]{1,0:T(8,128)} %constant.11.clone.source_ref) | copy-start | bytes 1990660
  5.3 20.2 %collective-permute-start.6 = (f32[3,32,1440]{2,1,0:T(8,128)S(1)}, f32[3,32,1440]{2,1,0:T(8,128)S(1)}, u32[]{:S(2)}, u32[]{:S(2)}) collective-permute-start(f32[3,32,1440]{2,1,0:T(8,128)S(1)} %get-tuple-element.18), channel_id=1, source_target_pairs={{0,1},{2,3},{4,5},{6,7},{8,9},{10,11},{12,13},{14,15},{1,0},{3,2},... | collective-permute-start | bytes 1658888 | tf_op jit(solution)/shard_map/ppermute | solution.py:421
  5.8 18.2 %copy-start.4 = (f32[4,32,1440]{2,1,0:T(8,128)S(1)}, f32[4,32,1440]{2,1,0:T(8,128)}, u32[]{:S(2)}) copy-start(f32[4,32,1440]{2,1,0:T(8,128)} %u_ref.1) | copy-start | bytes 2211844
  7.1 16.8 %copy-start.1 = (f32[4,32,1440]{2,1,0:T(8,128)S(1)}, f32[4,32,1440]{2,1,0:T(8,128)}, u32[]{:S(2)}) copy-start(f32[4,32,1440]{2,1,0:T(8,128)} %refs_5_.3) | copy-start | bytes 2211844
  7.1 20.9 %collective-permute-start.5 = (f32[3,360,128]{2,1,0:T(8,128)S(1)}, f32[3,360,128]{2,1,0:T(8,128)S(1)}, u32[]{:S(2)}, u32[]{:S(2)}) collective-permute-start(f32[3,360,128]{2,1,0:T(8,128)S(1)} %shard_map.111), channel_id=1, source_target_pairs={{1,2},{3,4},{5,6},{7,8},{9,10},{11,12},{13,14},{2,1},{4,3},{6,5},{... | collective-permute-start | bytes 1658888 | tf_op jit(solution)/shard_map/ppermute | solution.py:421
  9.8 1.2 %collective-permute-start = (f32[32,128]{1,0:T(8,128)S(1)}, f32[32,128]{1,0:T(8,128)S(1)}, u32[]{:S(2)}, u32[]{:S(2)}) collective-permute-start(f32[32,128]{1,0:T(8,128)S(1)} %get-tuple-element.16), channel_id=1, source_target_pairs={{0,1},{1,0},{2,3},{3,2},{4,5},{5,4},{6,7},{7,6},{8,9},{9,8},{10,11... | collective-permute-start | bytes 49160 | tf_op jit(solution)/shard_map/ppermute | solution.py:421
  11.0 10.5 %collective-permute-start.3 = (f32[32,128]{1,0:T(8,128)S(1)}, f32[32,128]{1,0:T(8,128)S(1)}, u32[]{:S(2)}, u32[]{:S(2)}) collective-permute-start(f32[32,128]{1,0:T(8,128)S(1)} %add.15), channel_id=1, source_target_pairs={{0,12},{1,13},{2,14},{3,15},{4,8},{5,9},{6,10},{7,11},{8,4},{9,5},... | collective-permute-start | bytes 49160 | tf_op jit(solution)/shard_map/ppermute | solution.py:421
  14.5 7.0 %collective-permute-start.2 = (f32[32,128]{1,0:T(8,128)S(1)}, f32[32,128]{1,0:T(8,128)S(1)}, u32[]{:S(2)}, u32[]{:S(2)}) collective-permute-start(f32[32,128]{1,0:T(8,128)S(1)} %add.15), channel_id=1, source_target_pairs={{0,8},{1,9},{2,10},{3,11},{4,12},{5,13},{6,14},{7,15},{8,0},{9,1},... | collective-permute-start | bytes 49160 | tf_op jit(solution)/shard_map/ppermute | solution.py:421
  14.5 7.0 %collective-permute-start.1 = (f32[32,128]{1,0:T(8,128)S(1)}, f32[32,128]{1,0:T(8,128)S(1)}, u32[]{:S(2)}, u32[]{:S(2)}) collective-permute-start(f32[32,128]{1,0:T(8,128)S(1)} %add.15), channel_id=1, source_target_pairs={{0,4},{1,5},{2,6},{3,7},{4,0},{5,1},{6,2},{7,3},{8,12},{9,13},{10,... | collective-permute-start | bytes 49160 | tf_op jit(solution)/shard_map/ppermute | solution.py:421
  21.5 3.9 %collective-permute-start.4 = (f32[32,128]{1,0:T(8,128)S(1)}, f32[32,128]{1,0:T(8,128)S(1)}, u32[]{:S(2)}, u32[]{:S(2)}) collective-permute-start(f32[32,128]{1,0:T(8,128)S(1)} %add_add_fusion), channel_id=1, source_target_pairs={{0,2},{1,3},{2,0},{3,1},{4,6},{5,7},{6,4},{7,5},{8,10},{9,11},{10,... | collective-permute-start | bytes 49160 | tf_op jit(solution)/shard_map/ppermute | solution.py:421
  24.0 1.4 %copy-start.3 = (f32[4,32,1440]{2,1,0:T(8,128)S(1)}, f32[4,32,1440]{2,1,0:T(8,128)}, u32[]{:S(2)}) copy-start(f32[4,32,1440]{2,1,0:T(8,128)} %refs_6_.1) | copy-start | bytes 2211844
  24.0 1.4 %copy-start.8 = (f32[64]{0:T(128)S(1)}, f32[64]{0:T(128)}, u32[]{:S(2)}) copy-start(f32[64]{0:T(128)} %constant.8.clone.cos_ref.refs_0_) | copy-start | bytes 772
  24.0 1.4 %copy-start.9 = (s32[64]{0:T(128)S(1)}, s32[64]{0:T(128)}, u32[]{:S(2)}) copy-start(s32[64]{0:T(128)} %refs_2_.3) | copy-start | bytes 772
  24.0 1.4 %copy-start.10 = (s32[64]{0:T(128)S(1)}, s32[64]{0:T(128)}, u32[]{:S(2)}) copy-start(s32[64]{0:T(128)} %refs_3_.3) | copy-start | bytes 772
  24.0 1.4 %copy-start.11 = (f32[65]{0:T(128)S(1)}, f32[65]{0:T(128)}, u32[]{:S(2)}) copy-start(f32[65]{0:T(128)} %constant.9.clone.refs_1_) | copy-start | bytes 784

commit v9 on v8

--- a/solution.py
+++ b/solution.py
@@ -109,26 +109,40 @@
     return jnp.where(upper, rows - 2, 1), jnp.where(upper, rows - 1, 0)
 
 
-def pack_kernel(h_ref, v_ref, out_ref, edge_ref, sem):
-    far, near = edge_rows(lax.axis_index("lat") % 2 == 1, h_ref.shape[0])
-    copies = [
-        pltpu.make_async_copy(ref.at[row], edge_ref.at[i], sem.at[i])
-        for i, (ref, row) in enumerate([(h_ref, far), (h_ref, near), (v_ref, near)])
-    ]
+def pack_kernel(
+    h_ref, v_ref, cos_ref, flags_ref, cutoffs_ref, out_ref, about_ref, edge_ref, cos, flags, cutoffs, sem
+):
+    rows = h_ref.shape[0]
+    nlat = flags_ref.shape[0]
+    position = lax.axis_index("lat")
+    first = position * rows
+    far, near = edge_rows(position % 2 == 1, rows)
+    moves = [(h_ref.at[far], edge_ref.at[0]), (h_ref.at[near], edge_ref.at[1]), (v_ref.at[near], edge_ref.at[2])]
+    moves += [(cos_ref, cos), (flags_ref, flags), (cutoffs_ref, cutoffs)]
+    copies = [pltpu.make_async_copy(source, target, sem.at[i]) for i, (source, target) in enumerate(moves)]
     for c in copies:
         c.start()
-    for c in copies:
+    for c in copies[3:]:
+        c.wait()
+    flat = (8, LANES)
+    for j in range(rows):
+        about_ref[j] = 1.0 / jnp.full(flat, cos[first + j])
+        about_ref[rows + j] = jnp.full(flat, flags[first + j].astype(jnp.float32))
+        about_ref[2 * rows + j] = jnp.full(flat, cutoffs[first + j].astype(jnp.float32))
+        about_ref[3 * rows + j] = jnp.full(flat, cos[first + j])
+    for f in range(rows + 1):
+        about_ref[4 * rows + f] = jnp.full(flat, cos[nlat + first + f] * (0.5 / 12.0))
+    for c in copies[:3]:
         c.wait()
     for i in range(3):
         pack_row(edge_ref[i], out_ref, i)
 
 
-def source_kernel(cos_ref, rates_ref, thresholds_ref, h_ref, v_ref, edge_ref, sum_ref, out_ref):
+def source_kernel(about_ref, rates_ref, thresholds_ref, h_ref, v_ref, edge_ref, sum_ref, out_ref):
     rows, levels, nlon = h_ref.shape
     full = round_up(nlon, LANES)
     base = base_of(nlon)
     position = lax.axis_index("lat")
-    first = position * rows
     rates = column(rates_ref[...])
     thresholds = column(thresholds_ref[...])
     total = jnp.zeros((levels, LANES), jnp.float32)
@@ -142,7 +156,8 @@
             acc = acc + jnp.concatenate(
                 [s[:, base:], jnp.zeros((levels, full - nlon), jnp.float32)], axis=1
             )
-        total = total + acc * cos_ref[first + j]
+        weight = about_ref[3 * rows + j]
+        total = total + acc * jnp.concatenate([weight] * (levels // 8), axis=0)
     total = jnp.broadcast_to(jnp.sum(total, axis=1, keepdims=True), (levels, LANES))
     sum_ref[...] = total
     far, near = edge_rows(position % 2 == 0, rows)
@@ -218,15 +233,13 @@
 
 
 class Side:
-    def __init__(self, lower, scalars, arrays):
-        self.cos_row_ref, self.cos_face_ref, self.flags_ref, self.cutoffs_ref = scalars
+    def __init__(self, lower, about_ref, arrays):
+        self.about_ref = about_ref
         self.h_ref, self.v_ref, self.part_ref = arrays
         self.rows, self.levels, self.nlon = self.h_ref.shape
         self.full = round_up(self.nlon, LANES)
         self.lower = lower
-        position = lax.axis_index("lat")
-        self.first = position * self.rows
-        self.outermost = position == jnp.where(lower, 0, lax.axis_size("lat") - 1)
+        self.outermost = lax.axis_index("lat") == jnp.where(lower, 0, lax.axis_size("lat") - 1)
 
     def row(self, i):
         return jnp.where(self.lower, i, self.rows - 1 - i)
@@ -236,22 +249,16 @@
             yield k, slice(8 * g, 8 * g + 8), slice(k * LANES, min((k + 1) * LANES, self.nlon))
 
     def any_marked(self):
-        marked = self.flags_ref[self.first]
+        marked = self.about_ref[self.rows]
         for j in range(1, self.rows):
-            marked = jnp.maximum(marked, self.flags_ref[self.first + j])
-        return marked > 0
-
-    def kept(self, i):
-        row = self.first + self.row(i)
-        cut = jnp.full((8, LANES), self.cutoffs_ref[row].astype(jnp.float32))
-        return jnp.where(self.flags_ref[row] > 0, jnp.minimum(1.0, cut * cut), 1.0)
+            marked = jnp.maximum(marked, self.about_ref[self.rows + j])
+        return marked[0, 0] > 0
 
     def update(self, count, halo_tile, out_ref):
         sign = jnp.where(self.lower, 1.0, -1.0)
-        scale = [sign / jnp.full((8, LANES), self.cos_row_ref[self.first + self.row(i)]) for i in range(count)]
+        scale = [self.about_ref[self.row(i)] * sign for i in range(count)]
         face_cos = [
-            self.cos_face_ref[self.first + jnp.where(self.lower, i, self.rows - i)] * (0.5 / 12.0)
-            for i in range(count + 1)
+            self.about_ref[4 * self.rows + jnp.where(self.lower, i, self.rows - i)] for i in range(count + 1)
         ]
         for g in range(self.levels // 8):
             for k, at, lanes in self.tiles(g):
@@ -262,7 +269,7 @@
                 flux = []
                 for f in range(count + 1):
                     p = 7.0 * (height[f + 1] + height[f + 2]) - (height[f] + height[f + 3])
-                    flux.append((speed[f] + speed[f + 1]) * face_cos[f] * p)
+                    flux.append((speed[f] + speed[f + 1]) * face_cos[f][:, :wide] * p)
                 for i in range(count):
                     div = (flux[i + 1] - flux[i]) * scale[i][:, :wide]
                     out_ref[i, at, lanes] = self.part_ref[self.row(i), at, lanes] - div
@@ -290,10 +297,10 @@
             inverse = 1.0 / jnp.maximum(waves, 1).astype(jnp.float32)
             factors = []
             for j in range(count):
-                row = self.first + self.row(j)
-                ratio = self.cutoffs_ref[row].astype(jnp.float32) * inverse
+                row = self.rows + self.row(j)
+                ratio = self.about_ref[self.rows + row][:, :1] * inverse
                 factor = (1.0 - jnp.minimum(1.0, ratio * ratio)) * weight
-                factor = jnp.where(self.flags_ref[row] > 0, factor, 0.0)
+                factor = jnp.where(self.about_ref[row][:, :1] > 0, factor, 0.0)
                 factors.append(jnp.concatenate([factor, factor], axis=1))
             for c in range(0, cols, chunk):
                 spectrum = products(y_ref.at[parity], high_ref, low_ref, c, chunk, units)
@@ -309,6 +316,11 @@
                 x, y = even[r : r + 16], uneven[r : r + 16]
                 out_ref[j, q : q + 16, c : c + chunk] -= x + y
                 d_ref[r : r + 16, c : c + chunk] = x - y
+        start = half // LANES * LANES
+        for r in range(0, units, 8):
+            j, q = divmod(r, levels)
+            d = jnp.concatenate([d_ref[r : r + 8, :], jnp.zeros((8, full - depth), jnp.float32)], axis=1)
+            out_ref[j, q : q + 8, start:] -= pltpu.roll(d, half, 1)[:, start:nlon]
 
 
 def put_parts(ref, parity, r, units, lanes, y):
@@ -317,83 +329,48 @@
     ref[parity, units + r : units + r + 16, lanes] = (y - high.astype(jnp.float32)).astype(jnp.bfloat16)
 
 
-def near_kernel(*refs):
-    scalars, arrays, a_ref, tables = refs[:4], refs[4:7], refs[7], refs[8:16]
-    out_ref, y_ref, s_ref, d_ref = refs[16:]
-    side = Side(lax.axis_index("lat") % 2 == 1, scalars, arrays)
+def near_kernel(about_ref, h_ref, v_ref, part_ref, a_ref, *refs):
+    tables, out_ref, scratch = refs[:8], refs[8], refs[9:]
+    side = Side(lax.axis_index("lat") % 2 == 1, about_ref, (h_ref, v_ref, part_ref))
     count = out_ref.shape[0]
 
     def halo_tile(i, g, k):
         return a_ref[i, 8 * g : 8 * g + 8, k * LANES : min((k + 1) * LANES, side.nlon)]
 
     side.update(count, halo_tile, out_ref)
-
-    @pl.when(side.any_marked())
-    def _():
-        side.filter(count, tables, y_ref, s_ref, d_ref, out_ref)
-        start = side.nlon // 2 // LANES * LANES
-        for r in range(0, count * side.levels, 8):
-            j, q = divmod(r, side.levels)
-            out_ref[j, q : q + 8, start:] -= shifted(d_ref, r, side)[:, start:]
-
-
-def shifted(d_ref, r, side):
-    depth = d_ref.shape[1]
-    d = jnp.concatenate([d_ref[r : r + 8, :], jnp.zeros((8, side.full - depth), jnp.float32)], axis=1)
-    return pltpu.roll(d, side.nlon // 2, 1)[:, : side.nlon]
-
-
-def finish_kernel(*refs):
-    scalars, sums_ref, arrays, b_ref, done_ref, tables = refs[:4], refs[4], refs[5:8], refs[8], refs[9], refs[10:18]
-    result_ref, out_ref, y_ref, s_ref, d_ref, sem = refs[18:]
+    pl.when(side.any_marked())(lambda: side.filter(count, tables, *scratch, out_ref))
+
+
+def far_kernel(about_ref, h_ref, v_ref, part_ref, b_ref, *refs):
+    tables, out_ref, scratch = refs[:8], refs[8], refs[9:]
+    side = Side(lax.axis_index("lat") % 2 == 0, about_ref, (h_ref, v_ref, part_ref))
+    count = out_ref.shape[0]
+    side.update(count, lambda i, g, k: packed_tile(b_ref, i, g, k, side.levels, side.nlon), out_ref)
+    pl.when(side.any_marked())(lambda: side.filter(count, tables, *scratch, out_ref))
+
+
+def mean_kernel(nlat, about_ref, sums_ref, near_ref, far_ref, out_ref, row_ref, sem):
+    rows, levels, nlon = row_ref.shape
     odd = lax.axis_index("lat") % 2 == 1
-    side, other = Side(odd == False, scalars, arrays), Side(odd, scalars, arrays)
-    levels, nlon = side.levels, side.nlon
-    done = done_ref.shape[0]
-    count = side.rows - done
-    nlat = scalars[0].shape[0]
     area = nlon * float(np.sum(np.sin(np.pi * (np.arange(nlat) + 0.5) / nlat)))
-    mean = sums_ref[:, :LANES] * (1.0 / area)
-    sends = []
-
-    def send(view, i):
-        n = len(sends)
-        sends.append(pltpu.make_async_copy(out_ref.at[n], result_ref.at[view.row(i)], sem.at[n]))
-        sends[-1].start()
-
-    for i in range(done):
-        kept = other.kept(i)
+    mean = sums_ref[...] * (1.0 / area)
+    done = near_ref.shape[0]
+    copies = []
+    for i in range(rows):
+        ref, k, lower = (near_ref, i, odd) if i < done else (far_ref, i - done, odd == False)
+        row = jnp.where(lower, k, rows - 1 - k)
+        cut = about_ref[2 * rows + row]
+        kept = jnp.where(about_ref[rows + row] > 0, jnp.minimum(1.0, cut * cut), 1.0)
         for g in range(levels // 8):
-            for _, at, lanes in side.tiles(g):
-                shift = (mean[at] * kept)[:, : lanes.stop - lanes.start]
-                out_ref[i, at, lanes] = done_ref[i, at, lanes] - shift
-        send(other, i)
-
-    new_ref = out_ref.at[pl.ds(done, count)]
-    side.update(count, lambda i, g, k: packed_tile(b_ref, i, g, k, levels, nlon), new_ref)
-    marked = side.any_marked()
-
-    @pl.when(marked)
-    def _():
-        side.filter(count, tables, y_ref, s_ref, d_ref, new_ref)
-
-    @pl.when(marked == False)
-    def _():
-        d_ref[...] = jnp.zeros_like(d_ref)
-
-    start = nlon // 2 // LANES * LANES
-    for i in range(count):
-        kept = side.kept(i)
-        for g in range(levels // 8):
-            d = shifted(d_ref, i * levels + 8 * g, side)
-            for _, at, lanes in side.tiles(g):
-                less = (mean[at] * kept)[:, : lanes.stop - lanes.start]
-                if lanes.start >= start:
-                    less = less + d[:, lanes]
-                new_ref[i, at, lanes] -= less
-        send(side, i)
-    for copy in sends:
-        copy.wait()
+            at = slice(8 * g, 8 * g + 8)
+            shift = mean[at] * kept
+            for t in range(0, nlon, LANES):
+                lanes = slice(t, min(t + LANES, nlon))
+                row_ref[i, at, lanes] = ref[k, at, lanes] - shift[:, : lanes.stop - lanes.start]
+        copies.append(pltpu.make_async_copy(row_ref.at[i], out_ref.at[row], sem.at[i]))
+        copies[-1].start()
+    for c in copies:
+        c.wait()
 
 
 def products(y_ref, high_ref, low_ref, c, chunk, units):
@@ -426,7 +403,7 @@
     count = lax.axis_size("lat")
     nlat = rows * count
     half = nlon // 2
-    smem, vmem, hbm = pltpu.SMEM, pltpu.VMEM, pltpu.HBM
+    vmem, hbm = pltpu.VMEM, pltpu.HBM
     f32 = jnp.float32
 
     between = [(i, i + 1) for i in range(1, count - 1, 2)]
@@ -439,25 +416,31 @@
         between += [(p * count + e, (p ^ 1) * count + e) for p in range(parts) for e in ends]
     within = within + [(j, i) for i, j in within]
     whole, _, extra = dense_tiles(levels, nlon)
-    (edge_b,) = call(
+    faces = np.sin(np.pi * np.arange(nlat + 1) / nlat)
+    faces[0] = faces[nlat] = 0.0
+    cosines = np.concatenate([np.sin(np.pi * (np.arange(nlat) + 0.5) / nlat), faces])
+    cosines = jnp.asarray(cosines.astype(np.float32))
+    edge_b, about = call(
         pack_kernel,
         [
-            (pltpu.with_memory_space_constraint(height, hbm), hbm),
-            (pltpu.with_memory_space_constraint(merid_courant, hbm), hbm),
+            (pltpu.with_memory_space_constraint(x, hbm), hbm)
+            for x in (height, merid_courant, cosines, flags, cutoffs)
         ],
-        [((3, 8 * (whole + extra), LANES), f32)],
+        [((3, 8 * (whole + extra), LANES), f32), ((5 * rows + 1, 8, LANES), f32)],
         4,
-        [pltpu.VMEM((3, levels, nlon), f32), pltpu.SemaphoreType.DMA((3,))],
+        [
+            pltpu.VMEM((3, levels, nlon), f32),
+            pltpu.SMEM(cosines.shape, f32),
+            pltpu.SMEM(flags.shape, jnp.int32),
+            pltpu.SMEM(cutoffs.shape, jnp.int32),
+            pltpu.SemaphoreType.DMA((6,)),
+        ],
     )
     b = permute(edge_b, between, ("member", "lat"))
 
-    cos_row = jnp.asarray(np.sin(np.pi * (np.arange(nlat) + 0.5) / nlat).astype(np.float32))
-    faces = np.sin(np.pi * np.arange(nlat + 1) / nlat)
-    faces[0] = faces[nlat] = 0.0
-    cos_face = jnp.asarray(faces.astype(np.float32))
     edge_a, sums, source = call(
         source_kernel,
-        [(cos_row, smem), (rates[None], vmem), (thresholds[None], vmem), (height, vmem), (merid_courant, vmem)],
+        [(x, vmem) for x in (about, rates[None], thresholds[None], height, merid_courant)],
         [((3, levels, nlon), f32), ((levels, LANES), f32), (height.shape, f32)],
         8,
     )
@@ -483,25 +466,27 @@
     else:
         sums = lax.psum(sums, "lat")
 
-    scalars = [(x, smem) for x in (cos_row, cos_face, flags, cutoffs)]
-    arrays = [(x, vmem) for x in (height, merid_courant, part)]
-    held = [(x, vmem) for x in tables]
-
-    def scratch(rows):
-        return [
-            pltpu.VMEM((2, 2 * rows * levels, depth), jnp.bfloat16),
-            pltpu.VMEM((2, 2 * rows * levels, cols), jnp.bfloat16),
-            pltpu.VMEM((rows * levels, depth), f32),
-        ]
-
-    done = rows - 2
-    (near,) = call(near_kernel, [*scalars, *arrays, (a, vmem), *held], [((done, levels, nlon), f32)], 16, scratch(done))
+    def rows_of(kernel, edge, rows):
+        return call(
+            kernel,
+            [(x, vmem) for x in (about, height, merid_courant, part, edge, *tables)],
+            [((rows, levels, nlon), f32)],
+            16,
+            [
+                pltpu.VMEM((2, 2 * rows * levels, depth), jnp.bfloat16),
+                pltpu.VMEM((2, 2 * rows * levels, cols), jnp.bfloat16),
+                pltpu.VMEM((rows * levels, depth), f32),
+            ],
+        )[0]
+
+    near = rows_of(near_kernel, a, rows - 2)
+    far = rows_of(far_kernel, b, 2)
     (out,) = call(
-        finish_kernel,
-        [*scalars, (sums, vmem), *arrays, (b, vmem), (near, vmem), *held],
+        functools.partial(mean_kernel, nlat),
+        [(x, vmem) for x in (about, sums, near, far)],
         [(height.shape, f32)],
-        16,
-        [pltpu.VMEM(height.shape, f32), *scratch(2), pltpu.SemaphoreType.DMA((rows,))],
+        4,
+        [pltpu.VMEM(height.shape, f32), pltpu.SemaphoreType.DMA((rows,))],
         hbm,
     )
     return out

time: 31.7 us -> 25.9 us (0.82)
  local copies, waits for them, and re-layouts: 4.28 us -> 0.23 us
  Pallas kernels: 12 us -> 10.5 us
    unnamed x28 -> x14, local copies, waits for them, and re-layouts: 4.28 us -> 0.23 us
    pallas_call x7 -> x8, Pallas kernels: 12 us -> 10.5 us  [call(): pl.pallas_call(kernel, in_specs=[pl.BlockSpec(memory_space=space) for _,...]
  transfers between devices with their start and end apart: 7 -> 7, of which waited for: 2 -> 2; matrix products, arithmetic and copies ran while one was open for 0% -> 0% of each run, Pallas kernels for 24% -> 22%
where the time goes in v9:
time: 25.9 us; the launch traced here: 25.7 us
  Pallas kernels  10.5 us (41%)
  starting transfers between devices  7.67 us (30%)
  waiting for transfers between devices  7.19 us (28%)
    pallas_call x8, Pallas kernels, call(): pl.pallas_call(kernel, in_specs=[pl.BlockSpec(memory_space=space) for _,...  10.5 us
    ppermute x7, starting transfers between devices, permute(): return lax.ppermute(x, axes, pairs)  7.67 us
    ppermute x7, waiting for transfers between devices, permute(): return lax.ppermute(x, axes, pairs)  7.19 us
  transfers between devices with their start and end apart: 7, of which 2 were waited for; matrix products, arithmetic and copies ran while one was open for 0% of the time, Pallas kernels for 22%

profile of v9, /device:TPU:0, one launch (start us, length us, event | category | flops | bytes accessed | tf_op | source)
XLA Modules:
  0.0 25.7 jit_solution(8251495551401074070)
XLA Ops:
  0.0 0.0 copy-start
  0.0 0.0 copy-start.1
  0.0 0.0 copy-start.6
  0.0 0.0 copy-start.5
  0.0 1.4 %shard_map.100 = (f32[3,360,128]{2,1,0:T(8,128)S(1)}, f32[21,8,128]{2,1,0:T(8,128)S(1)}) custom-call(f32[4,32,1440]{2,1,0:T(8,128)} %h_ref.9, f32[4,32,1440]{2,1,0:T(8,128)} %v_ref.7, f32[129]{0:T(256)} %constant.6.clone.cos_ref, s32[64]{0:T(128)} %flags_ref.1, s32[64]{0:T(128)} %cutoffs_ref.1), custom_call_target="tpu_custom_call" | custom-call | tf_op jit(solution)/shard_map/pallas_call | solution.py:387
  1.4 0.0 copy-start.4
  1.4 0.0 copy-done
  1.4 0.2 copy-done.1
  1.7 0.0 copy-done.6
  1.7 0.0 copy-done.5
  1.7 0.0 copy-start.3
  1.7 0.0 copy-start.2
  1.7 0.5 %shard_map.101 = (f32[3,32,1440]{2,1,0:T(8,128)S(1)}, f32[32,128]{1,0:T(8,128)S(1)}, f32[4,32,1440]{2,1,0:T(8,128)S(1)}) custom-call(f32[21,8,128]{2,1,0:T(8,128)S(1)} %get-tuple-element.18.about_ref, f32[1,32]{1,0:T(1,128)S(1)} %bitcast.2, f32[1,32]{1,0:T(1,128)S(1)} %bitcast.3, f32[4,32,1440]{2,1,0:T(8,128)S(1)} %copy-done, f32[4,32,1440]{2,1,0:T(8,128)S(1)} %copy-done.1), custom_call_target="tpu_custom_call" | custom-call | tf_op jit(solution)/shard_map/pallas_call | solution.py:387
  2.2 0.5 %collective-permute-start.5 = (f32[3,32,1440]{2,1,0:T(8,128)S(1)}, f32[3,32,1440]{2,1,0:T(8,128)S(1)}, u32[]{:S(2)}, u32[]{:S(2)}) collective-permute-start(f32[3,32,1440]{2,1,0:T(8,128)S(1)} %get-tuple-element.21), channel_id=1, source_target_pairs={{0,1},{2,3},{4,5},{6,7},{8,9},{10,11},{12,13},{14,15},{1,0},{3,2},... | collective-permute-start | bytes 1658888 | tf_op jit(solution)/shard_map/ppermute | solution.py:398
  2.7 2.6 %collective-permute-start.6 = (f32[3,360,128]{2,1,0:T(8,128)S(1)}, f32[3,360,128]{2,1,0:T(8,128)S(1)}, u32[]{:S(2)}, u32[]{:S(2)}) collective-permute-start(f32[3,360,128]{2,1,0:T(8,128)S(1)} %get-tuple-element.30), channel_id=1, source_target_pairs={{1,2},{3,4},{5,6},{7,8},{9,10},{11,12},{13,14},{2,1},{4,3},{6,5},{... | collective-permute-start | bytes 1658888 | tf_op jit(solution)/shard_map/ppermute | solution.py:398
  5.2 0.1 collective-permute-start
  5.4 1.0 %collective-permute-done = f32[32,128]{1,0:T(8,128)S(1)} collective-permute-done((f32[32,128]{1,0:T(8,128)S(1)}, f32[32,128]{1,0:T(8,128)S(1)}, u32[]{:S(2)}, u32[]{:S(2)}) %collective-permute-start) | collective-permute-done | bytes 16416 | tf_op jit(solution)/shard_map/ppermute | solution.py:398
  6.4 3.6 %collective-permute-start.3 = (f32[32,128]{1,0:T(8,128)S(1)}, f32[32,128]{1,0:T(8,128)S(1)}, u32[]{:S(2)}, u32[]{:S(2)}) collective-permute-start(f32[32,128]{1,0:T(8,128)S(1)} %add.15), channel_id=1, source_target_pairs={{0,12},{1,13},{2,14},{3,15},{4,8},{5,9},{6,10},{7,11},{8,4},{9,5},... | collective-permute-start | bytes 49160 | tf_op jit(solution)/shard_map/ppermute | solution.py:398
  10.0 0.0 collective-permute-start.2
  10.0 0.8 %collective-permute-start.1 = (f32[32,128]{1,0:T(8,128)S(1)}, f32[32,128]{1,0:T(8,128)S(1)}, u32[]{:S(2)}, u32[]{:S(2)}) collective-permute-start(f32[32,128]{1,0:T(8,128)S(1)} %add.15), channel_id=1, source_target_pairs={{0,4},{1,5},{2,6},{3,7},{4,0},{5,1},{6,2},{7,3},{8,12},{9,13},{10,... | collective-permute-start | bytes 49160 | tf_op jit(solution)/shard_map/ppermute | solution.py:398
  10.8 6.1 %collective-permute-done.3 = f32[32,128]{1,0:T(8,128)S(1)} collective-permute-done((f32[32,128]{1,0:T(8,128)S(1)}, f32[32,128]{1,0:T(8,128)S(1)}, u32[]{:S(2)}, u32[]{:S(2)}) %collective-permute-start.3) | collective-permute-done | bytes 16416 | tf_op jit(solution)/shard_map/ppermute | solution.py:398
  17.0 0.0 collective-permute-done.2
  17.0 0.0 collective-permute-done.1
  17.0 0.1 collective-permute-start.4
  17.1 0.0 copy-done.4
  17.1 1.2 %shard_map.103 = (bf16[768,768]{1,0:T(8,128)(2,1)S(1)}, bf16[768,768]{1,0:T(8,128)(2,1)S(1)}, bf16[768,768]{1,0:T(8,128)(2,1)S(1)}, bf16[768,768]{1,0:T(8,128)(2,1)S(1)}) custom-call(f32[216,768]{1,0:T(8,128)S(1)} %copy-done.4), custom_call_target="tpu_custom_call" | custom-call | tf_op jit(solution)/shard_map/pallas_call | solution.py:387
  18.2 0.0 copy-done.3
  18.3 1.2 %shard_map.104 = (bf16[768,768]{1,0:T(8,128)(2,1)S(1)}, bf16[768,768]{1,0:T(8,128)(2,1)S(1)}, bf16[768,768]{1,0:T(8,128)(2,1)S(1)}, bf16[768,768]{1,0:T(8,128)(2,1)S(1)}) custom-call(f32[216,768]{1,0:T(8,128)S(1)} %copy-done.3), custom_call_target="tpu_custom_call" | custom-call | tf_op jit(solution)/shard_map/pallas_call | solution.py:387
  19.4 0.0 copy-done.2
  19.4 1.4 %shard_map.102.part_ref = f32[4,32,1440]{2,1,0:T(8,128)S(1)} custom-call(f32[4,32,1440]{2,1,0:T(8,128)S(1)} %copy-done, f32[4,32,1440]{2,1,0:T(8,128)S(1)} %copy-done.2, f32[4,32,1440]{2,1,0:T(8,128)S(1)} %get-tuple-element.20.s_ref), custom_call_target="tpu_custom_call" | custom-call | tf_op jit(solution)/shard_map/pallas_call | solution.py:387
  20.8 0.0 collective-permute-done.4
  20.8 0.0 collective-permute-done.5.a_ref
  20.8 2.0 %shard_map.105.near_ref = f32[2,32,1440]{2,1,0:T(8,128)S(1)} custom-call(f32[21,8,128]{2,1,0:T(8,128)S(1)} %get-tuple-element.18.about_ref, f32[4,32,1440]{2,1,0:T(8,128)S(1)} %copy-done, f32[4,32,1440]{2,1,0:T(8,128)S(1)} %copy-done.1, f32[4,32,1440]{2,1,0:T(8,128)S(1)} %shard_map.102.part_ref, f32[3,32,1440]{2,1,0:T(8,128)S(1)} %collective-permute-done.5.a_ref, ...), custom_call_target="tpu_custom_call" | custom-call | tf_op jit(solution)/shard_map/pallas_call | solution.py:387
  22.8 0.0 collective-permute-done.6.b_ref
  22.8 2.0 %shard_map.106.far_ref = f32[2,32,1440]{2,1,0:T(8,128)S(1)} custom-call(f32[21,8,128]{2,1,0:T(8,128)S(1)} %get-tuple-element.18.about_ref, f32[4,32,1440]{2,1,0:T(8,128)S(1)} %copy-done, f32[4,32,1440]{2,1,0:T(8,128)S(1)} %copy-done.1, f32[4,32,1440]{2,1,0:T(8,128)S(1)} %shard_map.102.part_ref, f32[3,360,128]{2,1,0:T(8,128)S(1)} %collective-permute-done.6.b_ref, ...), custom_call_target="tpu_custom_call" | custom-call | tf_op jit(solution)/shard_map/pallas_call | solution.py:387
  24.8 0.9 %shard_map.107 = f32[4,32,1440]{2,1,0:T(8,128)} custom-call(f32[21,8,128]{2,1,0:T(8,128)S(1)} %get-tuple-element.18.about_ref, f32[32,128]{1,0:T(8,128)S(1)} %add.19.sums_ref, f32[2,32,1440]{2,1,0:T(8,128)S(1)} %shard_map.105.near_ref, f32[2,32,1440]{2,1,0:T(8,128)S(1)} %shard_map.106.far_ref), custom_call_target="tpu_custom_call" | custom-call | tf_op jit(solution)/shard_map/pallas_call | solution.py:387
  (3 shorter events, 0.0 us)
Async XLA Ops:
  0.0 1.4 %copy-start = (f32[4,32,1440]{2,1,0:T(8,128)S(1)}, f32[4,32,1440]{2,1,0:T(8,128)}, u32[]{:S(2)}) copy-start(f32[4,32,1440]{2,1,0:T(8,128)} %h_ref.9) | copy-start | bytes 2211844
  0.0 1.6 %copy-start.1 = (f32[4,32,1440]{2,1,0:T(8,128)S(1)}, f32[4,32,1440]{2,1,0:T(8,128)}, u32[]{:S(2)}) copy-start(f32[4,32,1440]{2,1,0:T(8,128)} %v_ref.7) | copy-start | bytes 2211844
  0.0 1.6 %copy-start.6 = (f32[32]{0:T(128)S(1)}, f32[32]{0:T(128)}, u32[]{:S(2)}) copy-start(f32[32]{0:T(128)} %param.14) | copy-start | bytes 388
  0.0 1.6 %copy-start.5 = (f32[32]{0:T(128)S(1)}, f32[32]{0:T(128)}, u32[]{:S(2)}) copy-start(f32[32]{0:T(128)} %param.13) | copy-start | bytes 388
  1.4 15.6 %copy-start.4 = (f32[216,768]{1,0:T(8,128)S(1)}, f32[216,768]{1,0:T(8,128)}, u32[]{:S(2)}) copy-start(f32[216,768]{1,0:T(8,128)} %constant.7.clone.source_ref) | copy-start | bytes 1990660
  1.7 16.6 %copy-start.3 = (f32[216,768]{1,0:T(8,128)S(1)}, f32[216,768]{1,0:T(8,128)}, u32[]{:S(2)}) copy-start(f32[216,768]{1,0:T(8,128)} %constant.8.clone.source_ref) | copy-start | bytes 1990660
  1.7 17.8 %copy-start.2 = (f32[4,32,1440]{2,1,0:T(8,128)S(1)}, f32[4,32,1440]{2,1,0:T(8,128)}, u32[]{:S(2)}) copy-start(f32[4,32,1440]{2,1,0:T(8,128)} %u_ref.1) | copy-start | bytes 2211844
  2.2 18.7 %collective-permute-start.5 = (f32[3,32,1440]{2,1,0:T(8,128)S(1)}, f32[3,32,1440]{2,1,0:T(8,128)S(1)}, u32[]{:S(2)}, u32[]{:S(2)}) collective-permute-start(f32[3,32,1440]{2,1,0:T(8,128)S(1)} %get-tuple-element.21), channel_id=1, source_target_pairs={{0,1},{2,3},{4,5},{6,7},{8,9},{10,11},{12,13},{14,15},{1,0},{3,2},... | collective-permute-start | bytes 1658888 | tf_op jit(solution)/shard_map/ppermute | solution.py:398
  2.7 20.1 %collective-permute-start.6 = (f32[3,360,128]{2,1,0:T(8,128)S(1)}, f32[3,360,128]{2,1,0:T(8,128)S(1)}, u32[]{:S(2)}, u32[]{:S(2)}) collective-permute-start(f32[3,360,128]{2,1,0:T(8,128)S(1)} %get-tuple-element.30), channel_id=1, source_target_pairs={{1,2},{3,4},{5,6},{7,8},{9,10},{11,12},{13,14},{2,1},{4,3},{6,5},{... | collective-permute-start | bytes 1658888 | tf_op jit(solution)/shard_map/ppermute | solution.py:398
  5.2 1.2 %collective-permute-start = (f32[32,128]{1,0:T(8,128)S(1)}, f32[32,128]{1,0:T(8,128)S(1)}, u32[]{:S(2)}, u32[]{:S(2)}) collective-permute-start(f32[32,128]{1,0:T(8,128)S(1)} %get-tuple-element.19), channel_id=1, source_target_pairs={{0,1},{1,0},{2,3},{3,2},{4,5},{5,4},{6,7},{7,6},{8,9},{9,8},{10,11... | collective-permute-start | bytes 49160 | tf_op jit(solution)/shard_map/ppermute | solution.py:398
  6.4 10.5 %collective-permute-start.3 = (f32[32,128]{1,0:T(8,128)S(1)}, f32[32,128]{1,0:T(8,128)S(1)}, u32[]{:S(2)}, u32[]{:S(2)}) collective-permute-start(f32[32,128]{1,0:T(8,128)S(1)} %add.15), channel_id=1, source_target_pairs={{0,12},{1,13},{2,14},{3,15},{4,8},{5,9},{6,10},{7,11},{8,4},{9,5},... | collective-permute-start | bytes 49160 | tf_op jit(solution)/shard_map/ppermute | solution.py:398
  10.0 7.0 %collective-permute-start.2 = (f32[32,128]{1,0:T(8,128)S(1)}, f32[32,128]{1,0:T(8,128)S(1)}, u32[]{:S(2)}, u32[]{:S(2)}) collective-permute-start(f32[32,128]{1,0:T(8,128)S(1)} %add.15), channel_id=1, source_target_pairs={{0,8},{1,9},{2,10},{3,11},{4,12},{5,13},{6,14},{7,15},{8,0},{9,1},... | collective-permute-start | bytes 49160 | tf_op jit(solution)/shard_map/ppermute | solution.py:398
  10.0 7.0 %collective-permute-start.1 = (f32[32,128]{1,0:T(8,128)S(1)}, f32[32,128]{1,0:T(8,128)S(1)}, u32[]{:S(2)}, u32[]{:S(2)}) collective-permute-start(f32[32,128]{1,0:T(8,128)S(1)} %add.15), channel_id=1, source_target_pairs={{0,4},{1,5},{2,6},{3,7},{4,0},{5,1},{6,2},{7,3},{8,12},{9,13},{10,... | collective-permute-start | bytes 49160 | tf_op jit(solution)/shard_map/ppermute | solution.py:398
  17.0 3.8 %collective-permute-start.4 = (f32[32,128]{1,0:T(8,128)S(1)}, f32[32,128]{1,0:T(8,128)S(1)}, u32[]{:S(2)}, u32[]{:S(2)}) collective-permute-start(f32[32,128]{1,0:T(8,128)S(1)} %add_add_fusion), channel_id=1, source_target_pairs={{0,2},{1,3},{2,0},{3,1},{4,6},{5,7},{6,4},{7,5},{8,10},{9,11},{10,... | collective-permute-start | bytes 49160 | tf_op jit(solution)/shard_map/ppermute | solution.py:398

commit v10 on v9

--- a/solution.py
+++ b/solution.py
@@ -57,6 +57,10 @@
     end = pltpu.roll(tail, full - base - rest, 1)
     tail = jnp.where(lane < rest, tail, jnp.where(lane < full - base - 8, head, end))
     return jnp.concatenate([body, tail], axis=1)
+
+
+def diagonal(shape):
+    return lax.broadcasted_iota(jnp.int32, shape, 0) == lax.broadcasted_iota(jnp.int32, shape, 1)
 
 
 def column(row):
@@ -158,8 +162,8 @@
             )
         weight = about_ref[3 * rows + j]
         total = total + acc * jnp.concatenate([weight] * (levels // 8), axis=0)
-    total = jnp.broadcast_to(jnp.sum(total, axis=1, keepdims=True), (levels, LANES))
-    sum_ref[...] = total
+    total = jnp.broadcast_to(jnp.sum(total, axis=1, keepdims=True), (levels, sum_ref.shape[1]))
+    sum_ref[...] = jnp.sum(jnp.where(diagonal(total.shape), total, 0.0), axis=0, keepdims=True)
     far, near = edge_rows(position % 2 == 0, rows)
     edge_ref[0] = h_ref[far]
     edge_ref[1] = h_ref[near]
@@ -353,7 +357,9 @@
     rows, levels, nlon = row_ref.shape
     odd = lax.axis_index("lat") % 2 == 1
     area = nlon * float(np.sum(np.sin(np.pi * (np.arange(nlat) + 0.5) / nlat)))
-    mean = sums_ref[...] * (1.0 / area)
+    width = sums_ref.shape[1]
+    mean = jnp.where(diagonal((levels, width)), sums_ref[...] * (1.0 / area), 0.0)
+    mean = jnp.broadcast_to(jnp.sum(mean, axis=1, keepdims=True), (levels, LANES))
     done = near_ref.shape[0]
     copies = []
     for i in range(rows):
@@ -441,7 +447,7 @@
     edge_a, sums, source = call(
         source_kernel,
         [(x, vmem) for x in (about, rates[None], thresholds[None], height, merid_courant)],
-        [((3, levels, nlon), f32), ((levels, LANES), f32), (height.shape, f32)],
+        [((3, levels, nlon), f32), ((1, round_up(levels, LANES)), f32), (height.shape, f32)],
         8,
     )
     a = permute(edge_a, within)
@@ -460,7 +466,7 @@
     bits = [1 << i for i in range((count - 1).bit_length())]
     if count == 1 << len(bits):
         far = bits[2:]
-        rounds = [bits[:1], *([*far[i : i + 2], sum(far[i : i + 2])] for i in range(0, len(far), 2)), bits[1:2]]
+        rounds = [bits[:1], *([mask | 1 for mask in (*far[i : i + 2], sum(far[i : i + 2]))] for i in range(0, len(far), 2)), [mask | 1 for mask in bits[1:2]]]
         for masks in rounds:
             sums = sums + sum(permute(sums, [(p, p ^ mask) for p in range(count)]) for mask in dict.fromkeys(masks))
     else:

time: 25.9 us -> 24.7 us (0.954)
  the two profiles are of different devices: /device:TPU:0 before, /device:TPU:1 now
where the time goes in v10:
time: 24.7 us; the launch traced here: 24.5 us
  Pallas kernels  10.6 us (43%)
  starting transfers between devices  7.21 us (29%)
  waiting for transfers between devices  6.34 us (26%)
    pallas_call x8, Pallas kernels, call(): pl.pallas_call(kernel, in_specs=[pl.BlockSpec(memory_space=space) for _,...  10.6 us
    ppermute x7, starting transfers between devices, permute(): return lax.ppermute(x, axes, pairs)  7.21 us
    ppermute x7, waiting for transfers between devices, permute(): return lax.ppermute(x, axes, pairs)  6.34 us
  transfers between devices with their start and end apart: 7, of which 2 were waited for; matrix products, arithmetic and copies ran while one was open for 0% of the time, Pallas kernels for 23%

profile of v10, /device:TPU:1, one launch (start us, length us, event | category | flops | bytes accessed | tf_op | source)
XLA Modules:
  0.0 24.5 jit_solution(10295396866971053070)
XLA Ops:
  0.0 0.0 copy-start
  0.0 0.0 copy-start.1
  0.0 0.0 copy-start.6
  0.0 0.0 copy-start.5
  0.0 1.4 %shard_map.100 = (f32[3,360,128]{2,1,0:T(8,128)S(1)}, f32[21,8,128]{2,1,0:T(8,128)S(1)}) custom-call(f32[4,32,1440]{2,1,0:T(8,128)} %h_ref.9, f32[4,32,1440]{2,1,0:T(8,128)} %v_ref.7, f32[129]{0:T(256)} %constant.6.clone.cos_ref, s32[64]{0:T(128)} %flags_ref.1, s32[64]{0:T(128)} %cutoffs_ref.1), custom_call_target="tpu_custom_call" | custom-call | tf_op jit(solution)/shard_map/pallas_call | solution.py:393
  1.4 0.0 copy-start.4
  1.4 0.0 copy-start.3
  1.5 0.0 copy-done
  1.5 0.2 copy-done.1
  1.7 0.0 copy-done.6
  1.7 0.0 copy-done.5
  1.7 0.0 copy-start.2
  1.7 0.5 %shard_map.101 = (f32[3,32,1440]{2,1,0:T(8,128)S(1)}, f32[1,128]{1,0:T(1,128)S(1)}, f32[4,32,1440]{2,1,0:T(8,128)S(1)}) custom-call(f32[21,8,128]{2,1,0:T(8,128)S(1)} %get-tuple-element.18.about_ref, f32[1,32]{1,0:T(1,128)S(1)} %bitcast.2, f32[1,32]{1,0:T(1,128)S(1)} %bitcast.3, f32[4,32,1440]{2,1,0:T(8,128)S(1)} %copy-done, f32[4,32,1440]{2,1,0:T(8,128)S(1)} %copy-done.1), custom_call_target="tpu_custom_call" | custom-call | tf_op jit(solution)/shard_map/pallas_call | solution.py:393
  2.2 0.0 collective-permute-start.5
  2.2 2.7 %collective-permute-start.6 = (f32[3,360,128]{2,1,0:T(8,128)S(1)}, f32[3,360,128]{2,1,0:T(8,128)S(1)}, u32[]{:S(2)}, u32[]{:S(2)}) collective-permute-start(f32[3,360,128]{2,1,0:T(8,128)S(1)} %get-tuple-element.30), channel_id=1, source_target_pairs={{1,2},{3,4},{5,6},{7,8},{9,10},{11,12},{13,14},{2,1},{4,3},{6,5},{... | collective-permute-start | bytes 1658888 | tf_op jit(solution)/shard_map/ppermute | solution.py:404
  4.9 0.4 %collective-permute-start = (f32[1,128]{1,0:T(1,128)S(1)}, f32[1,128]{1,0:T(1,128)S(1)}, u32[]{:S(2)}, u32[]{:S(2)}) collective-permute-start(f32[1,128]{1,0:T(1,128)S(1)} %get-tuple-element.19), channel_id=1, source_target_pairs={{0,1},{1,0},{2,3},{3,2},{4,5},{5,4},{6,7},{7,6},{8,9},{9,8},{10,11... | collective-permute-start | bytes 1544 | tf_op jit(solution)/shard_map/ppermute | solution.py:404
  5.3 0.8 %collective-permute-done = f32[1,128]{1,0:T(1,128)S(1)} collective-permute-done((f32[1,128]{1,0:T(1,128)S(1)}, f32[1,128]{1,0:T(1,128)S(1)}, u32[]{:S(2)}, u32[]{:S(2)}) %collective-permute-start) | collective-permute-done | bytes 544 | tf_op jit(solution)/shard_map/ppermute | solution.py:404
  6.1 3.5 %collective-permute-start.3 = (f32[1,128]{1,0:T(1,128)S(1)}, f32[1,128]{1,0:T(1,128)S(1)}, u32[]{:S(2)}, u32[]{:S(2)}) collective-permute-start(f32[1,128]{1,0:T(1,128)S(1)} %add.15), channel_id=1, source_target_pairs={{0,13},{1,12},{2,15},{3,14},{4,9},{5,8},{6,11},{7,10},{8,5},{9,4},... | collective-permute-start | bytes 1544 | tf_op jit(solution)/shard_map/ppermute | solution.py:404
  9.6 0.0 collective-permute-start.2
  9.6 0.6 %collective-permute-start.1 = (f32[1,128]{1,0:T(1,128)S(1)}, f32[1,128]{1,0:T(1,128)S(1)}, u32[]{:S(2)}, u32[]{:S(2)}) collective-permute-start(f32[1,128]{1,0:T(1,128)S(1)} %add.15), channel_id=1, source_target_pairs={{0,5},{1,4},{2,7},{3,6},{4,1},{5,0},{6,3},{7,2},{8,13},{9,12},{10,... | collective-permute-start | bytes 1544 | tf_op jit(solution)/shard_map/ppermute | solution.py:404
  10.1 5.5 %collective-permute-done.3 = f32[1,128]{1,0:T(1,128)S(1)} collective-permute-done((f32[1,128]{1,0:T(1,128)S(1)}, f32[1,128]{1,0:T(1,128)S(1)}, u32[]{:S(2)}, u32[]{:S(2)}) %collective-permute-start.3) | collective-permute-done | bytes 544 | tf_op jit(solution)/shard_map/ppermute | solution.py:404
  15.6 0.0 collective-permute-done.2
  15.6 0.0 collective-permute-done.1
  15.7 0.1 collective-permute-start.4
  15.7 0.0 copy-done.4
  15.7 1.2 %shard_map.103 = (bf16[768,768]{1,0:T(8,128)(2,1)S(1)}, bf16[768,768]{1,0:T(8,128)(2,1)S(1)}, bf16[768,768]{1,0:T(8,128)(2,1)S(1)}, bf16[768,768]{1,0:T(8,128)(2,1)S(1)}) custom-call(f32[216,768]{1,0:T(8,128)S(1)} %copy-done.4), custom_call_target="tpu_custom_call" | custom-call | tf_op jit(solution)/shard_map/pallas_call | solution.py:393
  16.9 0.0 copy-done.3
  16.9 1.2 %shard_map.104 = (bf16[768,768]{1,0:T(8,128)(2,1)S(1)}, bf16[768,768]{1,0:T(8,128)(2,1)S(1)}, bf16[768,768]{1,0:T(8,128)(2,1)S(1)}, bf16[768,768]{1,0:T(8,128)(2,1)S(1)}) custom-call(f32[216,768]{1,0:T(8,128)S(1)} %copy-done.3), custom_call_target="tpu_custom_call" | custom-call | tf_op jit(solution)/shard_map/pallas_call | solution.py:393
  18.1 0.0 copy-done.2
  18.1 1.4 %shard_map.102.part_ref = f32[4,32,1440]{2,1,0:T(8,128)S(1)} custom-call(f32[4,32,1440]{2,1,0:T(8,128)S(1)} %copy-done, f32[4,32,1440]{2,1,0:T(8,128)S(1)} %copy-done.2, f32[4,32,1440]{2,1,0:T(8,128)S(1)} %get-tuple-element.20.s_ref), custom_call_target="tpu_custom_call" | custom-call | tf_op jit(solution)/shard_map/pallas_call | solution.py:393
  19.5 0.0 collective-permute-done.4
  19.5 0.0 collective-permute-done.5.a_ref
  19.5 2.0 %shard_map.105.near_ref = f32[2,32,1440]{2,1,0:T(8,128)S(1)} custom-call(f32[21,8,128]{2,1,0:T(8,128)S(1)} %get-tuple-element.18.about_ref, f32[4,32,1440]{2,1,0:T(8,128)S(1)} %copy-done, f32[4,32,1440]{2,1,0:T(8,128)S(1)} %copy-done.1, f32[4,32,1440]{2,1,0:T(8,128)S(1)} %shard_map.102.part_ref, f32[3,32,1440]{2,1,0:T(8,128)S(1)} %collective-permute-done.5.a_ref, ...), custom_call_target="tpu_custom_call" | custom-call | tf_op jit(solution)/shard_map/pallas_call | solution.py:393
  21.5 0.0 collective-permute-done.6.b_ref
  21.5 2.0 %shard_map.106.far_ref = f32[2,32,1440]{2,1,0:T(8,128)S(1)} custom-call(f32[21,8,128]{2,1,0:T(8,128)S(1)} %get-tuple-element.18.about_ref, f32[4,32,1440]{2,1,0:T(8,128)S(1)} %copy-done, f32[4,32,1440]{2,1,0:T(8,128)S(1)} %copy-done.1, f32[4,32,1440]{2,1,0:T(8,128)S(1)} %shard_map.102.part_ref, f32[3,360,128]{2,1,0:T(8,128)S(1)} %collective-permute-done.6.b_ref, ...), custom_call_target="tpu_custom_call" | custom-call | tf_op jit(solution)/shard_map/pallas_call | solution.py:393
  23.5 1.0 %shard_map.107 = f32[4,32,1440]{2,1,0:T(8,128)} custom-call(f32[21,8,128]{2,1,0:T(8,128)S(1)} %get-tuple-element.18.about_ref, f32[1,128]{1,0:T(1,128)S(1)} %add.19.sums_ref, f32[2,32,1440]{2,1,0:T(8,128)S(1)} %shard_map.105.near_ref, f32[2,32,1440]{2,1,0:T(8,128)S(1)} %shard_map.106.far_ref), custom_call_target="tpu_custom_call" | custom-call | tf_op jit(solution)/shard_map/pallas_call | solution.py:393
  (3 shorter events, 0.0 us)
Async XLA Ops:
  0.0 1.5 %copy-start = (f32[4,32,1440]{2,1,0:T(8,128)S(1)}, f32[4,32,1440]{2,1,0:T(8,128)}, u32[]{:S(2)}) copy-start(f32[4,32,1440]{2,1,0:T(8,128)} %h_ref.9) | copy-start | bytes 2211844
  0.0 1.6 %copy-start.1 = (f32[4,32,1440]{2,1,0:T(8,128)S(1)}, f32[4,32,1440]{2,1,0:T(8,128)}, u32[]{:S(2)}) copy-start(f32[4,32,1440]{2,1,0:T(8,128)} %v_ref.7) | copy-start | bytes 2211844
  0.0 1.6 %copy-start.6 = (f32[32]{0:T(128)S(1)}, f32[32]{0:T(128)}, u32[]{:S(2)}) copy-start(f32[32]{0:T(128)} %param.14) | copy-start | bytes 388
  0.0 1.6 %copy-start.5 = (f32[32]{0:T(128)S(1)}, f32[32]{0:T(128)}, u32[]{:S(2)}) copy-start(f32[32]{0:T(128)} %param.13) | copy-start | bytes 388
  1.4 14.3 %copy-start.4 = (f32[216,768]{1,0:T(8,128)S(1)}, f32[216,768]{1,0:T(8,128)}, u32[]{:S(2)}) copy-start(f32[216,768]{1,0:T(8,128)} %constant.7.clone.source_ref) | copy-start | bytes 1990660
  1.4 15.5 %copy-start.3 = (f32[216,768]{1,0:T(8,128)S(1)}, f32[216,768]{1,0:T(8,128)}, u32[]{:S(2)}) copy-start(f32[216,768]{1,0:T(8,128)} %constant.8.clone.source_ref) | copy-start | bytes 1990660
  1.7 16.5 %copy-start.2 = (f32[4,32,1440]{2,1,0:T(8,128)S(1)}, f32[4,32,1440]{2,1,0:T(8,128)}, u32[]{:S(2)}) copy-start(f32[4,32,1440]{2,1,0:T(8,128)} %u_ref.1) | copy-start | bytes 2211844
  2.2 17.4 %collective-permute-start.5 = (f32[3,32,1440]{2,1,0:T(8,128)S(1)}, f32[3,32,1440]{2,1,0:T(8,128)S(1)}, u32[]{:S(2)}, u32[]{:S(2)}) collective-permute-start(f32[3,32,1440]{2,1,0:T(8,128)S(1)} %get-tuple-element.21), channel_id=1, source_target_pairs={{0,1},{2,3},{4,5},{6,7},{8,9},{10,11},{12,13},{14,15},{1,0},{3,2},... | collective-permute-start | bytes 1658888 | tf_op jit(solution)/shard_map/ppermute | solution.py:404
  2.2 19.3 %collective-permute-start.6 = (f32[3,360,128]{2,1,0:T(8,128)S(1)}, f32[3,360,128]{2,1,0:T(8,128)S(1)}, u32[]{:S(2)}, u32[]{:S(2)}) collective-permute-start(f32[3,360,128]{2,1,0:T(8,128)S(1)} %get-tuple-element.30), channel_id=1, source_target_pairs={{1,2},{3,4},{5,6},{7,8},{9,10},{11,12},{13,14},{2,1},{4,3},{6,5},{... | collective-permute-start | bytes 1658888 | tf_op jit(solution)/shard_map/ppermute | solution.py:404
  4.9 1.2 %collective-permute-start = (f32[1,128]{1,0:T(1,128)S(1)}, f32[1,128]{1,0:T(1,128)S(1)}, u32[]{:S(2)}, u32[]{:S(2)}) collective-permute-start(f32[1,128]{1,0:T(1,128)S(1)} %get-tuple-element.19), channel_id=1, source_target_pairs={{0,1},{1,0},{2,3},{3,2},{4,5},{5,4},{6,7},{7,6},{8,9},{9,8},{10,11... | collective-permute-start | bytes 1544 | tf_op jit(solution)/shard_map/ppermute | solution.py:404
  6.1 9.6 %collective-permute-start.3 = (f32[1,128]{1,0:T(1,128)S(1)}, f32[1,128]{1,0:T(1,128)S(1)}, u32[]{:S(2)}, u32[]{:S(2)}) collective-permute-start(f32[1,128]{1,0:T(1,128)S(1)} %add.15), channel_id=1, source_target_pairs={{0,13},{1,12},{2,15},{3,14},{4,9},{5,8},{6,11},{7,10},{8,5},{9,4},... | collective-permute-start | bytes 1544 | tf_op jit(solution)/shard_map/ppermute | solution.py:404
  9.6 6.1 %collective-permute-start.2 = (f32[1,128]{1,0:T(1,128)S(1)}, f32[1,128]{1,0:T(1,128)S(1)}, u32[]{:S(2)}, u32[]{:S(2)}) collective-permute-start(f32[1,128]{1,0:T(1,128)S(1)} %add.15), channel_id=1, source_target_pairs={{0,9},{1,8},{2,11},{3,10},{4,13},{5,12},{6,15},{7,14},{8,1},{9,0},... | collective-permute-start | bytes 1544 | tf_op jit(solution)/shard_map/ppermute | solution.py:404
  9.6 6.1 %collective-permute-start.1 = (f32[1,128]{1,0:T(1,128)S(1)}, f32[1,128]{1,0:T(1,128)S(1)}, u32[]{:S(2)}, u32[]{:S(2)}) collective-permute-start(f32[1,128]{1,0:T(1,128)S(1)} %add.15), channel_id=1, source_target_pairs={{0,5},{1,4},{2,7},{3,6},{4,1},{5,0},{6,3},{7,2},{8,13},{9,12},{10,... | collective-permute-start | bytes 1544 | tf_op jit(solution)/shard_map/ppermute | solution.py:404
  15.7 3.8 %collective-permute-start.4 = (f32[1,128]{1,0:T(1,128)S(1)}, f32[1,128]{1,0:T(1,128)S(1)}, u32[]{:S(2)}, u32[]{:S(2)}) collective-permute-start(f32[1,128]{1,0:T(1,128)S(1)} %add_add_fusion), channel_id=1, source_target_pairs={{0,3},{1,2},{2,1},{3,0},{4,7},{5,6},{6,5},{7,4},{8,11},{9,10},{10,... | collective-permute-start | bytes 1544 | tf_op jit(solution)/shard_map/ppermute | solution.py:404

commit v11 on v10

--- a/solution.py
+++ b/solution.py
@@ -373,8 +373,11 @@
             for t in range(0, nlon, LANES):
                 lanes = slice(t, min(t + LANES, nlon))
                 row_ref[i, at, lanes] = ref[k, at, lanes] - shift[:, : lanes.stop - lanes.start]
-        copies.append(pltpu.make_async_copy(row_ref.at[i], out_ref.at[row], sem.at[i]))
-        copies[-1].start()
+            if g % 2 == 1 or g == levels // 8 - 1:
+                at = pl.ds(8 * (g - g % 2), 8 * (g % 2) + 8)
+                n = len(copies)
+                copies.append(pltpu.make_async_copy(row_ref.at[i, at], out_ref.at[row, at], sem.at[n]))
+                copies[-1].start()
     for c in copies:
         c.wait()
 
@@ -492,7 +495,7 @@
         [(x, vmem) for x in (about, sums, near, far)],
         [(height.shape, f32)],
         4,
-        [pltpu.VMEM(height.shape, f32), pltpu.SemaphoreType.DMA((rows,))],
+        [pltpu.VMEM(height.shape, f32), pltpu.SemaphoreType.DMA((rows * (levels // 8),))],
         hbm,
     )
     return out

time: 24.7 us -> 24.8 us (level)
  no operation moved by 1% of the time
where the time goes in v11:
time: 24.8 us; the launch traced here: 24.6 us
  Pallas kernels  10.7 us (43%)
  starting transfers between devices  7.21 us (29%)
  waiting for transfers between devices  6.34 us (26%)
    pallas_call x8, Pallas kernels, call(): pl.pallas_call(kernel, in_specs=[pl.BlockSpec(memory_space=space) for _,...  10.7 us
    ppermute x7, starting transfers between devices, permute(): return lax.ppermute(x, axes, pairs)  7.21 us
    ppermute x7, waiting for transfers between devices, permute(): return lax.ppermute(x, axes, pairs)  6.34 us
  transfers between devices with their start and end apart: 7, of which 2 were waited for; matrix products, arithmetic and copies ran while one was open for 0% of the time, Pallas kernels for 23%

profile of v11, /device:TPU:1, one launch (start us, length us, event | category | flops | bytes accessed | tf_op | source)
XLA Modules:
  0.0 24.6 jit_solution(3887930654031625769)
XLA Ops:
  0.0 0.0 copy-start
  0.0 0.0 copy-start.1
  0.0 0.0 copy-start.6
  0.0 0.0 copy-start.5
  0.0 1.4 %shard_map.100 = (f32[3,360,128]{2,1,0:T(8,128)S(1)}, f32[21,8,128]{2,1,0:T(8,128)S(1)}) custom-call(f32[4,32,1440]{2,1,0:T(8,128)} %h_ref.9, f32[4,32,1440]{2,1,0:T(8,128)} %v_ref.7, f32[129]{0:T(256)} %constant.6.clone.cos_ref, s32[64]{0:T(128)} %flags_ref.1, s32[64]{0:T(128)} %cutoffs_ref.1), custom_call_target="tpu_custom_call" | custom-call | tf_op jit(solution)/shard_map/pallas_call | solution.py:396
  1.4 0.0 copy-start.4
  1.4 0.0 copy-start.3
  1.5 0.0 copy-done
  1.5 0.2 copy-done.1
  1.7 0.0 copy-done.6
  1.7 0.0 copy-done.5
  1.7 0.0 copy-start.2
  1.7 0.5 %shard_map.101 = (f32[3,32,1440]{2,1,0:T(8,128)S(1)}, f32[1,128]{1,0:T(1,128)S(1)}, f32[4,32,1440]{2,1,0:T(8,128)S(1)}) custom-call(f32[21,8,128]{2,1,0:T(8,128)S(1)} %get-tuple-element.18.about_ref, f32[1,32]{1,0:T(1,128)S(1)} %bitcast.2, f32[1,32]{1,0:T(1,128)S(1)} %bitcast.3, f32[4,32,1440]{2,1,0:T(8,128)S(1)} %copy-done, f32[4,32,1440]{2,1,0:T(8,128)S(1)} %copy-done.1), custom_call_target="tpu_custom_call" | custom-call | tf_op jit(solution)/shard_map/pallas_call | solution.py:396
  2.2 0.0 collective-permute-start.5
  2.2 2.7 %collective-permute-start.6 = (f32[3,360,128]{2,1,0:T(8,128)S(1)}, f32[3,360,128]{2,1,0:T(8,128)S(1)}, u32[]{:S(2)}, u32[]{:S(2)}) collective-permute-start(f32[3,360,128]{2,1,0:T(8,128)S(1)} %get-tuple-element.30), channel_id=1, source_target_pairs={{1,2},{3,4},{5,6},{7,8},{9,10},{11,12},{13,14},{2,1},{4,3},{6,5},{... | collective-permute-start | bytes 1658888 | tf_op jit(solution)/shard_map/ppermute | solution.py:407
  4.9 0.4 %collective-permute-start = (f32[1,128]{1,0:T(1,128)S(1)}, f32[1,128]{1,0:T(1,128)S(1)}, u32[]{:S(2)}, u32[]{:S(2)}) collective-permute-start(f32[1,128]{1,0:T(1,128)S(1)} %get-tuple-element.19), channel_id=1, source_target_pairs={{0,1},{1,0},{2,3},{3,2},{4,5},{5,4},{6,7},{7,6},{8,9},{9,8},{10,11... | collective-permute-start | bytes 1544 | tf_op jit(solution)/shard_map/ppermute | solution.py:407
  5.3 0.8 %collective-permute-done = f32[1,128]{1,0:T(1,128)S(1)} collective-permute-done((f32[1,128]{1,0:T(1,128)S(1)}, f32[1,128]{1,0:T(1,128)S(1)}, u32[]{:S(2)}, u32[]{:S(2)}) %collective-permute-start) | collective-permute-done | bytes 544 | tf_op jit(solution)/shard_map/ppermute | solution.py:407
  6.1 3.5 %collective-permute-start.3 = (f32[1,128]{1,0:T(1,128)S(1)}, f32[1,128]{1,0:T(1,128)S(1)}, u32[]{:S(2)}, u32[]{:S(2)}) collective-permute-start(f32[1,128]{1,0:T(1,128)S(1)} %add.15), channel_id=1, source_target_pairs={{0,13},{1,12},{2,15},{3,14},{4,9},{5,8},{6,11},{7,10},{8,5},{9,4},... | collective-permute-start | bytes 1544 | tf_op jit(solution)/shard_map/ppermute | solution.py:407
  9.6 0.0 collective-permute-start.2
  9.6 0.6 %collective-permute-start.1 = (f32[1,128]{1,0:T(1,128)S(1)}, f32[1,128]{1,0:T(1,128)S(1)}, u32[]{:S(2)}, u32[]{:S(2)}) collective-permute-start(f32[1,128]{1,0:T(1,128)S(1)} %add.15), channel_id=1, source_target_pairs={{0,5},{1,4},{2,7},{3,6},{4,1},{5,0},{6,3},{7,2},{8,13},{9,12},{10,... | collective-permute-start | bytes 1544 | tf_op jit(solution)/shard_map/ppermute | solution.py:407
  10.1 5.5 %collective-permute-done.3 = f32[1,128]{1,0:T(1,128)S(1)} collective-permute-done((f32[1,128]{1,0:T(1,128)S(1)}, f32[1,128]{1,0:T(1,128)S(1)}, u32[]{:S(2)}, u32[]{:S(2)}) %collective-permute-start.3) | collective-permute-done | bytes 544 | tf_op jit(solution)/shard_map/ppermute | solution.py:407
  15.6 0.0 collective-permute-done.2
  15.6 0.0 collective-permute-done.1
  15.7 0.1 collective-permute-start.4
  15.7 0.0 copy-done.4
  15.7 1.2 %shard_map.103 = (bf16[768,768]{1,0:T(8,128)(2,1)S(1)}, bf16[768,768]{1,0:T(8,128)(2,1)S(1)}, bf16[768,768]{1,0:T(8,128)(2,1)S(1)}, bf16[768,768]{1,0:T(8,128)(2,1)S(1)}) custom-call(f32[216,768]{1,0:T(8,128)S(1)} %copy-done.4), custom_call_target="tpu_custom_call" | custom-call | tf_op jit(solution)/shard_map/pallas_call | solution.py:396
  16.9 0.0 copy-done.3
  16.9 1.2 %shard_map.104 = (bf16[768,768]{1,0:T(8,128)(2,1)S(1)}, bf16[768,768]{1,0:T(8,128)(2,1)S(1)}, bf16[768,768]{1,0:T(8,128)(2,1)S(1)}, bf16[768,768]{1,0:T(8,128)(2,1)S(1)}) custom-call(f32[216,768]{1,0:T(8,128)S(1)} %copy-done.3), custom_call_target="tpu_custom_call" | custom-call | tf_op jit(solution)/shard_map/pallas_call | solution.py:396
  18.1 0.0 copy-done.2
  18.1 1.4 %shard_map.102.part_ref = f32[4,32,1440]{2,1,0:T(8,128)S(1)} custom-call(f32[4,32,1440]{2,1,0:T(8,128)S(1)} %copy-done, f32[4,32,1440]{2,1,0:T(8,128)S(1)} %copy-done.2, f32[4,32,1440]{2,1,0:T(8,128)S(1)} %get-tuple-element.20.s_ref), custom_call_target="tpu_custom_call" | custom-call | tf_op jit(solution)/shard_map/pallas_call | solution.py:396
  19.5 0.0 collective-permute-done.4
  19.5 0.0 collective-permute-done.5.a_ref
  19.5 2.0 %shard_map.105.near_ref = f32[2,32,1440]{2,1,0:T(8,128)S(1)} custom-call(f32[21,8,128]{2,1,0:T(8,128)S(1)} %get-tuple-element.18.about_ref, f32[4,32,1440]{2,1,0:T(8,128)S(1)} %copy-done, f32[4,32,1440]{2,1,0:T(8,128)S(1)} %copy-done.1, f32[4,32,1440]{2,1,0:T(8,128)S(1)} %shard_map.102.part_ref, f32[3,32,1440]{2,1,0:T(8,128)S(1)} %collective-permute-done.5.a_ref, ...), custom_call_target="tpu_custom_call" | custom-call | tf_op jit(solution)/shard_map/pallas_call | solution.py:396
  21.5 0.0 collective-permute-done.6.b_ref
  21.5 2.0 %shard_map.106.far_ref = f32[2,32,1440]{2,1,0:T(8,128)S(1)} custom-call(f32[21,8,128]{2,1,0:T(8,128)S(1)} %get-tuple-element.18.about_ref, f32[4,32,1440]{2,1,0:T(8,128)S(1)} %copy-done, f32[4,32,1440]{2,1,0:T(8,128)S(1)} %copy-done.1, f32[4,32,1440]{2,1,0:T(8,128)S(1)} %shard_map.102.part_ref, f32[3,360,128]{2,1,0:T(8,128)S(1)} %collective-permute-done.6.b_ref, ...), custom_call_target="tpu_custom_call" | custom-call | tf_op jit(solution)/shard_map/pallas_call | solution.py:396
  23.5 1.1 %shard_map.107 = f32[4,32,1440]{2,1,0:T(8,128)} custom-call(f32[21,8,128]{2,1,0:T(8,128)S(1)} %get-tuple-element.18.about_ref, f32[1,128]{1,0:T(1,128)S(1)} %add.19.sums_ref, f32[2,32,1440]{2,1,0:T(8,128)S(1)} %shard_map.105.near_ref, f32[2,32,1440]{2,1,0:T(8,128)S(1)} %shard_map.106.far_ref), custom_call_target="tpu_custom_call" | custom-call | tf_op jit(solution)/shard_map/pallas_call | solution.py:396
  (3 shorter events, 0.0 us)
Async XLA Ops:
  0.0 1.5 %copy-start = (f32[4,32,1440]{2,1,0:T(8,128)S(1)}, f32[4,32,1440]{2,1,0:T(8,128)}, u32[]{:S(2)}) copy-start(f32[4,32,1440]{2,1,0:T(8,128)} %h_ref.9) | copy-start | bytes 2211844
  0.0 1.6 %copy-start.1 = (f32[4,32,1440]{2,1,0:T(8,128)S(1)}, f32[4,32,1440]{2,1,0:T(8,128)}, u32[]{:S(2)}) copy-start(f32[4,32,1440]{2,1,0:T(8,128)} %v_ref.7) | copy-start | bytes 2211844
  0.0 1.6 %copy-start.6 = (f32[32]{0:T(128)S(1)}, f32[32]{0:T(128)}, u32[]{:S(2)}) copy-start(f32[32]{0:T(128)} %param.14) | copy-start | bytes 388
  0.0 1.6 %copy-start.5 = (f32[32]{0:T(128)S(1)}, f32[32]{0:T(128)}, u32[]{:S(2)}) copy-start(f32[32]{0:T(128)} %param.13) | copy-start | bytes 388
  1.4 14.3 %copy-start.4 = (f32[216,768]{1,0:T(8,128)S(1)}, f32[216,768]{1,0:T(8,128)}, u32[]{:S(2)}) copy-start(f32[216,768]{1,0:T(8,128)} %constant.7.clone.source_ref) | copy-start | bytes 1990660
  1.4 15.5 %copy-start.3 = (f32[216,768]{1,0:T(8,128)S(1)}, f32[216,768]{1,0:T(8,128)}, u32[]{:S(2)}) copy-start(f32[216,768]{1,0:T(8,128)} %constant.8.clone.source_ref) | copy-start | bytes 1990660
  1.7 16.5 %copy-start.2 = (f32[4,32,1440]{2,1,0:T(8,128)S(1)}, f32[4,32,1440]{2,1,0:T(8,128)}, u32[]{:S(2)}) copy-start(f32[4,32,1440]{2,1,0:T(8,128)} %u_ref.1) | copy-start | bytes 2211844
  2.2 17.4 %collective-permute-start.5 = (f32[3,32,1440]{2,1,0:T(8,128)S(1)}, f32[3,32,1440]{2,1,0:T(8,128)S(1)}, u32[]{:S(2)}, u32[]{:S(2)}) collective-permute-start(f32[3,32,1440]{2,1,0:T(8,128)S(1)} %get-tuple-element.21), channel_id=1, source_target_pairs={{0,1},{2,3},{4,5},{6,7},{8,9},{10,11},{12,13},{14,15},{1,0},{3,2},... | collective-permute-start | bytes 1658888 | tf_op jit(solution)/shard_map/ppermute | solution.py:407
  2.2 19.3 %collective-permute-start.6 = (f32[3,360,128]{2,1,0:T(8,128)S(1)}, f32[3,360,128]{2,1,0:T(8,128)S(1)}, u32[]{:S(2)}, u32[]{:S(2)}) collective-permute-start(f32[3,360,128]{2,1,0:T(8,128)S(1)} %get-tuple-element.30), channel_id=1, source_target_pairs={{1,2},{3,4},{5,6},{7,8},{9,10},{11,12},{13,14},{2,1},{4,3},{6,5},{... | collective-permute-start | bytes 1658888 | tf_op jit(solution)/shard_map/ppermute | solution.py:407
  4.9 1.2 %collective-permute-start = (f32[1,128]{1,0:T(1,128)S(1)}, f32[1,128]{1,0:T(1,128)S(1)}, u32[]{:S(2)}, u32[]{:S(2)}) collective-permute-start(f32[1,128]{1,0:T(1,128)S(1)} %get-tuple-element.19), channel_id=1, source_target_pairs={{0,1},{1,0},{2,3},{3,2},{4,5},{5,4},{6,7},{7,6},{8,9},{9,8},{10,11... | collective-permute-start | bytes 1544 | tf_op jit(solution)/shard_map/ppermute | solution.py:407
  6.1 9.6 %collective-permute-start.3 = (f32[1,128]{1,0:T(1,128)S(1)}, f32[1,128]{1,0:T(1,128)S(1)}, u32[]{:S(2)}, u32[]{:S(2)}) collective-permute-start(f32[1,128]{1,0:T(1,128)S(1)} %add.15), channel_id=1, source_target_pairs={{0,13},{1,12},{2,15},{3,14},{4,9},{5,8},{6,11},{7,10},{8,5},{9,4},... | collective-permute-start | bytes 1544 | tf_op jit(solution)/shard_map/ppermute | solution.py:407
  9.6 6.1 %collective-permute-start.2 = (f32[1,128]{1,0:T(1,128)S(1)}, f32[1,128]{1,0:T(1,128)S(1)}, u32[]{:S(2)}, u32[]{:S(2)}) collective-permute-start(f32[1,128]{1,0:T(1,128)S(1)} %add.15), channel_id=1, source_target_pairs={{0,9},{1,8},{2,11},{3,10},{4,13},{5,12},{6,15},{7,14},{8,1},{9,0},... | collective-permute-start | bytes 1544 | tf_op jit(solution)/shard_map/ppermute | solution.py:407
  9.6 6.1 %collective-permute-start.1 = (f32[1,128]{1,0:T(1,128)S(1)}, f32[1,128]{1,0:T(1,128)S(1)}, u32[]{:S(2)}, u32[]{:S(2)}) collective-permute-start(f32[1,128]{1,0:T(1,128)S(1)} %add.15), channel_id=1, source_target_pairs={{0,5},{1,4},{2,7},{3,6},{4,1},{5,0},{6,3},{7,2},{8,13},{9,12},{10,... | collective-permute-start | bytes 1544 | tf_op jit(solution)/shard_map/ppermute | solution.py:407
  15.7 3.8 %collective-permute-start.4 = (f32[1,128]{1,0:T(1,128)S(1)}, f32[1,128]{1,0:T(1,128)S(1)}, u32[]{:S(2)}, u32[]{:S(2)}) collective-permute-start(f32[1,128]{1,0:T(1,128)S(1)} %add_add_fusion), channel_id=1, source_target_pairs={{0,3},{1,2},{2,1},{3,0},{4,7},{5,6},{6,5},{7,4},{8,11},{9,10},{10,... | collective-permute-start | bytes 1544 | tf_op jit(solution)/shard_map/ppermute | solution.py:407
